TPU v7x, 32 devices: a whole 2x2x4 slice. The times are simulated.
32 devices in a mesh: gx: 16 (over z, x, core), gy: 2 (over y).
Axes of the slice: x: 2, y: 2, z: 4, core: 2. Of those that a mesh axis runs over, the one named last changes fastest.
Arguments:
- temp_adjoint: float32 [8, 256, 2048], P(None, 'gy', 'gx'), may hold values from -6 to 6
- height_adjoint: float32 [256, 2048], P('gy', 'gx'), may hold values from -6 to 6
- east_velocity: float32 [8, 256, 2048], P(None, 'gy', 'gx'), may hold values from -0.8 to 0.8
- north_velocity: float32 [8, 256, 2048], P(None, 'gy', 'gx'), may hold values from -0.8 to 0.8
- temp_store: float32 [8, 256, 2048], P(None, 'gy', 'gx'), may hold values from -4 to 4
- salt_store: float32 [8, 256, 2048], P(None, 'gy', 'gx'), may hold values from -4 to 4
- slot_map: int32 [16, 2, 8], P('gx', 'gy'), may hold values from 0 to 7, each once within a row
- land_mask: int32 [8, 256, 2048], P(None, 'gy', 'gx'), may hold values 0 or 1
- ocean_depth: float32 [256, 2048], P('gy', 'gx'), may hold values from 0.1 to 1
Outputs:
- temp_back: float32 [8, 256, 2048], P(None, 'gy', 'gx')
- salt_back: float32 [8, 256, 2048], P(None, 'gy', 'gx')
- surface_adjoint: float32 [256, 2048], P('gy', 'gx')
Inputs may be any that keep to these rules, and one draw needn't show every extreme that they name: `slot_map`: each tile's entries over the last dimension name every slot 0 to 7 once.
All inputs are finite; a program needn't handle non-finite values. No bound on the sum of `land_mask` on one device may be relied on, other than what follows from the above.
Results may differ from a plain program's by a relative error of at most 0.00013.
Values sent between devices are 32-bit elements; how exact they have to be, the bound alone decides.
No kernel may reach another device: no remote copies, remote signals or barrier semaphores. Data moves between devices by JAX's collectives and lax.ppermute only.
A program may use at most 64 MiB of HBM per device.

v0:
```python
import functools

import jax
import jax.numpy as jnp
from jax import lax
from jax.experimental import pallas as pl
from jax.experimental.pallas import tpu as pltpu
from jax.sharding import PartitionSpec as P


ITERS = 6
RING = 8
KERNEL_VMEM = 16 * 1024 * 1024
LANES = 128

DIFFUSE = 0.2
TIMESTEP = 1.0
STIFFNESS = 8.0
GRAVITY = 4.0
THERMAL = 0.5
NONLINEAR = 0.4
CABBELING = 0.3
HALINE = 0.8


VMEM = pl.BlockSpec(memory_space=pltpu.VMEM)
SMEM = pl.BlockSpec(memory_space=pltpu.SMEM)
HBM = pl.BlockSpec(memory_space=pltpu.HBM)

OFF_AT, WEIGHT_AT = 16, 32
PAIRS = [(i, j) for i in range(ITERS + 1) for j in range(i, ITERS + 1)]


def call(kernel, outs, args, specs=None, keep=None, flops=4000000):
    specs = specs or [VMEM] * len(args)
    keep = keep or [True] * len(outs)
    args = [
        pltpu.with_memory_space_constraint(arg, pltpu.VMEM) if held else arg for arg, held in args
    ]
    shapes = [
        pltpu.VMEM(shape, jnp.float32) if kept else jax.ShapeDtypeStruct(shape, jnp.float32)
        for shape, kept in zip(outs, keep)
    ]
    return pl.pallas_call(
        kernel,
        out_shape=shapes,
        in_specs=specs,
        out_specs=[VMEM] * len(outs),
        compiler_params=pltpu.CompilerParams(vmem_limit_bytes=KERNEL_VMEM),
        cost_estimate=pl.CostEstimate(flops=flops, bytes_accessed=1000000, transcendentals=0),
    )(*args)


def held(*arrays):
    return tuple((array, True) for array in arrays)


def free(*arrays):
    return tuple((array, False) for array in arrays)


def total(value):
    return jnp.sum(jnp.sum(value, axis=0, keepdims=True), axis=1, keepdims=True)


def lane_index(shape):
    return lax.broadcasted_iota(jnp.int32, shape, 1)


def pack_x_kernel(levels, height, mask, depth, temp, east, to_east, to_west):
    wet = mask[0].astype(jnp.float32)
    fields = (wet * height[...], wet, depth[...])
    for at, field in enumerate(fields):
        flipped = jnp.transpose(field)
        to_west[at * RING : (at + 1) * RING, :] = flipped[:RING]
        to_east[at * RING : (at + 1) * RING, :] = flipped[-RING:]
    base = 3 * RING
    for level in range(levels):
        masked = mask[level].astype(jnp.float32) * temp[level]
        flux_east = (DIFFUSE - 0.5 * east[level]) * masked
        flux_west = (DIFFUSE + 0.5 * east[level]) * masked
        last = jnp.transpose(flux_east[:, -LANES:])
        first = jnp.transpose(flux_west[:, :LANES])
        to_east[base + level : base + level + 1, :] = last[-1:]
        to_west[base + level : base + level + 1, :] = first[:1]


def pack_y_kernel(
    levels, height, mask, depth, temp, north, from_west, from_east, sides, tracer_sides, to_north, to_south
):
    rows, columns = height.shape
    wet = mask[0].astype(jnp.float32)
    fields = (wet * height[...], wet, depth[...])
    for at, field in enumerate(fields):
        span = slice(at * RING, (at + 1) * RING)
        middle = jnp.zeros((LANES - 2 * RING, rows), jnp.float32)
        side = jnp.transpose(jnp.concatenate([from_east[span, :], middle, from_west[span, :]], axis=0))
        sides[at] = side
        to_north[span, :columns] = field[-RING:]
        to_north[span, columns:] = side[-RING:]
        to_south[span, :columns] = field[:RING]
        to_south[span, columns:] = side[:RING]
    base = 3 * RING
    span = slice(base, base + levels)
    middle = jnp.zeros((LANES - 2 * levels, rows), jnp.float32)
    tracer_sides[...] = jnp.transpose(
        jnp.concatenate([from_east[span, :], middle, from_west[span, :]], axis=0)
    )
    to_north[span, columns:] = jnp.zeros((levels, LANES), jnp.float32)
    to_south[span, columns:] = jnp.zeros((levels, LANES), jnp.float32)
    for level in range(levels):
        masked = mask[level].astype(jnp.float32) * temp[level]
        flux_north = (DIFFUSE - 0.5 * north[level]) * masked
        flux_south = (DIFFUSE + 0.5 * north[level]) * masked
        to_north[base + level : base + level + 1, :columns] = flux_north[-1:]
        to_south[base + level : base + level + 1, :columns] = flux_south[:1]


def tile_basis_kernel(height, mask, depth, row_out):
    rows, columns = height.shape
    wet = mask[0].astype(jnp.float32)
    deep = depth[...]
    row = lax.broadcasted_iota(jnp.int32, (rows, columns), 0)
    lane = lane_index((rows, columns))
    east_weight = (
        STIFFNESS * 0.5 * (deep + pltpu.roll(deep, columns - 1, 1)) * wet * pltpu.roll(wet, columns - 1, 1)
    )
    east_weight = jnp.where(lane == columns - 1, 0.0, east_weight)
    west_weight = pltpu.roll(east_weight, 1, 1)
    north_weight = STIFFNESS * 0.5 * (deep + pltpu.roll(deep, rows - 1, 0)) * wet * pltpu.roll(wet, rows - 1, 0)
    north_weight = jnp.where(row == rows - 1, 0.0, north_weight)
    south_weight = pltpu.roll(north_weight, 1, 0)

    def spread(field):
        out = west_weight * (field - pltpu.roll(field, 1, 1))
        out = out + east_weight * (field - pltpu.roll(field, columns - 1, 1))
        out = out + south_weight * (field - pltpu.roll(field, 1, 0))
        return out + north_weight * (field - pltpu.roll(field, rows - 1, 0))

    field = wet * height[...]
    square = total(field * field)
    weight = jnp.sqrt(square)
    vector = field * jnp.where(square > 0.0, lax.rsqrt(jnp.maximum(square, 1e-30)), 0.0)
    before, link = jnp.zeros_like(vector), jnp.zeros_like(square)
    at = lane_index((1, LANES))
    out = jnp.where(at == WEIGHT_AT, weight, 0.0)
    for step in range(ITERS):
        image = spread(vector) - link * before
        along, size = total(image * vector), total(image * image)
        out = jnp.where(at == step, along, out)
        if step + 1 < ITERS:
            left = size - along * along
            alive = left > 1e-6 * size
            scale = jnp.where(alive, lax.rsqrt(jnp.maximum(left, 1e-30)), 0.0)
            link = jnp.where(alive, jnp.sqrt(jnp.maximum(left, 0.0)), 0.0)
            before, vector = vector, (image - along * vector) * scale
            out = jnp.where(at == OFF_AT + step, link, out)
    row_out[...] = out


def merged_recurrence(tiles):
    at = lane_index(tiles.shape)
    diagonal = jnp.where(at < ITERS, tiles, 0.0)
    above = jnp.where(at < ITERS - 1, pltpu.roll(tiles, LANES - OFF_AT, 1), 0.0)
    below = pltpu.roll(above, 1, 1)
    vector = jnp.where(at == 0, pltpu.roll(tiles, LANES - WEIGHT_AT, 1), 0.0)
    square = total(vector * vector)
    vector = vector * jnp.where(square > 0.0, lax.rsqrt(jnp.maximum(square, 1e-30)), 0.0)
    before, link = jnp.zeros_like(vector), jnp.zeros_like(square)
    running = jnp.ones_like(square)
    steps = []
    for _ in range(ITERS):
        image = diagonal * vector - link * before
        image = image + above * pltpu.roll(vector, LANES - 1, 1) + below * pltpu.roll(vector, 1, 1)
        along, size = total(image * vector), total(image * image)
        left = size - along * along
        alive = left > 1e-6 * size
        middle = jnp.where(running > 0.0, along, 4.0 * STIFFNESS)
        back = link
        scale = jnp.where(alive, lax.rsqrt(jnp.maximum(left, 1e-30)), 0.0)
        link = jnp.where(alive, jnp.sqrt(jnp.maximum(left, 0.0)), 0.0)
        steps.append((middle, jnp.where(alive, link, 2.0 * STIFFNESS), back))
        running = jnp.where(alive, running, 0.0)
        before, vector = vector, (image - along * vector) * scale
    return steps


def krylov_kernel(
    height, mask, depth, sides, from_south, from_north, tiles, basis, ground, products, steps_out
):
    rows, columns = height.shape
    full_rows, full_columns = rows + 2 * RING, columns + LANES
    wet = mask[0].astype(jnp.float32)
    own = (wet * height[...], wet, depth[...])

    def widened(at):
        span = slice(at * RING, (at + 1) * RING)
        tile = jnp.concatenate([own[at], sides[at]], axis=1)
        return jnp.concatenate([tile, from_north[span, :], from_south[span, :]], axis=0)

    field, opening, deep = widened(0), widened(1), widened(2)
    ground[0] = opening
    ground[1] = deep
    west_weight = STIFFNESS * 0.5 * (deep + pltpu.roll(deep, 1, 1)) * opening * pltpu.roll(opening, 1, 1)
    east_weight = pltpu.roll(west_weight, full_columns - 1, 1)
    south_weight = STIFFNESS * 0.5 * (deep + pltpu.roll(deep, 1, 0)) * opening * pltpu.roll(opening, 1, 0)
    north_weight = pltpu.roll(south_weight, full_rows - 1, 0)

    def spread(value):
        out = west_weight * (value - pltpu.roll(value, 1, 1))
        out = out + east_weight * (value - pltpu.roll(value, full_columns - 1, 1))
        out = out + south_weight * (value - pltpu.roll(value, 1, 0))
        return out + north_weight * (value - pltpu.roll(value, full_rows - 1, 0))

    steps = merged_recurrence(tiles[...])
    at = lane_index((1, LANES))
    row = jnp.zeros((1, LANES), jnp.float32)
    for step, entries in enumerate(steps):
        for kind, entry in enumerate(entries):
            row = jnp.where(at == kind * OFF_AT + step, entry, row)
    steps_out[...] = row
    vectors = [field]
    before, value = None, field
    basis[0] = field
    for step, (middle, link, back) in enumerate(steps):
        image = spread(value) - middle * value
        if step:
            image = image - back * before
        before, value = value, image * (1.0 / link)
        if step + 1 < ITERS:
            basis[step + 1] = value
        vectors.append(value)
    cut = [vector[:rows, :columns] for vector in vectors]
    partial = [jnp.sum(cut[i] * cut[j], axis=0, keepdims=True) for i, j in PAIRS]
    partial = [sum(part[:, k : k + LANES] for k in range(0, columns, LANES)) for part in partial]
    partial = partial + [jnp.zeros((LANES - len(partial), LANES), jnp.float32)]
    table = jnp.transpose(jnp.concatenate(partial, axis=0))
    products[...] = jnp.sum(table, axis=0, keepdims=True)


def solve_kernel(gathered, steps_in, basis, ground, surface, pressure):
    rows, columns = surface.shape
    summed = jnp.sum(gathered[...], axis=0, keepdims=True)
    known = steps_in[...]
    at = lane_index((1, LANES))

    def entry(row, index):
        return jnp.sum(jnp.where(at == index, row, 0.0), axis=1, keepdims=True)

    gram = {}
    for index, (i, j) in enumerate(PAIRS):
        gram[i, j] = gram[j, i] = entry(summed, index)
    middle = [entry(known, step) for step in range(ITERS)]
    link = [entry(known, OFF_AT + step) for step in range(ITERS)]
    back = [entry(known, 2 * OFF_AT + step) for step in range(ITERS)]
    zero = jnp.zeros((1, 1), jnp.float32)

    def applied(vector):
        out = [zero] * (len(vector) + 1)
        for i, part in enumerate(vector):
            out[i] = out[i] + part + middle[i] * part
            out[i + 1] = out[i + 1] + link[i] * part
            if i:
                out[i - 1] = out[i - 1] + back[i] * part
        return out

    def inner(left, right):
        out = zero
        for i, a in enumerate(left):
            part = zero
            for j, b in enumerate(right):
                part = part + gram[i, j] * b
            out = out + a * part
        return out

    def scaled_add(left, scale, right):
        size = max(len(left), len(right))
        left = left + [zero] * (size - len(left))
        right = right + [zero] * (size - len(right))
        return [a + scale * b for a, b in zip(left, right)]

    residual = direction = [jnp.ones((1, 1), jnp.float32)]
    iterate = [zero]
    norm_now = gram[0, 0]
    for iteration in range(ITERS):
        image = applied(direction)
        product = inner(direction, image)
        step_size = jnp.where(product > 0.0, norm_now / product, 0.0)
        iterate = scaled_add(iterate, step_size, direction)
        if iteration + 1 < ITERS:
            residual = scaled_add(residual, -step_size, image)
            norm_next = inner(residual, residual)
            growth = jnp.where(norm_now > 0.0, norm_next / norm_now, 0.0)
            direction = scaled_add(residual, growth, direction)
            norm_now = norm_next
    value = iterate[0] * basis[0]
    for k in range(1, ITERS):
        value = value + iterate[k] * basis[k]
    surface[...] = value[:rows, :columns]
    opening = ground[0]
    load = ground[1] * value
    full_rows, full_columns = value.shape
    pull = jnp.zeros_like(load)
    for shift, axis in ((1, 1), (full_columns - 1, 1), (1, 0), (full_rows - 1, 0)):
        pull = pull + opening * pltpu.roll(opening, shift, axis) * (pltpu.roll(load, shift, axis) - load)
    pressure[...] = -GRAVITY * pull[:rows, :columns]


def tracer_kernel(levels, temp, east, north, mask, tracer_sides, from_south, from_north, tracer):
    rows, columns = temp.shape[1:]
    row = lax.broadcasted_iota(jnp.int32, (rows, columns), 0)
    lane = lane_index((rows, columns))
    base = 3 * RING
    for level in range(levels):
        masked = mask[level].astype(jnp.float32) * temp[level]
        east_coef = DIFFUSE - 0.5 * east[level]
        west_coef = DIFFUSE + 0.5 * east[level]
        north_coef = DIFFUSE - 0.5 * north[level]
        south_coef = DIFFUSE + 0.5 * north[level]
        side_west = tracer_sides[:, LANES - levels + level : LANES - levels + level + 1]
        side_east = tracer_sides[:, level : level + 1]
        side_south = from_south[base + level : base + level + 1, :columns]
        side_north = from_north[base + level : base + level + 1, :columns]
        inflow = jnp.where(lane == 0, side_west, pltpu.roll(east_coef * masked, 1, 1))
        inflow = inflow + jnp.where(
            lane == columns - 1, side_east, pltpu.roll(west_coef * masked, columns - 1, 1)
        )
        inflow = inflow + jnp.where(row == 0, side_south, pltpu.roll(north_coef * masked, 1, 0))
        inflow = inflow + jnp.where(
            row == rows - 1, side_north, pltpu.roll(south_coef * masked, rows - 1, 0)
        )
        tracer[level] = masked + TIMESTEP * (
            inflow - (east_coef + west_coef + north_coef + south_coef) * masked
        )


def level_of_slot(slots, slot, levels):
    level = jnp.int32(0)
    for k in range(1, levels):
        level = jnp.where(slots[k] == slot, jnp.int32(k), level)
    return level


def density(level, levels, pressure, mask):
    thickness = 1.0 + level.astype(jnp.float32) / levels
    return thickness * pressure[...] * mask[level].astype(jnp.float32)


def warm_kernel(levels, sizes, slots, tracer, pressure, mask, *refs):
    parts, (partial, salt) = refs[: len(sizes)], refs[len(sizes) :]
    slot = 0
    for size, part in zip(sizes, parts):
        for at in range(size):
            level = level_of_slot(slots, slot, levels)
            dense = density(level, levels, pressure, mask)
            warm = part[at]
            salt[level] = (HALINE + CABBELING * warm) * dense
            partial[level] = tracer[level] + (THERMAL + 2.0 * NONLINEAR * warm) * dense
            slot += 1


def salt_kernel(levels, first, slots, partial, pressure, mask, part, *refs):
    result, done, sems = refs[-3:]
    size = part.shape[0]
    copies = []
    for at in range(size):
        level = level_of_slot(slots, first + at, levels)
        dense = density(level, levels, pressure, mask)
        done[at] = partial[level] + CABBELING * part[at] * dense
        copies.append(pltpu.make_async_copy(done.at[at], result.at[level], sems.at[at]))
        copies[-1].start()
    for copy in copies:
        copy.wait()


def finish(levels, first, args, before):
    part = args[-1]
    shape = (levels,) + part.shape[1:]
    held_args = [pltpu.with_memory_space_constraint(arg, pltpu.VMEM) for arg in args[1:]]
    operands = [args[0]] + held_args + ([] if before is None else [before])
    return pl.pallas_call(
        functools.partial(salt_kernel, levels, first),
        out_shape=jax.ShapeDtypeStruct(shape, jnp.float32),
        in_specs=[SMEM] + [VMEM] * len(held_args) + ([] if before is None else [HBM]),
        out_specs=HBM,
        scratch_shapes=[
            pltpu.VMEM(part.shape, jnp.float32),
            pltpu.SemaphoreType.DMA((part.shape[0],)),
        ],
        input_output_aliases={} if before is None else {len(operands) - 1: 0},
        compiler_params=pltpu.CompilerParams(vmem_limit_bytes=KERNEL_VMEM),
        cost_estimate=pl.CostEstimate(flops=1000000, bytes_accessed=1000000, transcendentals=0),
    )(*operands)


def shifted(value, axis, steps, around):
    count = lax.axis_size(axis)
    pairs = [(i, (i + steps) % count) for i in range(count) if around or 0 <= i + steps < count]
    return lax.ppermute(value, axis, pairs)


def shared(row):
    axes = ("gx", "gy")
    count = lax.axis_size("gx") * lax.axis_size("gy")
    rows = jnp.broadcast_to(row[None], (count,) + row.shape)
    rows = lax.all_to_all(rows, axes, 0, 0)
    return rows.reshape(count, LANES)


def runs(levels):
    quarter, half = levels // 4, levels // 2
    return (quarter, quarter, levels - 2 * quarter), (half, levels - half)


def body(
    temp_adjoint,
    height_adjoint,
    east_velocity,
    north_velocity,
    temp_store,
    salt_store,
    slot_map,
    land_mask,
    ocean_depth,
):
    levels, rows, columns = temp_adjoint.shape
    half_cycle = lax.axis_size("gx") // 2
    strip = 3 * RING + levels
    full = (rows + 2 * RING, columns + LANES)
    surface_args = free(height_adjoint, land_mask, ocean_depth)

    def fetched(store, sizes):
        parts, start = [], 0
        for size in sizes:
            part = lax.slice_in_dim(store, start, start + size)
            parts.append(shifted(part, "gx", half_cycle, True))
            start += size
        return parts

    warm_sizes, salt_sizes = runs(levels)
    slots = shifted(slot_map, "gx", half_cycle, True).reshape(-1)
    warm_parts = fetched(temp_store, warm_sizes)
    salt_parts = fetched(salt_store, salt_sizes)

    to_east, to_west = call(
        functools.partial(pack_x_kernel, levels), [(strip, rows)] * 2, surface_args + free(temp_adjoint, east_velocity)
    )
    from_west = shifted(to_east, "gx", 1, True)
    from_east = shifted(to_west, "gx", -1, True)
    (tile_row,) = call(tile_basis_kernel, [(1, LANES)], surface_args)
    tiles = shared(tile_row)
    sides, tracer_sides, to_north, to_south = call(
        functools.partial(pack_y_kernel, levels),
        [(3, rows, LANES), (rows, LANES), (strip, full[1]), (strip, full[1])],
        surface_args + free(temp_adjoint, north_velocity) + held(from_west, from_east),
    )
    from_south = shifted(to_north, "gy", 1, False)
    from_north = shifted(to_south, "gy", -1, False)
    basis, ground, products, steps = call(
        krylov_kernel,
        [(ITERS,) + full, (2,) + full, (1, LANES), (1, LANES)],
        surface_args + held(sides, from_south, from_north, tiles),
    )
    gathered = shared(products)
    (tracer,) = call(
        functools.partial(tracer_kernel, levels),
        [temp_adjoint.shape],
        free(temp_adjoint, east_velocity, north_velocity, land_mask)
        + held(tracer_sides, from_south, from_north),
    )
    surface, pressure = call(
        solve_kernel, [(rows, columns)] * 2, held(gathered, steps, basis, ground), keep=[False, True]
    )
    partial, salt_back = call(
        functools.partial(warm_kernel, levels, warm_sizes),
        [temp_adjoint.shape] * 2,
        free(slots) + held(tracer, pressure, land_mask, *warm_parts),
        specs=[SMEM] + [VMEM] * (3 + len(warm_sizes)),
        keep=[True, False],
    )
    temp_back, first = None, 0
    for size, part in zip(salt_sizes, salt_parts):
        args = (slots, partial, pressure, land_mask, part)
        temp_back = finish(levels, first, args, temp_back)
        first += size
    return (temp_back, salt_back, surface)


def solution(mesh):
    return jax.shard_map(
        body,
        mesh=mesh,
        in_specs=(
            P(None, "gy", "gx"),
            P("gy", "gx"),
            P(None, "gy", "gx"),
            P(None, "gy", "gx"),
            P(None, "gy", "gx"),
            P(None, "gy", "gx"),
            P("gx", "gy", None),
            P(None, "gy", "gx"),
            P("gy", "gx"),
        ),
        out_specs=(P(None, "gy", "gx"), P(None, "gy", "gx"), P("gy", "gx")),
        check_vma=False,
    )
```

profile of v0, /device:TPU:0, one launch (start us, length us, event | category | flops | bytes accessed | tf_op | source)
XLA Modules:
  0.0 84.7 jit_solution(5207045130512609137)
XLA Ops:
  0.6 1.0 %copy-done = s32[8,128,128]{2,1,0:T(8,128)S(1)} copy-done((s32[8,128,128]{2,1,0:T(8,128)S(1)}, s32[8,128,128]{2,1,0:T(8,128)}, u32[]{:S(2)}) %copy-start) | copy-done | bytes 524312
  1.7 1.0 %copy-done.2 = f32[8,128,128]{2,1,0:T(8,128)S(1)} copy-done((f32[8,128,128]{2,1,0:T(8,128)S(1)}, f32[8,128,128]{2,1,0:T(8,128)}, u32[]{:S(2)}) %copy-start.2) | copy-done | bytes 524312
  2.7 1.0 %copy-done.4 = f32[8,128,128]{2,1,0:T(8,128)S(1)} copy-done((f32[8,128,128]{2,1,0:T(8,128)S(1)}, f32[8,128,128]{2,1,0:T(8,128)}, u32[]{:S(2)}) %copy-start.4) | copy-done | bytes 524312
  3.8 0.8 copy-done.7
  6.4 5.0 %collective-permute-start.2 = (f32[32,128]{1,0:T(8,128)S(1)}, f32[32,128]{1,0:T(8,128)S(1)}, u32[]{:S(2)}, u32[]{:S(2)}) collective-permute-start(f32[32,128]{1,0:T(8,128)S(1)} %get-tuple-element.18), channel_id=1, source_target_pairs={{0,30},{2,0},{4,2},{6,4},{8,6},{10,8},{12,10},{14,12},{16,14},{18,... | collective-permute-start | bytes 49160 | tf_op jit(solution)/shard_map/ppermute | solution.py:399
  11.4 1.2 %collective-permute-start = (s32[1,1,8]{2,1,0:T(1,128)S(1)}, s32[1,1,8]{2,1,0:T(1,128)S(1)}, u32[]{:S(2)}, u32[]{:S(2)}) collective-permute-start(s32[1,1,8]{2,1,0:T(1,128)S(1)} %copy-done.21), channel_id=1, source_target_pairs={{0,16},{2,18},{4,20},{6,22},{8,24},{10,26},{12,28},{14,30},{16,0},... | collective-permute-start | bytes 104 | tf_op jit(solution)/shard_map/ppermute | solution.py:399
  13.3 1.7 %collective-permute-start.7 = (f32[4,128,128]{2,1,0:T(8,128)}, f32[4,128,128]{2,1,0:T(8,128)}, u32[]{:S(2)}, u32[]{:S(2)}) collective-permute-start(f32[4,128,128]{2,1,0:T(8,128)} %slice.17), channel_id=1, source_target_pairs={{0,16},{2,18},{4,20},{6,22},{8,24},{10,26},{12,28},{14,30},{16,0},... | collective-permute-start | bytes 786440 | tf_op jit(solution)/shard_map/ppermute | solution.py:399
  15.0 0.9 %fusion = (f32[4,128,128]{2,1,0:T(8,128)}, f32[4,128,128]{2,1,0:T(8,128)}) fusion(f32[8,128,128]{2,1,0:T(8,128)S(1)} %copy-done.19), kind=kLoop, calls=%fused_computation | loop fusion | bytes 1048576 | tf_op jit(solution)/shard_map/slice | solution.py:435
  15.9 1.2 %collective-permute-start.9 = (f32[4,128,128]{2,1,0:T(8,128)}, f32[4,128,128]{2,1,0:T(8,128)}, u32[]{:S(2)}, u32[]{:S(2)}) collective-permute-start(f32[4,128,128]{2,1,0:T(8,128)} %get-tuple-element.31), channel_id=1, source_target_pairs={{0,16},{2,18},{4,20},{6,22},{8,24},{10,26},{12,28},{14,30},{16,0},... | collective-permute-start | bytes 786440 | tf_op jit(solution)/shard_map/ppermute | solution.py:399
  17.1 1.7 %collective-permute-start.8 = (f32[4,128,128]{2,1,0:T(8,128)}, f32[4,128,128]{2,1,0:T(8,128)}, u32[]{:S(2)}, u32[]{:S(2)}) collective-permute-start(f32[4,128,128]{2,1,0:T(8,128)} %get-tuple-element.32), channel_id=1, source_target_pairs={{0,16},{2,18},{4,20},{6,22},{8,24},{10,26},{12,28},{14,30},{16,0},... | collective-permute-start | bytes 786440 | tf_op jit(solution)/shard_map/ppermute | solution.py:399
  19.6 3.8 %collective-permute-start.3 = (f32[32,256]{1,0:T(8,128)S(1)}, f32[32,256]{1,0:T(8,128)S(1)}, u32[]{:S(2)}, u32[]{:S(2)}) collective-permute-start(f32[32,256]{1,0:T(8,128)S(1)} %get-tuple-element.20), channel_id=1, source_target_pairs={{0,1},{2,3},{4,5},{6,7},{8,9},{10,11},{12,13},{14,15},{16,17},{18,... | collective-permute-start | bytes 98312 | tf_op jit(solution)/shard_map/ppermute | solution.py:399
  24.0 1.3 %collective-permute-start.4 = (f32[32,256]{1,0:T(8,128)S(1)}, f32[32,256]{1,0:T(8,128)S(1)}, u32[]{:S(2)}, u32[]{:S(2)}) collective-permute-start(f32[32,256]{1,0:T(8,128)S(1)} %get-tuple-element.21), channel_id=1, source_target_pairs={{1,0},{3,2},{5,4},{7,6},{9,8},{11,10},{13,12},{15,14},{17,16},{19,... | collective-permute-start | bytes 98312 | tf_op jit(solution)/shard_map/ppermute | solution.py:399
  26.8 3.0 %collective-permute-done.4.from_north = f32[32,256]{1,0:T(8,128)S(1)} collective-permute-done((f32[32,256]{1,0:T(8,128)S(1)}, f32[32,256]{1,0:T(8,128)S(1)}, u32[]{:S(2)}, u32[]{:S(2)}) %collective-permute-start.4) | collective-permute-done | bytes 32800 | tf_op jit(solution)/shard_map/ppermute | solution.py:399
  30.6 1.3 %shard_map.115 = f32[1,128]{1,0:T(1,128)S(1)} custom-call(f32[128,128]{1,0:T(8,128)S(1)} %copy-done.7, s32[8,128,128]{2,1,0:T(8,128)S(1)} %copy-done, f32[128,128]{1,0:T(8,128)S(1)} %copy-done.8), custom_call_target="tpu_custom_call" | custom-call | flops 4000000 | bytes 1000000 | tf_op jit(solution)/shard_map/pallas_call | solution.py:44
  31.9 30.9 %all_to_all.10 = f32[32,1,128]{2,1,0:T(1,128)S(1)} all-to-all(f32[32,1,128]{2,1,0:T(1,128)S(1)} %broadcast_in_dim.17), channel_id=1, replica_groups=mesh['gx'=16,'gy'=2] {'gx','gy'}, dimensions={0} | all-to-all | bytes 32768 | tf_op jit(solution)/shard_map/all_to_all | solution.py:406
  62.8 1.6 %shard_map.116 = (f32[6,144,256]{2,1,0:T(8,128)S(1)}, f32[2,144,256]{2,1,0:T(8,128)S(1)}, f32[1,128]{1,0:T(1,128)S(1)}, f32[1,128]{1,0:T(1,128)S(1)}) custom-call(f32[128,128]{1,0:T(8,128)S(1)} %copy-done.7, s32[8,128,128]{2,1,0:T(8,128)S(1)} %copy-done, f32[128,128]{1,0:T(8,128)S(1)} %copy-done.8, f32[3,128,128]{2,1,0:T(8,128)S(1)} %get-tuple-element.22.sides, ...), custom_call_target="tpu_custom_call" | custom-call | flops 4000000 | bytes 1000000 | tf_op jit(solution)/shard_map/pallas_call | solution.py:44
  66.2 2.5 %all-to-all-start.1 = ((f32[32,1,128]{2,1,0:T(1,128)}), f32[32,1,128]{2,1,0:T(1,128)S(1)}, u32[]{:S(2)}, u32[]{:S(2)}) async-start(f32[32,1,128]{2,1,0:T(1,128)} %broadcast_in_dim.19), calls=%async_computation.1 | async-start | bytes 32768 | tf_op jit(solution)/shard_map/all_to_all | solution.py:406
  69.5 0.8 copy-done.14
  71.1 4.9 %all-to-all-done.1 = f32[32,1,128]{2,1,0:T(1,128)S(1)} async-done(((f32[32,1,128]{2,1,0:T(1,128)}), f32[32,1,128]{2,1,0:T(1,128)S(1)}, u32[]{:S(2)}, u32[]{:S(2)}) %all-to-all-start.1) | async-done | bytes 16416 | tf_op jit(solution)/shard_map/all_to_all | solution.py:406
  76.6 1.0 %copy-done.10 = f32[2,144,256]{2,1,0:T(8,128)S(1)} copy-done((f32[2,144,256]{2,1,0:T(8,128)S(1)}, f32[2,144,256]{2,1,0:T(8,128)}, u32[]{:S(2)}) %copy-start.10) | copy-done | bytes 294936
  77.5 1.0 %shard_map.117 = (f32[128,128]{1,0:T(8,128)}, f32[128,128]{1,0:T(8,128)S(1)}) custom-call(f32[32,128]{1,0:T(8,128)S(1)} %bitcast.5, f32[1,128]{1,0:T(1,128)S(1)} %copy-done.18, f32[6,144,256]{2,1,0:T(8,128)S(1)} %get-tuple-element.25.basis, f32[2,144,256]{2,1,0:T(8,128)S(1)} %copy-done.10), custom_call_target="tpu_custom_call" | custom-call | flops 4000000 | bytes 1000000 | tf_op jit(solution)/shard_map/pallas_call | solution.py:44
  79.2 2.1 %shard_map.118 = (f32[8,128,128]{2,1,0:T(8,128)S(1)}, f32[8,128,128]{2,1,0:T(8,128)}) custom-call(s32[8]{0:T(128)S(1)} %bitcast.7, f32[8,128,128]{2,1,0:T(8,128)S(1)} %shard_map.114.tracer, f32[128,128]{1,0:T(8,128)S(1)} %get-tuple-element.27.pressure, s32[8,128,128]{2,1,0:T(8,128)S(1)} %copy-done.1, f32[2,128,128]{2,1,0:T(8,128)} %collective-permute-done.5.refs_0_, ...), custom_call_target="tpu_custom_call" | custom-call | flops 4000000 | bytes 1000000 | tf_op jit(solution)/shard_map/pallas_call | solution.py:44
  81.2 1.7 %shard_map.119.refs_0_ = f32[8,128,128]{2,1,0:T(8,128)} custom-call(s32[8]{0:T(128)S(1)} %bitcast.8, f32[8,128,128]{2,1,0:T(8,128)S(1)} %get-tuple-element.28.partial, f32[128,128]{1,0:T(8,128)S(1)} %get-tuple-element.27.pressure, s32[8,128,128]{2,1,0:T(8,128)S(1)} %copy-done.1, f32[4,128,128]{2,1,0:T(8,128)} %collective-permute-done.9.part), custom_call_target="tpu_custom_call" | custom-call | flops 1000000 | bytes 1000000 | tf_op jit(solution)/shard_map/pallas_call | solution.py:381
  82.9 1.7 %shard_map.120 = f32[8,128,128]{2,1,0:T(8,128)} custom-call(s32[8]{0:T(128)S(1)} %bitcast.9, f32[8,128,128]{2,1,0:T(8,128)S(1)} %get-tuple-element.28.partial, f32[128,128]{1,0:T(8,128)S(1)} %get-tuple-element.27.pressure, s32[8,128,128]{2,1,0:T(8,128)S(1)} %copy-done.1, f32[4,128,128]{2,1,0:T(8,128)} %collective-permute-done.8.part, ...), custom_call_target="tpu_custom_call", output_to_operand_aliasing={{}: (5, {})} | custom-call | flops 1000000 | bytes 1000000 | tf_op jit(solution)/shard_map/pallas_call | solution.py:381
  (57 shorter events, 10.7 us)
Async XLA Ops:
  0.6 1.0 %copy-start = (s32[8,128,128]{2,1,0:T(8,128)S(1)}, s32[8,128,128]{2,1,0:T(8,128)}, u32[]{:S(2)}) copy-start(s32[8,128,128]{2,1,0:T(8,128)} %mask.15) | copy-start | bytes 1572868
  1.7 1.0 %copy-start.2 = (f32[8,128,128]{2,1,0:T(8,128)S(1)}, f32[8,128,128]{2,1,0:T(8,128)}, u32[]{:S(2)}) copy-start(f32[8,128,128]{2,1,0:T(8,128)} %temp.5) | copy-start | bytes 1572868
  2.7 1.0 %copy-start.4 = (f32[8,128,128]{2,1,0:T(8,128)S(1)}, f32[8,128,128]{2,1,0:T(8,128)}, u32[]{:S(2)}) copy-start(f32[8,128,128]{2,1,0:T(8,128)} %east.3) | copy-start | bytes 1572868
  3.8 0.8 copy-start.7
  5.4 5.9 %copy-start.21 = (s32[1,1,8]{2,1,0:T(1,128)S(1)}, s32[1,1,8]{2,1,0:T(1,128)}, u32[]{:S(2)}) copy-start(s32[1,1,8]{2,1,0:T(1,128)} %param.15) | copy-start | bytes 100
  5.4 7.1 %copy-start.20 = (f32[8,128,128]{2,1,0:T(8,128)S(1)}, f32[8,128,128]{2,1,0:T(8,128)}, u32[]{:S(2)}) copy-start(f32[8,128,128]{2,1,0:T(8,128)} %param.13) | copy-start | bytes 1572868
  5.8 9.2 %copy-start.19 = (f32[8,128,128]{2,1,0:T(8,128)S(1)}, f32[8,128,128]{2,1,0:T(8,128)}, u32[]{:S(2)}) copy-start(f32[8,128,128]{2,1,0:T(8,128)} %param.14) | copy-start | bytes 1572868
  5.8 11.3 %collective-permute-start.1 = (f32[32,128]{1,0:T(8,128)S(1)}, f32[32,128]{1,0:T(8,128)S(1)}, u32[]{:S(2)}, u32[]{:S(2)}) collective-permute-start(f32[32,128]{1,0:T(8,128)S(1)} %get-tuple-element.17), channel_id=1, source_target_pairs={{0,2},{2,4},{4,6},{6,8},{8,10},{10,12},{12,14},{14,16},{16,18},{18... | collective-permute-start | bytes 49160 | tf_op jit(solution)/shard_map/ppermute | solution.py:399
  6.4 12.5 %collective-permute-start.2 = (f32[32,128]{1,0:T(8,128)S(1)}, f32[32,128]{1,0:T(8,128)S(1)}, u32[]{:S(2)}, u32[]{:S(2)}) collective-permute-start(f32[32,128]{1,0:T(8,128)S(1)} %get-tuple-element.18), channel_id=1, source_target_pairs={{0,30},{2,0},{4,2},{6,4},{8,6},{10,8},{12,10},{14,12},{16,14},{18,... | collective-permute-start | bytes 49160 | tf_op jit(solution)/shard_map/ppermute | solution.py:399
  11.4 12.0 %collective-permute-start = (s32[1,1,8]{2,1,0:T(1,128)S(1)}, s32[1,1,8]{2,1,0:T(1,128)S(1)}, u32[]{:S(2)}, u32[]{:S(2)}) collective-permute-start(s32[1,1,8]{2,1,0:T(1,128)S(1)} %copy-done.21), channel_id=1, source_target_pairs={{0,16},{2,18},{4,20},{6,22},{8,24},{10,26},{12,28},{14,30},{16,0},... | collective-permute-start | bytes 104 | tf_op jit(solution)/shard_map/ppermute | solution.py:399
  13.3 5.5 %copy-start.6 = (f32[8,128,128]{2,1,0:T(8,128)S(1)}, f32[8,128,128]{2,1,0:T(8,128)}, u32[]{:S(2)}) copy-start(f32[8,128,128]{2,1,0:T(8,128)} %north.3) | copy-start | bytes 1572868
  13.3 65.2 %collective-permute-start.7 = (f32[4,128,128]{2,1,0:T(8,128)}, f32[4,128,128]{2,1,0:T(8,128)}, u32[]{:S(2)}, u32[]{:S(2)}) collective-permute-start(f32[4,128,128]{2,1,0:T(8,128)} %slice.17), channel_id=1, source_target_pairs={{0,16},{2,18},{4,20},{6,22},{8,24},{10,26},{12,28},{14,30},{16,0},... | collective-permute-start | bytes 786440 | tf_op jit(solution)/shard_map/ppermute | solution.py:399
  15.9 65.3 %collective-permute-start.9 = (f32[4,128,128]{2,1,0:T(8,128)}, f32[4,128,128]{2,1,0:T(8,128)}, u32[]{:S(2)}, u32[]{:S(2)}) collective-permute-start(f32[4,128,128]{2,1,0:T(8,128)} %get-tuple-element.31), channel_id=1, source_target_pairs={{0,16},{2,18},{4,20},{6,22},{8,24},{10,26},{12,28},{14,30},{16,0},... | collective-permute-start | bytes 786440 | tf_op jit(solution)/shard_map/ppermute | solution.py:399
  17.1 65.8 %collective-permute-start.8 = (f32[4,128,128]{2,1,0:T(8,128)}, f32[4,128,128]{2,1,0:T(8,128)}, u32[]{:S(2)}, u32[]{:S(2)}) collective-permute-start(f32[4,128,128]{2,1,0:T(8,128)} %get-tuple-element.32), channel_id=1, source_target_pairs={{0,16},{2,18},{4,20},{6,22},{8,24},{10,26},{12,28},{14,30},{16,0},... | collective-permute-start | bytes 786440 | tf_op jit(solution)/shard_map/ppermute | solution.py:399
  19.6 6.4 %collective-permute-start.3 = (f32[32,256]{1,0:T(8,128)S(1)}, f32[32,256]{1,0:T(8,128)S(1)}, u32[]{:S(2)}, u32[]{:S(2)}) collective-permute-start(f32[32,256]{1,0:T(8,128)S(1)} %get-tuple-element.20), channel_id=1, source_target_pairs={{0,1},{2,3},{4,5},{6,7},{8,9},{10,11},{12,13},{14,15},{16,17},{18,... | collective-permute-start | bytes 98312 | tf_op jit(solution)/shard_map/ppermute | solution.py:399
  24.0 5.8 %collective-permute-start.4 = (f32[32,256]{1,0:T(8,128)S(1)}, f32[32,256]{1,0:T(8,128)S(1)}, u32[]{:S(2)}, u32[]{:S(2)}) collective-permute-start(f32[32,256]{1,0:T(8,128)S(1)} %get-tuple-element.21), channel_id=1, source_target_pairs={{1,0},{3,2},{5,4},{7,6},{9,8},{11,10},{13,12},{15,14},{17,16},{19,... | collective-permute-start | bytes 98312 | tf_op jit(solution)/shard_map/ppermute | solution.py:399
  26.0 52.5 %collective-permute-start.5 = (f32[2,128,128]{2,1,0:T(8,128)}, f32[2,128,128]{2,1,0:T(8,128)}, u32[]{:S(2)}, u32[]{:S(2)}) collective-permute-start(f32[2,128,128]{2,1,0:T(8,128)} %get-tuple-element.34), channel_id=1, source_target_pairs={{0,16},{2,18},{4,20},{6,22},{8,24},{10,26},{12,28},{14,30},{16,0},... | collective-permute-start | bytes 393224 | tf_op jit(solution)/shard_map/ppermute | solution.py:399
  29.8 33.0 %copy-start.11 = (f32[32,256]{1,0:T(8,128)}, f32[32,256]{1,0:T(8,128)S(1)}, u32[]{:S(2)}) copy-start(f32[32,256]{1,0:T(8,128)S(1)} %collective-permute-done.4.from_north) | copy-start | bytes 98308
  29.8 48.7 %collective-permute-start.6 = (f32[2,128,128]{2,1,0:T(8,128)}, f32[2,128,128]{2,1,0:T(8,128)}, u32[]{:S(2)}, u32[]{:S(2)}) collective-permute-start(f32[2,128,128]{2,1,0:T(8,128)} %get-tuple-element.33), channel_id=1, source_target_pairs={{0,16},{2,18},{4,20},{6,22},{8,24},{10,26},{12,28},{14,30},{16,0},... | collective-permute-start | bytes 393224 | tf_op jit(solution)/shard_map/ppermute | solution.py:399
  30.6 38.2 %copy-start.3 = (f32[8,128,128]{2,1,0:T(8,128)S(1)}, f32[8,128,128]{2,1,0:T(8,128)}, u32[]{:S(2)}) copy-start(f32[8,128,128]{2,1,0:T(8,128)} %temp.5) | copy-start | bytes 1572868
  30.6 38.2 %copy-start.5 = (f32[8,128,128]{2,1,0:T(8,128)S(1)}, f32[8,128,128]{2,1,0:T(8,128)}, u32[]{:S(2)}) copy-start(f32[8,128,128]{2,1,0:T(8,128)} %east.3) | copy-start | bytes 1572868
  31.9 36.9 %copy-start.1 = (s32[8,128,128]{2,1,0:T(8,128)S(1)}, s32[8,128,128]{2,1,0:T(8,128)}, u32[]{:S(2)}) copy-start(s32[8,128,128]{2,1,0:T(8,128)} %mask.15) | copy-start | bytes 1572868
  66.2 9.7 %all-to-all-start.1 = ((f32[32,1,128]{2,1,0:T(1,128)}), f32[32,1,128]{2,1,0:T(1,128)S(1)}, u32[]{:S(2)}, u32[]{:S(2)}) async-start(f32[32,1,128]{2,1,0:T(1,128)} %broadcast_in_dim.19), calls=%async_computation.1 | async-start | bytes 32768 | tf_op jit(solution)/shard_map/all_to_all | solution.py:406
  76.6 1.0 %copy-start.10 = (f32[2,144,256]{2,1,0:T(8,128)S(1)}, f32[2,144,256]{2,1,0:T(8,128)}, u32[]{:S(2)}) copy-start(f32[2,144,256]{2,1,0:T(8,128)} %copy-done.9) | copy-start | bytes 884740
  (9 other events, 6.1 us)
where the time goes:
time: 85.4 us; the launch traced here: 84.7 us
  blocking collectives  30.9 us (36%)
  starting transfers between devices  20.6 us (24%)
  local copies, waits for them, and re-layouts  13.9 us (16%)
  Pallas kernels  10.5 us (12%)
  waiting for transfers between devices  7.9 us (9%)
    all_to_all x1, blocking collectives, shared(): rows = lax.all_to_all(rows, axes, 0, 0)  30.9 us
    ppermute x10, starting transfers between devices, shifted(): return lax.ppermute(value, axis, pairs)  18.1 us
    unnamed x44, local copies, waits for them, and re-layouts  11 us
    pallas_call x7, Pallas kernels, call(): pl.pallas_call(kernel, out_shape=shapes, in_specs=specs, out_specs=[VMEM]...  7.11 us
    all_to_all x1, waiting for transfers between devices, shared(): rows = lax.all_to_all(rows, axes, 0, 0)  4.89 us
    pallas_call x2, Pallas kernels, finish(): pl.pallas_call(functools.partial(salt_kernel, levels, first), out_shape=j...  3.44 us
    ppermute x10, waiting for transfers between devices, shifted(): return lax.ppermute(value, axis, pairs)  3.01 us
    all_to_all x1, starting transfers between devices, shared(): rows = lax.all_to_all(rows, axes, 0, 0)  2.5 us
  transfers between devices with their start and end apart: 11, of which 2 were waited for; matrix products, arithmetic and copies ran while one was open for 3% of the time, Pallas kernels for 10%

commit v1 on v0

--- a/solution.py
+++ b/solution.py
@@ -31,11 +31,11 @@
 PAIRS = [(i, j) for i in range(ITERS + 1) for j in range(i, ITERS + 1)]
 
 
-def call(kernel, outs, args, specs=None, keep=None, flops=4000000):
+def call(kernel, outs, args, specs=None, keep=None, grid=(), flops=4000000):
     specs = specs or [VMEM] * len(args)
     keep = keep or [True] * len(outs)
     args = [
-        pltpu.with_memory_space_constraint(arg, pltpu.VMEM) if held else arg for arg, held in args
+        arg if space is None else pltpu.with_memory_space_constraint(arg, space) for arg, space in args
     ]
     shapes = [
         pltpu.VMEM(shape, jnp.float32) if kept else jax.ShapeDtypeStruct(shape, jnp.float32)
@@ -44,6 +44,7 @@
     return pl.pallas_call(
         kernel,
         out_shape=shapes,
+        grid=grid,
         in_specs=specs,
         out_specs=[VMEM] * len(outs),
         compiler_params=pltpu.CompilerParams(vmem_limit_bytes=KERNEL_VMEM),
@@ -52,11 +53,15 @@
 
 
 def held(*arrays):
-    return tuple((array, True) for array in arrays)
+    return tuple((array, pltpu.VMEM) for array in arrays)
+
+
+def stored(*arrays):
+    return tuple((array, pltpu.HBM) for array in arrays)
 
 
 def free(*arrays):
-    return tuple((array, False) for array in arrays)
+    return tuple((array, None) for array in arrays)
 
 
 def total(value):
@@ -67,53 +72,55 @@
     return lax.broadcasted_iota(jnp.int32, shape, 1)
 
 
-def pack_x_kernel(levels, height, mask, depth, temp, east, to_east, to_west):
+def pack_y_kernel(levels, height, mask, depth, temp, north, to_north, to_south):
     wet = mask[0].astype(jnp.float32)
     fields = (wet * height[...], wet, depth[...])
     for at, field in enumerate(fields):
-        flipped = jnp.transpose(field)
-        to_west[at * RING : (at + 1) * RING, :] = flipped[:RING]
-        to_east[at * RING : (at + 1) * RING, :] = flipped[-RING:]
+        to_south[at * RING : (at + 1) * RING, :] = field[:RING]
+        to_north[at * RING : (at + 1) * RING, :] = field[-RING:]
     base = 3 * RING
     for level in range(levels):
-        masked = mask[level].astype(jnp.float32) * temp[level]
-        flux_east = (DIFFUSE - 0.5 * east[level]) * masked
-        flux_west = (DIFFUSE + 0.5 * east[level]) * masked
-        last = jnp.transpose(flux_east[:, -LANES:])
-        first = jnp.transpose(flux_west[:, :LANES])
-        to_east[base + level : base + level + 1, :] = last[-1:]
-        to_west[base + level : base + level + 1, :] = first[:1]
-
-
-def pack_y_kernel(
-    levels, height, mask, depth, temp, north, from_west, from_east, sides, tracer_sides, to_north, to_south
+        first, last = slice(0, RING), slice(temp.shape[1] - RING, temp.shape[1])
+        flux_south = (DIFFUSE + 0.5 * north[level, first]) * (
+            mask[level, first].astype(jnp.float32) * temp[level, first]
+        )
+        flux_north = (DIFFUSE - 0.5 * north[level, last]) * (
+            mask[level, last].astype(jnp.float32) * temp[level, last]
+        )
+        to_south[base + level : base + level + 1, :] = flux_south[:1]
+        to_north[base + level : base + level + 1, :] = flux_north[-1:]
+
+
+def pack_x_kernel(
+    levels, height, mask, depth, temp, east, from_south, from_north, to_east, to_west
 ):
-    rows, columns = height.shape
+    rows = height.shape[0]
     wet = mask[0].astype(jnp.float32)
     fields = (wet * height[...], wet, depth[...])
     for at, field in enumerate(fields):
         span = slice(at * RING, (at + 1) * RING)
-        middle = jnp.zeros((LANES - 2 * RING, rows), jnp.float32)
-        side = jnp.transpose(jnp.concatenate([from_east[span, :], middle, from_west[span, :]], axis=0))
-        sides[at] = side
-        to_north[span, :columns] = field[-RING:]
-        to_north[span, columns:] = side[-RING:]
-        to_south[span, :columns] = field[:RING]
-        to_south[span, columns:] = side[:RING]
+        beside = [from_north[span, :], from_south[span, :]]
+        beside.append(jnp.zeros((LANES - 2 * RING, field.shape[1]), jnp.float32))
+        flipped = jnp.transpose(jnp.concatenate([field] + beside, axis=0))
+        to_west[span, :] = flipped[:RING]
+        to_east[span, :] = flipped[-RING:]
     base = 3 * RING
-    span = slice(base, base + levels)
-    middle = jnp.zeros((LANES - 2 * levels, rows), jnp.float32)
-    tracer_sides[...] = jnp.transpose(
-        jnp.concatenate([from_east[span, :], middle, from_west[span, :]], axis=0)
-    )
-    to_north[span, columns:] = jnp.zeros((levels, LANES), jnp.float32)
-    to_south[span, columns:] = jnp.zeros((levels, LANES), jnp.float32)
     for level in range(levels):
+        at = slice(base + level, base + level + 1)
         masked = mask[level].astype(jnp.float32) * temp[level]
-        flux_north = (DIFFUSE - 0.5 * north[level]) * masked
-        flux_south = (DIFFUSE + 0.5 * north[level]) * masked
-        to_north[base + level : base + level + 1, :columns] = flux_north[-1:]
-        to_south[base + level : base + level + 1, :columns] = flux_south[:1]
+        flux_east = (DIFFUSE - 0.5 * east[level]) * masked
+        flux_west = (DIFFUSE + 0.5 * east[level]) * masked
+        to_east[at, :rows] = jnp.transpose(flux_east[:, -LANES:])[-1:]
+        to_west[at, :rows] = jnp.transpose(flux_west[:, :LANES])[:1]
+    spare = slice(base, base + levels)
+    to_east[spare, rows:] = jnp.zeros((levels, LANES), jnp.float32)
+    to_west[spare, rows:] = jnp.zeros((levels, LANES), jnp.float32)
+
+
+def beside_tile(from_west, from_east, start, size):
+    span = slice(start, start + size)
+    middle = jnp.zeros((LANES - 2 * size, from_west.shape[1]), jnp.float32)
+    return jnp.transpose(jnp.concatenate([from_east[span, :], middle, from_west[span, :]], axis=0))
 
 
 def tile_basis_kernel(height, mask, depth, row_out):
@@ -155,7 +162,7 @@
             link = jnp.where(alive, jnp.sqrt(jnp.maximum(left, 0.0)), 0.0)
             before, vector = vector, (image - along * vector) * scale
             out = jnp.where(at == OFF_AT + step, link, out)
-    row_out[...] = out
+    row_out[...] = jnp.broadcast_to(out[None], row_out.shape)
 
 
 def merged_recurrence(tiles):
@@ -186,7 +193,7 @@
 
 
 def krylov_kernel(
-    height, mask, depth, sides, from_south, from_north, tiles, basis, ground, products, steps_out
+    height, mask, depth, from_south, from_north, from_west, from_east, tiles, basis, products
 ):
     rows, columns = height.shape
     full_rows, full_columns = rows + 2 * RING, columns + LANES
@@ -195,12 +202,13 @@
 
     def widened(at):
         span = slice(at * RING, (at + 1) * RING)
-        tile = jnp.concatenate([own[at], sides[at]], axis=1)
-        return jnp.concatenate([tile, from_north[span, :], from_south[span, :]], axis=0)
+        tile = jnp.concatenate([own[at], from_north[span, :], from_south[span, :]], axis=0)
+        side = beside_tile(from_west, from_east, at * RING, RING)
+        return jnp.concatenate([tile, side[:full_rows]], axis=1)
 
     field, opening, deep = widened(0), widened(1), widened(2)
-    ground[0] = opening
-    ground[1] = deep
+    basis[ITERS] = opening
+    basis[ITERS + 1] = deep
     west_weight = STIFFNESS * 0.5 * (deep + pltpu.roll(deep, 1, 1)) * opening * pltpu.roll(opening, 1, 1)
     east_weight = pltpu.roll(west_weight, full_columns - 1, 1)
     south_weight = STIFFNESS * 0.5 * (deep + pltpu.roll(deep, 1, 0)) * opening * pltpu.roll(opening, 1, 0)
@@ -218,7 +226,7 @@
     for step, entries in enumerate(steps):
         for kind, entry in enumerate(entries):
             row = jnp.where(at == kind * OFF_AT + step, entry, row)
-    steps_out[...] = row
+    basis[ITERS + 2, :1, :LANES] = row
     vectors = [field]
     before, value = None, field
     basis[0] = field
@@ -235,13 +243,13 @@
     partial = [sum(part[:, k : k + LANES] for k in range(0, columns, LANES)) for part in partial]
     partial = partial + [jnp.zeros((LANES - len(partial), LANES), jnp.float32)]
     table = jnp.transpose(jnp.concatenate(partial, axis=0))
-    products[...] = jnp.sum(table, axis=0, keepdims=True)
-
-
-def solve_kernel(gathered, steps_in, basis, ground, surface, pressure):
+    products[...] = jnp.broadcast_to(jnp.sum(table, axis=0, keepdims=True)[None], products.shape)
+
+
+def solve_kernel(gathered, basis, surface, pressure):
     rows, columns = surface.shape
     summed = jnp.sum(gathered[...], axis=0, keepdims=True)
-    known = steps_in[...]
+    known = basis[ITERS + 2, :1, :LANES]
     at = lane_index((1, LANES))
 
     def entry(row, index):
@@ -297,8 +305,8 @@
     for k in range(1, ITERS):
         value = value + iterate[k] * basis[k]
     surface[...] = value[:rows, :columns]
-    opening = ground[0]
-    load = ground[1] * value
+    opening = basis[ITERS]
+    load = basis[ITERS + 1] * value
     full_rows, full_columns = value.shape
     pull = jnp.zeros_like(load)
     for shift, axis in ((1, 1), (full_columns - 1, 1), (1, 0), (full_rows - 1, 0)):
@@ -306,11 +314,14 @@
     pressure[...] = -GRAVITY * pull[:rows, :columns]
 
 
-def tracer_kernel(levels, temp, east, north, mask, tracer_sides, from_south, from_north, tracer):
+def tracer_kernel(
+    levels, temp, east, north, mask, from_south, from_north, from_west, from_east, tracer
+):
     rows, columns = temp.shape[1:]
     row = lax.broadcasted_iota(jnp.int32, (rows, columns), 0)
     lane = lane_index((rows, columns))
     base = 3 * RING
+    tracer_sides = beside_tile(from_west, from_east, base, levels)[:rows]
     for level in range(levels):
         masked = mask[level].astype(jnp.float32) * temp[level]
         east_coef = DIFFUSE - 0.5 * east[level]
@@ -319,8 +330,8 @@
         south_coef = DIFFUSE + 0.5 * north[level]
         side_west = tracer_sides[:, LANES - levels + level : LANES - levels + level + 1]
         side_east = tracer_sides[:, level : level + 1]
-        side_south = from_south[base + level : base + level + 1, :columns]
-        side_north = from_north[base + level : base + level + 1, :columns]
+        side_south = from_south[base + level : base + level + 1, :]
+        side_north = from_north[base + level : base + level + 1, :]
         inflow = jnp.where(lane == 0, side_west, pltpu.roll(east_coef * masked, 1, 1))
         inflow = inflow + jnp.where(
             lane == columns - 1, side_east, pltpu.roll(west_coef * masked, columns - 1, 1)
@@ -399,17 +410,13 @@
     return lax.ppermute(value, axis, pairs)
 
 
-def shared(row):
-    axes = ("gx", "gy")
-    count = lax.axis_size("gx") * lax.axis_size("gy")
-    rows = jnp.broadcast_to(row[None], (count,) + row.shape)
-    rows = lax.all_to_all(rows, axes, 0, 0)
-    return rows.reshape(count, LANES)
+def shared(rows):
+    rows = lax.all_to_all(rows, ("gx", "gy"), 0, 0)
+    return rows.reshape(rows.shape[0], LANES)
 
 
 def runs(levels):
-    quarter, half = levels // 4, levels // 2
-    return (quarter, quarter, levels - 2 * quarter), (half, levels - half)
+    return (levels,), (levels // 2, levels - levels // 2)
 
 
 def body(
@@ -425,14 +432,16 @@
 ):
     levels, rows, columns = temp_adjoint.shape
     half_cycle = lax.axis_size("gx") // 2
+    devices = lax.axis_size("gx") * lax.axis_size("gy")
     strip = 3 * RING + levels
     full = (rows + 2 * RING, columns + LANES)
-    surface_args = free(height_adjoint, land_mask, ocean_depth)
+    surface_args = stored(height_adjoint, land_mask, ocean_depth)
+    top = pl.BlockSpec((1, rows, columns), lambda _: (0, 0, 0))
 
     def fetched(store, sizes):
         parts, start = [], 0
         for size in sizes:
-            part = lax.slice_in_dim(store, start, start + size)
+            part = store if size == levels else lax.slice_in_dim(store, start, start + size)
             parts.append(shifted(part, "gx", half_cycle, True))
             start += size
         return parts
@@ -442,39 +451,41 @@
     warm_parts = fetched(temp_store, warm_sizes)
     salt_parts = fetched(salt_store, salt_sizes)
 
+    to_north, to_south = call(
+        functools.partial(pack_y_kernel, levels),
+        [(strip, columns)] * 2,
+        surface_args + stored(temp_adjoint, north_velocity),
+    )
+    from_south = shifted(to_north, "gy", 1, False)
+    from_north = shifted(to_south, "gy", -1, False)
+    (tile_rows,) = call(tile_basis_kernel, [(devices, 1, LANES)], surface_args, specs=[VMEM, top, VMEM], grid=(1,))
     to_east, to_west = call(
-        functools.partial(pack_x_kernel, levels), [(strip, rows)] * 2, surface_args + free(temp_adjoint, east_velocity)
+        functools.partial(pack_x_kernel, levels),
+        [(strip, rows + LANES)] * 2,
+        surface_args + stored(temp_adjoint, east_velocity) + held(from_south, from_north),
     )
     from_west = shifted(to_east, "gx", 1, True)
     from_east = shifted(to_west, "gx", -1, True)
-    (tile_row,) = call(tile_basis_kernel, [(1, LANES)], surface_args)
-    tiles = shared(tile_row)
-    sides, tracer_sides, to_north, to_south = call(
-        functools.partial(pack_y_kernel, levels),
-        [(3, rows, LANES), (rows, LANES), (strip, full[1]), (strip, full[1])],
-        surface_args + free(temp_adjoint, north_velocity) + held(from_west, from_east),
-    )
-    from_south = shifted(to_north, "gy", 1, False)
-    from_north = shifted(to_south, "gy", -1, False)
-    basis, ground, products, steps = call(
+    tiles = shared(tile_rows)
+    beside = held(from_south, from_north, from_west, from_east)
+    basis, products = call(
         krylov_kernel,
-        [(ITERS,) + full, (2,) + full, (1, LANES), (1, LANES)],
-        surface_args + held(sides, from_south, from_north, tiles),
+        [(ITERS + 3,) + full, (devices, 1, LANES)],
+        surface_args + beside + held(tiles),
+        specs=[VMEM, top] + [VMEM] * 6,
+        grid=(1,),
     )
     gathered = shared(products)
     (tracer,) = call(
         functools.partial(tracer_kernel, levels),
         [temp_adjoint.shape],
-        free(temp_adjoint, east_velocity, north_velocity, land_mask)
-        + held(tracer_sides, from_south, from_north),
-    )
-    surface, pressure = call(
-        solve_kernel, [(rows, columns)] * 2, held(gathered, steps, basis, ground), keep=[False, True]
-    )
+        stored(temp_adjoint, east_velocity, north_velocity, land_mask) + beside,
+    )
+    surface, pressure = call(solve_kernel, [(rows, columns)] * 2, held(gathered, basis), keep=[False, True])
     partial, salt_back = call(
         functools.partial(warm_kernel, levels, warm_sizes),
         [temp_adjoint.shape] * 2,
-        free(slots) + held(tracer, pressure, land_mask, *warm_parts),
+        free(slots) + held(tracer, pressure) + free(land_mask, *warm_parts),
         specs=[SMEM] + [VMEM] * (3 + len(warm_sizes)),
         keep=[True, False],
     )

time: 85.4 us -> 73 us (0.85)
  local copies, waits for them, and re-layouts: 13.9 us -> 1.85 us
  blocking collectives: 30.9 us -> 24.6 us
  Pallas kernels: 10.5 us -> 16.1 us
  starting transfers between devices: 20.6 us -> 22.9 us
  waiting for transfers between devices: 7.9 us -> 6.46 us
    unnamed x44 -> x4, local copies, waits for them, and re-layouts: 11 us -> 0.01 us
    pallas_call x7, Pallas kernels: 7.11 us -> 13.5 us  [call(): pl.pallas_call(kernel, out_shape=shapes, grid=grid, in_specs=specs, out_s...]
    all_to_all x1, blocking collectives: 30.9 us -> 24.6 us  [shared(): rows = lax.all_to_all(rows, ('gx', 'gy'), 0, 0)]
    all_to_all x1, waiting for transfers between devices: 4.89 us -> 2.12 us  [shared(): rows = lax.all_to_all(rows, ('gx', 'gy'), 0, 0)]
    all_to_all x1, starting transfers between devices: 2.5 us -> 3.89 us  [shared(): rows = lax.all_to_all(rows, ('gx', 'gy'), 0, 0)]
    ppermute x10 -> x8, waiting for transfers between devices: 3.01 us -> 4.35 us  [shifted(): return lax.ppermute(value, axis, pairs)]
    ppermute x10 -> x8, starting transfers between devices: 18.1 us -> 19 us  [shifted(): return lax.ppermute(value, axis, pairs)]
    slice x3 -> x1, local copies, waits for them, and re-layouts: 2.3 us -> 1.84 us  [fetched(): lax.slice_in_dim(store, start, start + size)]
  transfers between devices with their start and end apart: 11 -> 9, of which waited for: 2 -> 3; matrix products, arithmetic and copies ran while one was open for 3% -> 3% of each run, Pallas kernels for 10% -> 20%
where the time goes in v1:
time: 73 us; the launch traced here: 72.6 us
  blocking collectives  24.6 us (34%)
  starting transfers between devices  22.9 us (31%)
  Pallas kernels  16.1 us (22%)
  waiting for transfers between devices  6.46 us (9%)
  local copies, waits for them, and re-layouts  1.85 us (3%)
  between operations  0.74 us (1%)
    all_to_all x1, blocking collectives, shared(): rows = lax.all_to_all(rows, ('gx', 'gy'), 0, 0)  24.6 us
    ppermute x8, starting transfers between devices, shifted(): return lax.ppermute(value, axis, pairs)  19 us
    pallas_call x7, Pallas kernels, call(): pl.pallas_call(kernel, out_shape=shapes, grid=grid, in_specs=specs, out_s...  13.5 us
    ppermute x8, waiting for transfers between devices, shifted(): return lax.ppermute(value, axis, pairs)  4.35 us
    all_to_all x1, starting transfers between devices, shared(): rows = lax.all_to_all(rows, ('gx', 'gy'), 0, 0)  3.89 us
    pallas_call x2, Pallas kernels, finish(): pl.pallas_call(functools.partial(salt_kernel, levels, first), out_shape=j...  2.6 us
    all_to_all x1, waiting for transfers between devices, shared(): rows = lax.all_to_all(rows, ('gx', 'gy'), 0, 0)  2.12 us
    slice x1, local copies, waits for them, and re-layouts, fetched(): lax.slice_in_dim(store, start, start + size)  1.84 us
  transfers between devices with their start and end apart: 9, of which 3 were waited for; matrix products, arithmetic and copies ran while one was open for 3% of the time, Pallas kernels for 20%

profile of v1, /device:TPU:0, one launch (start us, length us, event | category | flops | bytes accessed | tf_op | source)
XLA Modules:
  0.0 72.6 jit_solution(6035116475852938941)
XLA Ops:
  0.6 4.1 %collective-permute-start.5 = (f32[8,128,128]{2,1,0:T(8,128)}, f32[8,128,128]{2,1,0:T(8,128)S(1)}, u32[]{:S(2)}, u32[]{:S(2)}) collective-permute-start(f32[8,128,128]{2,1,0:T(8,128)} %param.13), channel_id=1, source_target_pairs={{0,16},{2,18},{4,20},{6,22},{8,24},{10,26},{12,28},{14,30},{16,0},... | collective-permute-start | bytes 1572872 | tf_op jit(solution)/shard_map/ppermute | solution.py:410
  4.8 1.8 %fusion = (f32[4,128,128]{2,1,0:T(8,128)}, f32[4,128,128]{2,1,0:T(8,128)}) fusion(f32[8,128,128]{2,1,0:T(8,128)} %param.14), kind=kLoop, calls=%fused_computation | loop fusion | bytes 1048576 | tf_op jit(solution)/shard_map/slice | solution.py:444
  6.6 0.0 collective-permute-start.7
  6.6 2.9 %collective-permute-start.6 = (f32[4,128,128]{2,1,0:T(8,128)}, f32[4,128,128]{2,1,0:T(8,128)S(1)}, u32[]{:S(2)}, u32[]{:S(2)}) collective-permute-start(f32[4,128,128]{2,1,0:T(8,128)} %get-tuple-element.24), channel_id=1, source_target_pairs={{0,16},{2,18},{4,20},{6,22},{8,24},{10,26},{12,28},{14,30},{16,0},... | collective-permute-start | bytes 786440 | tf_op jit(solution)/shard_map/ppermute | solution.py:410
  9.5 1.4 %shard_map.112 = (f32[32,128]{1,0:T(8,128)S(1)}, f32[32,128]{1,0:T(8,128)S(1)}) custom-call(f32[128,128]{1,0:T(8,128)} %height.7, s32[8,128,128]{2,1,0:T(8,128)} %mask.15, f32[128,128]{1,0:T(8,128)} %depth.7, f32[8,128,128]{2,1,0:T(8,128)} %temp.5, f32[8,128,128]{2,1,0:T(8,128)} %north.3), custom_call_target="tpu_custom_call" | custom-call | flops 4000000 | bytes 1000000 | tf_op jit(solution)/shard_map/pallas_call | solution.py:44
  10.9 3.4 %collective-permute-start.1 = (f32[32,128]{1,0:T(8,128)S(1)}, f32[32,128]{1,0:T(8,128)S(1)}, u32[]{:S(2)}, u32[]{:S(2)}) collective-permute-start(f32[32,128]{1,0:T(8,128)S(1)} %get-tuple-element.13), channel_id=1, source_target_pairs={{0,1},{2,3},{4,5},{6,7},{8,9},{10,11},{12,13},{14,15},{16,17},{18,... | collective-permute-start | bytes 49160 | tf_op jit(solution)/shard_map/ppermute | solution.py:410
  14.4 1.3 %collective-permute-start.2 = (f32[32,128]{1,0:T(8,128)S(1)}, f32[32,128]{1,0:T(8,128)S(1)}, u32[]{:S(2)}, u32[]{:S(2)}) collective-permute-start(f32[32,128]{1,0:T(8,128)S(1)} %get-tuple-element.14), channel_id=1, source_target_pairs={{1,0},{3,2},{5,4},{7,6},{9,8},{11,10},{13,12},{15,14},{17,16},{19,... | collective-permute-start | bytes 49160 | tf_op jit(solution)/shard_map/ppermute | solution.py:410
  15.7 0.1 collective-permute-done.1.from_south
  15.8 4.2 %collective-permute-done.2.from_north = f32[32,128]{1,0:T(8,128)S(1)} collective-permute-done((f32[32,128]{1,0:T(8,128)S(1)}, f32[32,128]{1,0:T(8,128)S(1)}, u32[]{:S(2)}, u32[]{:S(2)}) %collective-permute-start.2) | collective-permute-done | bytes 16416 | tf_op jit(solution)/shard_map/ppermute | solution.py:410
  20.0 1.8 %shard_map.113 = (f32[32,256]{1,0:T(8,128)S(1)}, f32[32,256]{1,0:T(8,128)S(1)}) custom-call(f32[128,128]{1,0:T(8,128)} %height.7, s32[8,128,128]{2,1,0:T(8,128)} %mask.15, f32[128,128]{1,0:T(8,128)} %depth.7, f32[8,128,128]{2,1,0:T(8,128)} %temp.5, f32[8,128,128]{2,1,0:T(8,128)} %east.3, f32[32,128]{1,0:T(8,128)S(1)} %collective-permute-done.1.from_south, ...), custom_call_target="tpu_custom_call" | custom-call | flops 4000000 | bytes 1000000 | tf_op jit(solution)/shard_map/pallas_call | solution.py:44
  21.8 0.1 collective-permute-start.3
  21.9 4.4 %collective-permute-start.4 = (f32[32,256]{1,0:T(8,128)S(1)}, f32[32,256]{1,0:T(8,128)S(1)}, u32[]{:S(2)}, u32[]{:S(2)}) collective-permute-start(f32[32,256]{1,0:T(8,128)S(1)} %get-tuple-element.16), channel_id=1, source_target_pairs={{0,30},{2,0},{4,2},{6,4},{8,6},{10,8},{12,10},{14,12},{16,14},{18,... | collective-permute-start | bytes 98312 | tf_op jit(solution)/shard_map/ppermute | solution.py:410
  26.3 2.2 %shard_map.115 = f32[32,1,128]{2,1,0:T(1,128)S(1)} custom-call(f32[128,128]{1,0:T(8,128)} %height.7, s32[8,128,128]{2,1,0:T(8,128)} %mask.15, f32[128,128]{1,0:T(8,128)} %depth.7), custom_call_target="tpu_custom_call" | custom-call | flops 4000000 | bytes 1000000 | tf_op jit(solution)/shard_map/pallas_call | solution.py:44
  28.6 24.6 %all_to_all.10 = f32[32,1,128]{2,1,0:T(1,128)S(1)} all-to-all(f32[32,1,128]{2,1,0:T(1,128)S(1)} %shard_map.115), channel_id=1, replica_groups=mesh['gx'=16,'gy'=2] {'gx','gy'}, dimensions={0} | all-to-all | bytes 32768 | tf_op jit(solution)/shard_map/all_to_all | solution.py:414
  53.2 3.3 %shard_map.116 = (f32[9,144,256]{2,1,0:T(8,128)S(1)}, f32[32,1,128]{2,1,0:T(1,128)}) custom-call(f32[128,128]{1,0:T(8,128)} %height.7, s32[8,128,128]{2,1,0:T(8,128)} %mask.15, f32[128,128]{1,0:T(8,128)} %depth.7, f32[32,128]{1,0:T(8,128)S(1)} %collective-permute-done.1.from_south, f32[32,128]{1,0:T(8,128)S(1)} %collective-permute-done.2.from_north, ...), custom_call_target="tpu_custom_call" | custom-call | flops 4000000 | bytes 1000000 | tf_op jit(solution)/shard_map/pallas_call | solution.py:44
  56.5 3.9 %all-to-all-start.1 = ((f32[32,1,128]{2,1,0:T(1,128)}), f32[32,1,128]{2,1,0:T(1,128)S(1)}, u32[]{:S(2)}, u32[]{:S(2)}) async-start(f32[32,1,128]{2,1,0:T(1,128)} %get-tuple-element.17), calls=%async_computation.1 | async-start | bytes 32768 | tf_op jit(solution)/shard_map/all_to_all | solution.py:414
  60.4 2.7 %collective-permute-start = (s32[1,1,8]{2,1,0:T(1,128)S(1)}, s32[1,1,8]{2,1,0:T(1,128)S(1)}, u32[]{:S(2)}, u32[]{:S(2)}) collective-permute-start(s32[1,1,8]{2,1,0:T(1,128)S(1)} %copy-done.1), channel_id=1, source_target_pairs={{0,16},{2,18},{4,20},{6,22},{8,24},{10,26},{12,28},{14,30},{16,0},... | collective-permute-start | bytes 104 | tf_op jit(solution)/shard_map/ppermute | solution.py:410
  63.1 2.3 %shard_map.114.tracer = f32[8,128,128]{2,1,0:T(8,128)S(1)} custom-call(f32[8,128,128]{2,1,0:T(8,128)} %temp.5, f32[8,128,128]{2,1,0:T(8,128)} %east.3, f32[8,128,128]{2,1,0:T(8,128)} %north.3, s32[8,128,128]{2,1,0:T(8,128)} %mask.15, f32[32,128]{1,0:T(8,128)S(1)} %collective-permute-done.1.from_south, f32[32,128]{1,0:T(8,128)S(1)} %collective-permute-done.2.from_north, ...), custom_call_target="tpu_custom_call" | custom-call | flops 4000000 | bytes 1000000 | tf_op jit(solution)/shard_map/pallas_call | solution.py:44
  65.4 0.0 copy-start
  65.4 2.1 %all-to-all-done.1 = f32[32,1,128]{2,1,0:T(1,128)S(1)} async-done(((f32[32,1,128]{2,1,0:T(1,128)}), f32[32,1,128]{2,1,0:T(1,128)S(1)}, u32[]{:S(2)}, u32[]{:S(2)}) %all-to-all-start.1) | async-done | bytes 16416 | tf_op jit(solution)/shard_map/all_to_all | solution.py:414
  67.5 1.0 %shard_map.117 = (f32[128,128]{1,0:T(8,128)}, f32[128,128]{1,0:T(8,128)S(1)}) custom-call(f32[32,128]{1,0:T(8,128)S(1)} %bitcast.3, f32[9,144,256]{2,1,0:T(8,128)S(1)} %get-tuple-element.18.basis), custom_call_target="tpu_custom_call" | custom-call | flops 4000000 | bytes 1000000 | tf_op jit(solution)/shard_map/pallas_call | solution.py:44
  68.5 1.5 %shard_map.118 = (f32[8,128,128]{2,1,0:T(8,128)S(1)}, f32[8,128,128]{2,1,0:T(8,128)}) custom-call(s32[8]{0:T(128)S(1)} %bitcast.5, f32[8,128,128]{2,1,0:T(8,128)S(1)} %shard_map.114.tracer, f32[128,128]{1,0:T(8,128)S(1)} %get-tuple-element.19.pressure, s32[8,128,128]{2,1,0:T(8,128)S(1)} %copy-done, f32[8,128,128]{2,1,0:T(8,128)S(1)} %collective-permute-done.5.refs_0_), custom_call_target="tpu_custom_call" | custom-call | flops 4000000 | bytes 1000000 | tf_op jit(solution)/shard_map/pallas_call | solution.py:44
  70.0 1.3 %shard_map.119.refs_0_ = f32[8,128,128]{2,1,0:T(8,128)} custom-call(s32[8]{0:T(128)S(1)} %bitcast.6, f32[8,128,128]{2,1,0:T(8,128)S(1)} %get-tuple-element.20.partial, f32[128,128]{1,0:T(8,128)S(1)} %get-tuple-element.19.pressure, s32[8,128,128]{2,1,0:T(8,128)S(1)} %copy-done, f32[4,128,128]{2,1,0:T(8,128)S(1)} %collective-permute-done.7.part), custom_call_target="tpu_custom_call" | custom-call | flops 1000000 | bytes 1000000 | tf_op jit(solution)/shard_map/pallas_call | solution.py:392
  71.3 1.3 %shard_map.120 = f32[8,128,128]{2,1,0:T(8,128)} custom-call(s32[8]{0:T(128)S(1)} %bitcast.7, f32[8,128,128]{2,1,0:T(8,128)S(1)} %get-tuple-element.20.partial, f32[128,128]{1,0:T(8,128)S(1)} %get-tuple-element.19.pressure, s32[8,128,128]{2,1,0:T(8,128)S(1)} %copy-done, ...), custom_call_target="tpu_custom_call", output_to_operand_aliasing={{}: (5, {})} | custom-call | flops 1000000 | bytes 1000000 | tf_op jit(solution)/shard_map/pallas_call | solution.py:392
  (9 shorter events, 0.0 us)
Async XLA Ops:
  0.6 67.9 %collective-permute-start.5 = (f32[8,128,128]{2,1,0:T(8,128)}, f32[8,128,128]{2,1,0:T(8,128)S(1)}, u32[]{:S(2)}, u32[]{:S(2)}) collective-permute-start(f32[8,128,128]{2,1,0:T(8,128)} %param.13), channel_id=1, source_target_pairs={{0,16},{2,18},{4,20},{6,22},{8,24},{10,26},{12,28},{14,30},{16,0},... | collective-permute-start | bytes 1572872 | tf_op jit(solution)/shard_map/ppermute | solution.py:410
  6.6 63.4 %collective-permute-start.7 = (f32[4,128,128]{2,1,0:T(8,128)}, f32[4,128,128]{2,1,0:T(8,128)S(1)}, u32[]{:S(2)}, u32[]{:S(2)}) collective-permute-start(f32[4,128,128]{2,1,0:T(8,128)} %get-tuple-element.23), channel_id=1, source_target_pairs={{0,16},{2,18},{4,20},{6,22},{8,24},{10,26},{12,28},{14,30},{16,0},... | collective-permute-start | bytes 786440 | tf_op jit(solution)/shard_map/ppermute | solution.py:410
  6.6 64.7 %collective-permute-start.6 = (f32[4,128,128]{2,1,0:T(8,128)}, f32[4,128,128]{2,1,0:T(8,128)S(1)}, u32[]{:S(2)}, u32[]{:S(2)}) collective-permute-start(f32[4,128,128]{2,1,0:T(8,128)} %get-tuple-element.24), channel_id=1, source_target_pairs={{0,16},{2,18},{4,20},{6,22},{8,24},{10,26},{12,28},{14,30},{16,0},... | collective-permute-start | bytes 786440 | tf_op jit(solution)/shard_map/ppermute | solution.py:410
  10.9 4.9 %collective-permute-start.1 = (f32[32,128]{1,0:T(8,128)S(1)}, f32[32,128]{1,0:T(8,128)S(1)}, u32[]{:S(2)}, u32[]{:S(2)}) collective-permute-start(f32[32,128]{1,0:T(8,128)S(1)} %get-tuple-element.13), channel_id=1, source_target_pairs={{0,1},{2,3},{4,5},{6,7},{8,9},{10,11},{12,13},{14,15},{16,17},{18,... | collective-permute-start | bytes 49160 | tf_op jit(solution)/shard_map/ppermute | solution.py:410
  14.4 46.0 %copy-start.1 = (s32[1,1,8]{2,1,0:T(1,128)S(1)}, s32[1,1,8]{2,1,0:T(1,128)}, u32[]{:S(2)}) copy-start(s32[1,1,8]{2,1,0:T(1,128)} %param.15) | copy-start | bytes 100
  14.4 5.6 %collective-permute-start.2 = (f32[32,128]{1,0:T(8,128)S(1)}, f32[32,128]{1,0:T(8,128)S(1)}, u32[]{:S(2)}, u32[]{:S(2)}) collective-permute-start(f32[32,128]{1,0:T(8,128)S(1)} %get-tuple-element.14), channel_id=1, source_target_pairs={{1,0},{3,2},{5,4},{7,6},{9,8},{11,10},{13,12},{15,14},{17,16},{19,... | collective-permute-start | bytes 49160 | tf_op jit(solution)/shard_map/ppermute | solution.py:410
  21.8 31.3 %collective-permute-start.3 = (f32[32,256]{1,0:T(8,128)S(1)}, f32[32,256]{1,0:T(8,128)S(1)}, u32[]{:S(2)}, u32[]{:S(2)}) collective-permute-start(f32[32,256]{1,0:T(8,128)S(1)} %get-tuple-element.15), channel_id=1, source_target_pairs={{0,2},{2,4},{4,6},{6,8},{8,10},{10,12},{12,14},{14,16},{16,18},{18... | collective-permute-start | bytes 98312 | tf_op jit(solution)/shard_map/ppermute | solution.py:410
  21.9 31.3 %collective-permute-start.4 = (f32[32,256]{1,0:T(8,128)S(1)}, f32[32,256]{1,0:T(8,128)S(1)}, u32[]{:S(2)}, u32[]{:S(2)}) collective-permute-start(f32[32,256]{1,0:T(8,128)S(1)} %get-tuple-element.16), channel_id=1, source_target_pairs={{0,30},{2,0},{4,2},{6,4},{8,6},{10,8},{12,10},{14,12},{16,14},{18,... | collective-permute-start | bytes 98312 | tf_op jit(solution)/shard_map/ppermute | solution.py:410
  56.5 11.0 %all-to-all-start.1 = ((f32[32,1,128]{2,1,0:T(1,128)}), f32[32,1,128]{2,1,0:T(1,128)S(1)}, u32[]{:S(2)}, u32[]{:S(2)}) async-start(f32[32,1,128]{2,1,0:T(1,128)} %get-tuple-element.17), calls=%async_computation.1 | async-start | bytes 32768 | tf_op jit(solution)/shard_map/all_to_all | solution.py:414
  60.4 8.1 %collective-permute-start = (s32[1,1,8]{2,1,0:T(1,128)S(1)}, s32[1,1,8]{2,1,0:T(1,128)S(1)}, u32[]{:S(2)}, u32[]{:S(2)}) collective-permute-start(s32[1,1,8]{2,1,0:T(1,128)S(1)} %copy-done.1), channel_id=1, source_target_pairs={{0,16},{2,18},{4,20},{6,22},{8,24},{10,26},{12,28},{14,30},{16,0},... | collective-permute-start | bytes 104 | tf_op jit(solution)/shard_map/ppermute | solution.py:410
  65.4 3.1 %copy-start = (s32[8,128,128]{2,1,0:T(8,128)S(1)}, s32[8,128,128]{2,1,0:T(8,128)}, u32[]{:S(2)}) copy-start(s32[8,128,128]{2,1,0:T(8,128)} %mask.15) | copy-start | bytes 1572868

commit v2 on v1

--- a/solution.py
+++ b/solution.py
@@ -31,7 +31,7 @@
 PAIRS = [(i, j) for i in range(ITERS + 1) for j in range(i, ITERS + 1)]
 
 
-def call(kernel, outs, args, specs=None, keep=None, grid=(), flops=4000000):
+def call(kernel, outs, args, specs=None, keep=None, flops=4000000):
     specs = specs or [VMEM] * len(args)
     keep = keep or [True] * len(outs)
     args = [
@@ -44,7 +44,6 @@
     return pl.pallas_call(
         kernel,
         out_shape=shapes,
-        grid=grid,
         in_specs=specs,
         out_specs=[VMEM] * len(outs),
         compiler_params=pltpu.CompilerParams(vmem_limit_bytes=KERNEL_VMEM),
@@ -72,36 +71,49 @@
     return lax.broadcasted_iota(jnp.int32, shape, 1)
 
 
-def pack_y_kernel(levels, height, mask, depth, temp, north, to_north, to_south):
+def pack_y_kernel(levels, height, mask, depth, temp, north, fields, *messages):
     wet = mask[0].astype(jnp.float32)
-    fields = (wet * height[...], wet, depth[...])
-    for at, field in enumerate(fields):
-        to_south[at * RING : (at + 1) * RING, :] = field[:RING]
-        to_north[at * RING : (at + 1) * RING, :] = field[-RING:]
+    fields[0] = wet * height[...]
+    fields[1] = wet
+    fields[2] = depth[...]
+    first, last = slice(0, RING), slice(temp.shape[1] - RING, temp.shape[1])
+
+    def send(span, to_north, to_south):
+        if len(messages) == 1:
+            messages[0][span, :] = jnp.where(lax.axis_index("gy") == 0, to_north, to_south)
+        else:
+            messages[0][span, :] = to_north
+            messages[1][span, :] = to_south
+
+    for at in range(3):
+        field = fields[at]
+        send(slice(at * RING, (at + 1) * RING), field[last], field[first])
     base = 3 * RING
     for level in range(levels):
-        first, last = slice(0, RING), slice(temp.shape[1] - RING, temp.shape[1])
         flux_south = (DIFFUSE + 0.5 * north[level, first]) * (
             mask[level, first].astype(jnp.float32) * temp[level, first]
         )
         flux_north = (DIFFUSE - 0.5 * north[level, last]) * (
             mask[level, last].astype(jnp.float32) * temp[level, last]
         )
-        to_south[base + level : base + level + 1, :] = flux_south[:1]
-        to_north[base + level : base + level + 1, :] = flux_north[-1:]
-
-
-def pack_x_kernel(
-    levels, height, mask, depth, temp, east, from_south, from_north, to_east, to_west
-):
-    rows = height.shape[0]
-    wet = mask[0].astype(jnp.float32)
-    fields = (wet * height[...], wet, depth[...])
-    for at, field in enumerate(fields):
+        send(slice(base + level, base + level + 1), flux_north[-1:], flux_south[:1])
+
+
+def pack_x_kernel(levels, received, fields, mask, temp, east, *refs):
+    arrived, (from_south, from_north, to_east, to_west) = refs[:received], refs[received:]
+    if received == 1:
+        lower = lax.axis_index("gy") == 0
+        from_south[...] = jnp.where(lower, 0.0, arrived[0][...])
+        from_north[...] = jnp.where(lower, arrived[0][...], 0.0)
+    else:
+        from_south[...] = arrived[0][...]
+        from_north[...] = arrived[1][...]
+    rows = fields.shape[1]
+    for at in range(3):
         span = slice(at * RING, (at + 1) * RING)
         beside = [from_north[span, :], from_south[span, :]]
-        beside.append(jnp.zeros((LANES - 2 * RING, field.shape[1]), jnp.float32))
-        flipped = jnp.transpose(jnp.concatenate([field] + beside, axis=0))
+        beside.append(jnp.zeros((LANES - 2 * RING, fields.shape[2]), jnp.float32))
+        flipped = jnp.transpose(jnp.concatenate([fields[at]] + beside, axis=0))
         to_west[span, :] = flipped[:RING]
         to_east[span, :] = flipped[-RING:]
     base = 3 * RING
@@ -123,10 +135,9 @@
     return jnp.transpose(jnp.concatenate([from_east[span, :], middle, from_west[span, :]], axis=0))
 
 
-def tile_basis_kernel(height, mask, depth, row_out):
-    rows, columns = height.shape
-    wet = mask[0].astype(jnp.float32)
-    deep = depth[...]
+def tile_basis_kernel(fields, row_out):
+    rows, columns = fields.shape[1:]
+    wet, deep = fields[1], fields[2]
     row = lax.broadcasted_iota(jnp.int32, (rows, columns), 0)
     lane = lane_index((rows, columns))
     east_weight = (
@@ -144,7 +155,7 @@
         out = out + south_weight * (field - pltpu.roll(field, 1, 0))
         return out + north_weight * (field - pltpu.roll(field, rows - 1, 0))
 
-    field = wet * height[...]
+    field = fields[0]
     square = total(field * field)
     weight = jnp.sqrt(square)
     vector = field * jnp.where(square > 0.0, lax.rsqrt(jnp.maximum(square, 1e-30)), 0.0)
@@ -192,17 +203,13 @@
     return steps
 
 
-def krylov_kernel(
-    height, mask, depth, from_south, from_north, from_west, from_east, tiles, basis, products
-):
-    rows, columns = height.shape
+def krylov_kernel(fields, from_south, from_north, from_west, from_east, tiles, basis, products):
+    rows, columns = fields.shape[1:]
     full_rows, full_columns = rows + 2 * RING, columns + LANES
-    wet = mask[0].astype(jnp.float32)
-    own = (wet * height[...], wet, depth[...])
 
     def widened(at):
         span = slice(at * RING, (at + 1) * RING)
-        tile = jnp.concatenate([own[at], from_north[span, :], from_south[span, :]], axis=0)
+        tile = jnp.concatenate([fields[at], from_north[span, :], from_south[span, :]], axis=0)
         side = beside_tile(from_west, from_east, at * RING, RING)
         return jnp.concatenate([tile, side[:full_rows]], axis=1)
 
@@ -416,7 +423,8 @@
 
 
 def runs(levels):
-    return (levels,), (levels // 2, levels - levels // 2)
+    most = 5 * levels // 8
+    return (levels,), (most, levels - most)
 
 
 def body(
@@ -435,45 +443,40 @@
     devices = lax.axis_size("gx") * lax.axis_size("gy")
     strip = 3 * RING + levels
     full = (rows + 2 * RING, columns + LANES)
-    surface_args = stored(height_adjoint, land_mask, ocean_depth)
-    top = pl.BlockSpec((1, rows, columns), lambda _: (0, 0, 0))
-
-    def fetched(store, sizes):
-        parts, start = [], 0
-        for size in sizes:
-            part = store if size == levels else lax.slice_in_dim(store, start, start + size)
-            parts.append(shifted(part, "gx", half_cycle, True))
-            start += size
-        return parts
 
     warm_sizes, salt_sizes = runs(levels)
     slots = shifted(slot_map, "gx", half_cycle, True).reshape(-1)
-    warm_parts = fetched(temp_store, warm_sizes)
-    salt_parts = fetched(salt_store, salt_sizes)
-
-    to_north, to_south = call(
+    warm_parts = [shifted(temp_store, "gx", half_cycle, True)]
+
+    swap = lax.axis_size("gy") == 2
+    fields, *messages = call(
         functools.partial(pack_y_kernel, levels),
-        [(strip, columns)] * 2,
-        surface_args + stored(temp_adjoint, north_velocity),
-    )
-    from_south = shifted(to_north, "gy", 1, False)
-    from_north = shifted(to_south, "gy", -1, False)
-    (tile_rows,) = call(tile_basis_kernel, [(devices, 1, LANES)], surface_args, specs=[VMEM, top, VMEM], grid=(1,))
-    to_east, to_west = call(
-        functools.partial(pack_x_kernel, levels),
-        [(strip, rows + LANES)] * 2,
-        surface_args + stored(temp_adjoint, east_velocity) + held(from_south, from_north),
+        [(3, rows, columns)] + [(strip, columns)] * (1 if swap else 2),
+        stored(height_adjoint, land_mask, ocean_depth, temp_adjoint, north_velocity),
+    )
+    if swap:
+        arrived = [shifted(messages[0], "gy", 1, True)]
+    else:
+        arrived = [shifted(messages[0], "gy", 1, False)]
+        arrived += [shifted(messages[1], "gy", -1, False)]
+    (tile_rows,) = call(tile_basis_kernel, [(devices, 1, LANES)], held(fields))
+    from_south, from_north, to_east, to_west = call(
+        functools.partial(pack_x_kernel, levels, len(arrived)),
+        [(strip, columns)] * 2 + [(strip, rows + LANES)] * 2,
+        held(fields) + stored(land_mask, temp_adjoint, east_velocity) + held(*arrived),
     )
     from_west = shifted(to_east, "gx", 1, True)
     from_east = shifted(to_west, "gx", -1, True)
+    cuts, start = [], 0
+    for size in salt_sizes:
+        cuts.append(lax.slice_in_dim(salt_store, start, start + size))
+        start += size
+    *cuts, tile_rows = lax.optimization_barrier((*cuts, tile_rows))
     tiles = shared(tile_rows)
+    salt_parts = [shifted(cut, "gx", half_cycle, True) for cut in cuts]
     beside = held(from_south, from_north, from_west, from_east)
     basis, products = call(
-        krylov_kernel,
-        [(ITERS + 3,) + full, (devices, 1, LANES)],
-        surface_args + beside + held(tiles),
-        specs=[VMEM, top] + [VMEM] * 6,
-        grid=(1,),
+        krylov_kernel, [(ITERS + 3,) + full, (devices, 1, LANES)], held(fields) + beside + held(tiles)
     )
     gathered = shared(products)
     (tracer,) = call(

time: 73 us -> 72 us (0.986)
  blocking collectives: 24.6 us -> 29.3 us
  starting transfers between devices: 22.9 us -> 19.8 us
  waiting for transfers between devices: 6.46 us -> 4.35 us
  Pallas kernels: 16.1 us -> 14.2 us
  local copies, waits for them, and re-layouts: 1.85 us -> 3.35 us
    all_to_all x1, blocking collectives: 24.6 us -> 29.3 us  [shared(): rows = lax.all_to_all(rows, ('gx', 'gy'), 0, 0)]
    ppermute x8 -> x7, starting transfers between devices: 19 us -> 15.9 us  [shifted(): return lax.ppermute(value, axis, pairs)]
    ppermute x8 -> x7, waiting for transfers between devices: 4.35 us -> 2.23 us  [shifted(): return lax.ppermute(value, axis, pairs)]
    pallas_call x7, Pallas kernels: 13.5 us -> 11.6 us  [call(): pl.pallas_call(kernel, out_shape=shapes, in_specs=specs, out_specs=[VMEM]...]
    slice x1 -> x2, local copies, waits for them, and re-layouts: 1.84 us -> 3.34 us  [body(): cuts.append(lax.slice_in_dim(salt_store, start, start + size))]
  transfers between devices with their start and end apart: 9 -> 8, of which waited for: 3 -> 2; matrix products, arithmetic and copies ran while one was open for 3% -> 5% of each run, Pallas kernels for 20% -> 18%
where the time goes in v2:
time: 72 us; the launch traced here: 71.7 us
  blocking collectives  29.3 us (41%)
  starting transfers between devices  19.8 us (28%)
  Pallas kernels  14.2 us (20%)
  waiting for transfers between devices  4.35 us (6%)
  local copies, waits for them, and re-layouts  3.35 us (5%)
    all_to_all x1, blocking collectives, shared(): rows = lax.all_to_all(rows, ('gx', 'gy'), 0, 0)  29.3 us
    ppermute x7, starting transfers between devices, shifted(): return lax.ppermute(value, axis, pairs)  15.9 us
    pallas_call x7, Pallas kernels, call(): pl.pallas_call(kernel, out_shape=shapes, in_specs=specs, out_specs=[VMEM]...  11.6 us
    all_to_all x1, starting transfers between devices, shared(): rows = lax.all_to_all(rows, ('gx', 'gy'), 0, 0)  3.92 us
    slice x2, local copies, waits for them, and re-layouts, body(): cuts.append(lax.slice_in_dim(salt_store, start, start + size))  3.34 us
    pallas_call x2, Pallas kernels, finish(): pl.pallas_call(functools.partial(salt_kernel, levels, first), out_shape=j...  2.6 us
    ppermute x7, waiting for transfers between devices, shifted(): return lax.ppermute(value, axis, pairs)  2.23 us
    all_to_all x1, waiting for transfers between devices, shared(): rows = lax.all_to_all(rows, ('gx', 'gy'), 0, 0)  2.12 us
  transfers between devices with their start and end apart: 8, of which 2 were waited for; matrix products, arithmetic and copies ran while one was open for 5% of the time, Pallas kernels for 18%

profile of v2, /device:TPU:0, one launch (start us, length us, event | category | flops | bytes accessed | tf_op | source)
XLA Modules:
  0.0 71.7 jit_solution(4670585864591015717)
XLA Ops:
  0.6 4.1 %collective-permute-start.4 = (f32[8,128,128]{2,1,0:T(8,128)}, f32[8,128,128]{2,1,0:T(8,128)S(1)}, u32[]{:S(2)}, u32[]{:S(2)}) collective-permute-start(f32[8,128,128]{2,1,0:T(8,128)} %param.13), channel_id=1, source_target_pairs={{0,16},{2,18},{4,20},{6,22},{8,24},{10,26},{12,28},{14,30},{16,0},... | collective-permute-start | bytes 1572872 | tf_op jit(solution)/shard_map/ppermute | solution.py:417
  4.8 1.7 %slice.6 = f32[5,128,128]{2,1,0:T(8,128)} slice(f32[8,128,128]{2,1,0:T(8,128)} %param.14), slice={[0:5], [0:128], [0:128]} | slice | bytes 655360 | tf_op jit(solution)/shard_map/slice | solution.py:472
  6.5 1.6 %slice.7 = f32[3,128,128]{2,1,0:T(8,128)} slice(f32[8,128,128]{2,1,0:T(8,128)} %param.14), slice={[5:8], [0:128], [0:128]} | slice | bytes 393216 | tf_op jit(solution)/shard_map/slice | solution.py:472
  8.1 1.4 %shard_map.112 = (f32[3,128,128]{2,1,0:T(8,128)S(1)}, f32[32,128]{1,0:T(8,128)S(1)}) custom-call(f32[128,128]{1,0:T(8,128)} %height.1, s32[8,128,128]{2,1,0:T(8,128)} %mask.11, f32[128,128]{1,0:T(8,128)} %depth.1, f32[8,128,128]{2,1,0:T(8,128)} %temp.5, f32[8,128,128]{2,1,0:T(8,128)} %north.3), custom_call_target="tpu_custom_call" | custom-call | flops 4000000 | bytes 1000000 | tf_op jit(solution)/shard_map/pallas_call | solution.py:44
  9.5 0.0 copy-start.1
  9.5 1.3 %shard_map.115 = f32[32,1,128]{2,1,0:T(1,128)S(1)} custom-call(f32[3,128,128]{2,1,0:T(8,128)S(1)} %get-tuple-element.18.fields), custom_call_target="tpu_custom_call" | custom-call | flops 4000000 | bytes 1000000 | tf_op jit(solution)/shard_map/pallas_call | solution.py:44
  10.9 0.1 collective-permute-start.6
  10.9 2.9 %collective-permute-start.5 = (f32[3,128,128]{2,1,0:T(8,128)}, f32[3,128,128]{2,1,0:T(8,128)S(1)}, u32[]{:S(2)}, u32[]{:S(2)}) collective-permute-start(f32[3,128,128]{2,1,0:T(8,128)} %slice.7), channel_id=1, source_target_pairs={{0,16},{2,18},{4,20},{6,22},{8,24},{10,26},{12,28},{14,30},{16,0},... | collective-permute-start | bytes 589832 | tf_op jit(solution)/shard_map/ppermute | solution.py:417
  13.8 1.5 %collective-permute-start.1 = (f32[32,128]{1,0:T(8,128)S(1)}, f32[32,128]{1,0:T(8,128)S(1)}, u32[]{:S(2)}, u32[]{:S(2)}) collective-permute-start(f32[32,128]{1,0:T(8,128)S(1)} %get-tuple-element.19), channel_id=1, source_target_pairs={{0,1},{1,0},{2,3},{3,2},{4,5},{5,4},{6,7},{7,6},{8,9},{9,8},{10,11... | collective-permute-start | bytes 49160 | tf_op jit(solution)/shard_map/ppermute | solution.py:417
  15.4 2.2 %collective-permute-done.1.refs_0_ = f32[32,128]{1,0:T(8,128)S(1)} collective-permute-done((f32[32,128]{1,0:T(8,128)S(1)}, f32[32,128]{1,0:T(8,128)S(1)}, u32[]{:S(2)}, u32[]{:S(2)}) %collective-permute-start.1) | collective-permute-done | bytes 16416 | tf_op jit(solution)/shard_map/ppermute | solution.py:417
  17.6 1.8 %shard_map.113 = (f32[32,128]{1,0:T(8,128)S(1)}, f32[32,128]{1,0:T(8,128)S(1)}, f32[32,256]{1,0:T(8,128)S(1)}, f32[32,256]{1,0:T(8,128)S(1)}) custom-call(f32[3,128,128]{2,1,0:T(8,128)S(1)} %get-tuple-element.18.fields, s32[8,128,128]{2,1,0:T(8,128)} %mask.11, f32[8,128,128]{2,1,0:T(8,128)} %temp.5, f32[8,128,128]{2,1,0:T(8,128)} %east.3, ...), custom_call_target="tpu_custom_call" | custom-call | flops 4000000 | bytes 1000000 | tf_op jit(solution)/shard_map/pallas_call | solution.py:44
  19.4 0.1 collective-permute-start.2
  19.4 4.4 %collective-permute-start.3 = (f32[32,256]{1,0:T(8,128)S(1)}, f32[32,256]{1,0:T(8,128)S(1)}, u32[]{:S(2)}, u32[]{:S(2)}) collective-permute-start(f32[32,256]{1,0:T(8,128)S(1)} %get-tuple-element.23), channel_id=1, source_target_pairs={{0,30},{2,0},{4,2},{6,4},{8,6},{10,8},{12,10},{14,12},{16,14},{18,... | collective-permute-start | bytes 98312 | tf_op jit(solution)/shard_map/ppermute | solution.py:417
  23.9 29.3 %all_to_all.10 = f32[32,1,128]{2,1,0:T(1,128)S(1)} all-to-all(f32[32,1,128]{2,1,0:T(1,128)S(1)} %shard_map.115), channel_id=1, replica_groups=mesh['gx'=16,'gy'=2] {'gx','gy'}, dimensions={0} | all-to-all | bytes 32768 | tf_op jit(solution)/shard_map/all_to_all | solution.py:421
  53.2 2.4 %shard_map.116 = (f32[9,144,256]{2,1,0:T(8,128)S(1)}, f32[32,1,128]{2,1,0:T(1,128)}) custom-call(f32[3,128,128]{2,1,0:T(8,128)S(1)} %get-tuple-element.18.fields, f32[32,128]{1,0:T(8,128)S(1)} %get-tuple-element.20.from_south, f32[32,128]{1,0:T(8,128)S(1)} %get-tuple-element.21.from_north, f32[32,256]{1,0:T(8,128)S(1)} %collective-permute-done.2.from_west, ...), custom_call_target="tpu_custom_call" | custom-call | flops 4000000 | bytes 1000000 | tf_op jit(solution)/shard_map/pallas_call | solution.py:44
  55.5 3.9 %all-to-all-start.1 = ((f32[32,1,128]{2,1,0:T(1,128)}), f32[32,1,128]{2,1,0:T(1,128)S(1)}, u32[]{:S(2)}, u32[]{:S(2)}) async-start(f32[32,1,128]{2,1,0:T(1,128)} %get-tuple-element.25), calls=%async_computation.1 | async-start | bytes 32768 | tf_op jit(solution)/shard_map/all_to_all | solution.py:421
  59.5 2.7 %collective-permute-start = (s32[1,1,8]{2,1,0:T(1,128)S(1)}, s32[1,1,8]{2,1,0:T(1,128)S(1)}, u32[]{:S(2)}, u32[]{:S(2)}) collective-permute-start(s32[1,1,8]{2,1,0:T(1,128)S(1)} %copy-done.1), channel_id=1, source_target_pairs={{0,16},{2,18},{4,20},{6,22},{8,24},{10,26},{12,28},{14,30},{16,0},... | collective-permute-start | bytes 104 | tf_op jit(solution)/shard_map/ppermute | solution.py:417
  62.2 2.3 %shard_map.114.tracer = f32[8,128,128]{2,1,0:T(8,128)S(1)} custom-call(f32[8,128,128]{2,1,0:T(8,128)} %temp.5, f32[8,128,128]{2,1,0:T(8,128)} %east.3, f32[8,128,128]{2,1,0:T(8,128)} %north.3, s32[8,128,128]{2,1,0:T(8,128)} %mask.11, f32[32,128]{1,0:T(8,128)S(1)} %get-tuple-element.20.from_south, f32[32,128]{1,0:T(8,128)S(1)} %get-tuple-element.21.from_north, ...), custom_call_target="tpu_custom_call" | custom-call | flops 4000000 | bytes 1000000 | tf_op jit(solution)/shard_map/pallas_call | solution.py:44
  64.5 0.0 copy-start
  64.5 2.1 %all-to-all-done.1 = f32[32,1,128]{2,1,0:T(1,128)S(1)} async-done(((f32[32,1,128]{2,1,0:T(1,128)}), f32[32,1,128]{2,1,0:T(1,128)S(1)}, u32[]{:S(2)}, u32[]{:S(2)}) %all-to-all-start.1) | async-done | bytes 16416 | tf_op jit(solution)/shard_map/all_to_all | solution.py:421
  66.6 1.0 %shard_map.117 = (f32[128,128]{1,0:T(8,128)}, f32[128,128]{1,0:T(8,128)S(1)}) custom-call(f32[32,128]{1,0:T(8,128)S(1)} %bitcast.3, f32[9,144,256]{2,1,0:T(8,128)S(1)} %get-tuple-element.26.basis), custom_call_target="tpu_custom_call" | custom-call | flops 4000000 | bytes 1000000 | tf_op jit(solution)/shard_map/pallas_call | solution.py:44
  67.6 1.5 %shard_map.118 = (f32[8,128,128]{2,1,0:T(8,128)S(1)}, f32[8,128,128]{2,1,0:T(8,128)}) custom-call(s32[8]{0:T(128)S(1)} %bitcast.5, f32[8,128,128]{2,1,0:T(8,128)S(1)} %shard_map.114.tracer, f32[128,128]{1,0:T(8,128)S(1)} %get-tuple-element.27.pressure, s32[8,128,128]{2,1,0:T(8,128)S(1)} %copy-done, f32[8,128,128]{2,1,0:T(8,128)S(1)} %collective-permute-done.4.refs_0_), custom_call_target="tpu_custom_call" | custom-call | flops 4000000 | bytes 1000000 | tf_op jit(solution)/shard_map/pallas_call | solution.py:44
  69.1 1.3 %shard_map.119.refs_0_ = f32[8,128,128]{2,1,0:T(8,128)} custom-call(s32[8]{0:T(128)S(1)} %bitcast.6, f32[8,128,128]{2,1,0:T(8,128)S(1)} %get-tuple-element.28.partial, f32[128,128]{1,0:T(8,128)S(1)} %get-tuple-element.27.pressure, s32[8,128,128]{2,1,0:T(8,128)S(1)} %copy-done, f32[5,128,128]{2,1,0:T(8,128)S(1)} %collective-permute-done.6.part), custom_call_target="tpu_custom_call" | custom-call | flops 1000000 | bytes 1000000 | tf_op jit(solution)/shard_map/pallas_call | solution.py:399
  70.5 1.3 %shard_map.120 = f32[8,128,128]{2,1,0:T(8,128)} custom-call(s32[8]{0:T(128)S(1)} %bitcast.7, f32[8,128,128]{2,1,0:T(8,128)S(1)} %get-tuple-element.28.partial, f32[128,128]{1,0:T(8,128)S(1)} %get-tuple-element.27.pressure, s32[8,128,128]{2,1,0:T(8,128)S(1)} %copy-done, ...), custom_call_target="tpu_custom_call", output_to_operand_aliasing={{}: (5, {})} | custom-call | flops 1000000 | bytes 1000000 | tf_op jit(solution)/shard_map/pallas_call | solution.py:399
  (8 shorter events, 0.0 us)
Async XLA Ops:
  0.6 67.0 %collective-permute-start.4 = (f32[8,128,128]{2,1,0:T(8,128)}, f32[8,128,128]{2,1,0:T(8,128)S(1)}, u32[]{:S(2)}, u32[]{:S(2)}) collective-permute-start(f32[8,128,128]{2,1,0:T(8,128)} %param.13), channel_id=1, source_target_pairs={{0,16},{2,18},{4,20},{6,22},{8,24},{10,26},{12,28},{14,30},{16,0},... | collective-permute-start | bytes 1572872 | tf_op jit(solution)/shard_map/ppermute | solution.py:417
  9.5 49.9 %copy-start.1 = (s32[1,1,8]{2,1,0:T(1,128)S(1)}, s32[1,1,8]{2,1,0:T(1,128)}, u32[]{:S(2)}) copy-start(s32[1,1,8]{2,1,0:T(1,128)} %param.15) | copy-start | bytes 100
  10.9 58.3 %collective-permute-start.6 = (f32[5,128,128]{2,1,0:T(8,128)}, f32[5,128,128]{2,1,0:T(8,128)S(1)}, u32[]{:S(2)}, u32[]{:S(2)}) collective-permute-start(f32[5,128,128]{2,1,0:T(8,128)} %slice.6), channel_id=1, source_target_pairs={{0,16},{2,18},{4,20},{6,22},{8,24},{10,26},{12,28},{14,30},{16,0},... | collective-permute-start | bytes 983048 | tf_op jit(solution)/shard_map/ppermute | solution.py:417
  10.9 59.5 %collective-permute-start.5 = (f32[3,128,128]{2,1,0:T(8,128)}, f32[3,128,128]{2,1,0:T(8,128)S(1)}, u32[]{:S(2)}, u32[]{:S(2)}) collective-permute-start(f32[3,128,128]{2,1,0:T(8,128)} %slice.7), channel_id=1, source_target_pairs={{0,16},{2,18},{4,20},{6,22},{8,24},{10,26},{12,28},{14,30},{16,0},... | collective-permute-start | bytes 589832 | tf_op jit(solution)/shard_map/ppermute | solution.py:417
  13.8 3.7 %collective-permute-start.1 = (f32[32,128]{1,0:T(8,128)S(1)}, f32[32,128]{1,0:T(8,128)S(1)}, u32[]{:S(2)}, u32[]{:S(2)}) collective-permute-start(f32[32,128]{1,0:T(8,128)S(1)} %get-tuple-element.19), channel_id=1, source_target_pairs={{0,1},{1,0},{2,3},{3,2},{4,5},{5,4},{6,7},{7,6},{8,9},{9,8},{10,11... | collective-permute-start | bytes 49160 | tf_op jit(solution)/shard_map/ppermute | solution.py:417
  19.4 33.8 %collective-permute-start.2 = (f32[32,256]{1,0:T(8,128)S(1)}, f32[32,256]{1,0:T(8,128)S(1)}, u32[]{:S(2)}, u32[]{:S(2)}) collective-permute-start(f32[32,256]{1,0:T(8,128)S(1)} %get-tuple-element.22), channel_id=1, source_target_pairs={{0,2},{2,4},{4,6},{6,8},{8,10},{10,12},{12,14},{14,16},{16,18},{18... | collective-permute-start | bytes 98312 | tf_op jit(solution)/shard_map/ppermute | solution.py:417
  19.4 33.7 %collective-permute-start.3 = (f32[32,256]{1,0:T(8,128)S(1)}, f32[32,256]{1,0:T(8,128)S(1)}, u32[]{:S(2)}, u32[]{:S(2)}) collective-permute-start(f32[32,256]{1,0:T(8,128)S(1)} %get-tuple-element.23), channel_id=1, source_target_pairs={{0,30},{2,0},{4,2},{6,4},{8,6},{10,8},{12,10},{14,12},{16,14},{18,... | collective-permute-start | bytes 98312 | tf_op jit(solution)/shard_map/ppermute | solution.py:417
  55.5 11.1 %all-to-all-start.1 = ((f32[32,1,128]{2,1,0:T(1,128)}), f32[32,1,128]{2,1,0:T(1,128)S(1)}, u32[]{:S(2)}, u32[]{:S(2)}) async-start(f32[32,1,128]{2,1,0:T(1,128)} %get-tuple-element.25), calls=%async_computation.1 | async-start | bytes 32768 | tf_op jit(solution)/shard_map/all_to_all | solution.py:421
  59.5 8.1 %collective-permute-start = (s32[1,1,8]{2,1,0:T(1,128)S(1)}, s32[1,1,8]{2,1,0:T(1,128)S(1)}, u32[]{:S(2)}, u32[]{:S(2)}) collective-permute-start(s32[1,1,8]{2,1,0:T(1,128)S(1)} %copy-done.1), channel_id=1, source_target_pairs={{0,16},{2,18},{4,20},{6,22},{8,24},{10,26},{12,28},{14,30},{16,0},... | collective-permute-start | bytes 104 | tf_op jit(solution)/shard_map/ppermute | solution.py:417
  64.5 3.1 %copy-start = (s32[8,128,128]{2,1,0:T(8,128)S(1)}, s32[8,128,128]{2,1,0:T(8,128)}, u32[]{:S(2)}) copy-start(s32[8,128,128]{2,1,0:T(8,128)} %mask.11) | copy-start | bytes 1572868

commit v3 on v2

--- a/solution.py
+++ b/solution.py
@@ -321,27 +321,22 @@
     pressure[...] = -GRAVITY * pull[:rows, :columns]
 
 
-def tracer_kernel(
-    levels, temp, east, north, mask, from_south, from_north, from_west, from_east, tracer
-):
+def tracer_kernel(levels, temp, east, north, mask, from_south, from_north, tracer):
     rows, columns = temp.shape[1:]
     row = lax.broadcasted_iota(jnp.int32, (rows, columns), 0)
     lane = lane_index((rows, columns))
     base = 3 * RING
-    tracer_sides = beside_tile(from_west, from_east, base, levels)[:rows]
     for level in range(levels):
         masked = mask[level].astype(jnp.float32) * temp[level]
         east_coef = DIFFUSE - 0.5 * east[level]
         west_coef = DIFFUSE + 0.5 * east[level]
         north_coef = DIFFUSE - 0.5 * north[level]
         south_coef = DIFFUSE + 0.5 * north[level]
-        side_west = tracer_sides[:, LANES - levels + level : LANES - levels + level + 1]
-        side_east = tracer_sides[:, level : level + 1]
         side_south = from_south[base + level : base + level + 1, :]
         side_north = from_north[base + level : base + level + 1, :]
-        inflow = jnp.where(lane == 0, side_west, pltpu.roll(east_coef * masked, 1, 1))
+        inflow = jnp.where(lane == 0, 0.0, pltpu.roll(east_coef * masked, 1, 1))
         inflow = inflow + jnp.where(
-            lane == columns - 1, side_east, pltpu.roll(west_coef * masked, columns - 1, 1)
+            lane == columns - 1, 0.0, pltpu.roll(west_coef * masked, columns - 1, 1)
         )
         inflow = inflow + jnp.where(row == 0, side_south, pltpu.roll(north_coef * masked, 1, 0))
         inflow = inflow + jnp.where(
@@ -364,17 +359,21 @@
     return thickness * pressure[...] * mask[level].astype(jnp.float32)
 
 
-def warm_kernel(levels, sizes, slots, tracer, pressure, mask, *refs):
-    parts, (partial, salt) = refs[: len(sizes)], refs[len(sizes) :]
-    slot = 0
-    for size, part in zip(sizes, parts):
-        for at in range(size):
-            level = level_of_slot(slots, slot, levels)
-            dense = density(level, levels, pressure, mask)
-            warm = part[at]
-            salt[level] = (HALINE + CABBELING * warm) * dense
-            partial[level] = tracer[level] + (THERMAL + 2.0 * NONLINEAR * warm) * dense
-            slot += 1
+def warm_kernel(levels, slots, tracer, pressure, from_west, from_east, mask, warm, partial, salt):
+    rows, columns = pressure.shape
+    lane = lane_index((rows, columns))
+    sides = beside_tile(from_west, from_east, 3 * RING, levels)[:rows]
+    for level in range(levels):
+        side_west = sides[:, LANES - levels + level : LANES - levels + level + 1]
+        side_east = sides[:, level : level + 1]
+        edge = jnp.where(lane == 0, side_west, 0.0) + jnp.where(lane == columns - 1, side_east, 0.0)
+        partial[level] = tracer[level] + TIMESTEP * edge
+    for slot in range(levels):
+        level = level_of_slot(slots, slot, levels)
+        dense = density(level, levels, pressure, mask)
+        value = warm[slot]
+        salt[level] = (HALINE + CABBELING * value) * dense
+        partial[level] = partial[level] + (THERMAL + 2.0 * NONLINEAR * value) * dense
 
 
 def salt_kernel(levels, first, slots, partial, pressure, mask, part, *refs):
@@ -423,8 +422,7 @@
 
 
 def runs(levels):
-    most = 5 * levels // 8
-    return (levels,), (most, levels - most)
+    return levels // 2, levels - levels // 2
 
 
 def body(
@@ -444,9 +442,9 @@
     strip = 3 * RING + levels
     full = (rows + 2 * RING, columns + LANES)
 
-    warm_sizes, salt_sizes = runs(levels)
+    salt_sizes = runs(levels)
     slots = shifted(slot_map, "gx", half_cycle, True).reshape(-1)
-    warm_parts = [shifted(temp_store, "gx", half_cycle, True)]
+    warm = shifted(temp_store, "gx", half_cycle, True)
 
     swap = lax.axis_size("gy") == 2
     fields, *messages = call(
@@ -467,11 +465,17 @@
     )
     from_west = shifted(to_east, "gx", 1, True)
     from_east = shifted(to_west, "gx", -1, True)
+    (tracer,) = call(
+        functools.partial(tracer_kernel, levels),
+        [temp_adjoint.shape],
+        stored(temp_adjoint, east_velocity, north_velocity, land_mask)
+        + held(from_south, from_north),
+        keep=[False],
+    )
     cuts, start = [], 0
     for size in salt_sizes:
         cuts.append(lax.slice_in_dim(salt_store, start, start + size))
         start += size
-    *cuts, tile_rows = lax.optimization_barrier((*cuts, tile_rows))
     tiles = shared(tile_rows)
     salt_parts = [shifted(cut, "gx", half_cycle, True) for cut in cuts]
     beside = held(from_south, from_north, from_west, from_east)
@@ -479,17 +483,12 @@
         krylov_kernel, [(ITERS + 3,) + full, (devices, 1, LANES)], held(fields) + beside + held(tiles)
     )
     gathered = shared(products)
-    (tracer,) = call(
-        functools.partial(tracer_kernel, levels),
-        [temp_adjoint.shape],
-        stored(temp_adjoint, east_velocity, north_velocity, land_mask) + beside,
-    )
     surface, pressure = call(solve_kernel, [(rows, columns)] * 2, held(gathered, basis), keep=[False, True])
     partial, salt_back = call(
-        functools.partial(warm_kernel, levels, warm_sizes),
+        functools.partial(warm_kernel, levels),
         [temp_adjoint.shape] * 2,
-        free(slots) + held(tracer, pressure) + free(land_mask, *warm_parts),
-        specs=[SMEM] + [VMEM] * (3 + len(warm_sizes)),
+        free(slots) + stored(tracer) + held(pressure, from_west, from_east) + free(land_mask, warm),
+        specs=[SMEM] + [VMEM] * 6,
         keep=[True, False],
     )
     temp_back, first = None, 0

time: 72 us -> 73.1 us (1.015)
  blocking collectives: 29.3 us -> 31.5 us
  local copies, waits for them, and re-layouts: 3.35 us -> 1.86 us
  Pallas kernels: 14.2 us -> 15 us
    slice x2 -> x1, local copies, waits for them, and re-layouts: 3.34 us -> 1.06 us  [body(): cuts.append(lax.slice_in_dim(salt_store, start, start + size))]
    all_to_all x1, blocking collectives: 29.3 us -> 31.5 us  [shared(): rows = lax.all_to_all(rows, ('gx', 'gy'), 0, 0)]
    unnamed x4 -> x6, local copies, waits for them, and re-layouts: 0.01 us -> 0.8 us
    pallas_call x7, Pallas kernels: 11.6 us -> 12.4 us  [call(): pl.pallas_call(kernel, out_shape=shapes, in_specs=specs, out_specs=[VMEM]...]
  transfers between devices with their start and end apart: 8 -> 8, of which waited for: 2 -> 2; matrix products, arithmetic and copies ran while one was open for 5% -> 1% of each run, Pallas kernels for 18% -> 19%
where the time goes in v3:
time: 73.1 us; the launch traced here: 72.8 us
  blocking collectives  31.5 us (43%)
  starting transfers between devices  19.8 us (27%)
  Pallas kernels  15 us (21%)
  waiting for transfers between devices  3.82 us (5%)
  local copies, waits for them, and re-layouts  1.86 us (3%)
    all_to_all x1, blocking collectives, shared(): rows = lax.all_to_all(rows, ('gx', 'gy'), 0, 0)  31.5 us
    ppermute x7, starting transfers between devices, shifted(): return lax.ppermute(value, axis, pairs)  15.9 us
    pallas_call x7, Pallas kernels, call(): pl.pallas_call(kernel, out_shape=shapes, in_specs=specs, out_specs=[VMEM]...  12.4 us
    all_to_all x1, starting transfers between devices, shared(): rows = lax.all_to_all(rows, ('gx', 'gy'), 0, 0)  3.92 us
    pallas_call x2, Pallas kernels, finish(): pl.pallas_call(functools.partial(salt_kernel, levels, first), out_shape=j...  2.6 us
    ppermute x7, waiting for transfers between devices, shifted(): return lax.ppermute(value, axis, pairs)  2.23 us
    all_to_all x1, waiting for transfers between devices, shared(): rows = lax.all_to_all(rows, ('gx', 'gy'), 0, 0)  1.59 us
  transfers between devices with their start and end apart: 8, of which 2 were waited for; matrix products, arithmetic and copies ran while one was open for 1% of the time, Pallas kernels for 19%

profile of v3, /device:TPU:0, one launch (start us, length us, event | category | flops | bytes accessed | tf_op | source)
XLA Modules:
  0.0 72.8 jit_solution(5988252267418958045)
XLA Ops:
  0.6 4.1 %collective-permute-start.4 = (f32[8,128,128]{2,1,0:T(8,128)}, f32[8,128,128]{2,1,0:T(8,128)S(1)}, u32[]{:S(2)}, u32[]{:S(2)}) collective-permute-start(f32[8,128,128]{2,1,0:T(8,128)} %param.13), channel_id=1, source_target_pairs={{0,16},{2,18},{4,20},{6,22},{8,24},{10,26},{12,28},{14,30},{16,0},... | collective-permute-start | bytes 1572872 | tf_op jit(solution)/shard_map/ppermute | solution.py:416
  4.8 1.1 %fusion = (f32[4,128,128]{2,1,0:T(8,128)S(1)}, f32[4,128,128]{2,1,0:T(8,128)S(1)}) fusion(f32[8,128,128]{2,1,0:T(8,128)} %param.14), kind=kLoop, calls=%fused_computation | loop fusion | bytes 1048576 | tf_op jit(solution)/shard_map/slice | solution.py:477
  5.8 0.1 collective-permute-start.6
  5.9 2.9 %collective-permute-start.5 = (f32[4,128,128]{2,1,0:T(8,128)S(1)}, f32[4,128,128]{2,1,0:T(8,128)S(1)}, u32[]{:S(2)}, u32[]{:S(2)}) collective-permute-start(f32[4,128,128]{2,1,0:T(8,128)S(1)} %get-tuple-element.28), channel_id=1, source_target_pairs={{0,16},{2,18},{4,20},{6,22},{8,24},{10,26},{12,28},{14,30},{16,0},... | collective-permute-start | bytes 786440 | tf_op jit(solution)/shard_map/ppermute | solution.py:416
  8.8 1.4 %shard_map.112 = (f32[3,128,128]{2,1,0:T(8,128)S(1)}, f32[32,128]{1,0:T(8,128)S(1)}) custom-call(f32[128,128]{1,0:T(8,128)} %height.1, s32[8,128,128]{2,1,0:T(8,128)} %mask.11, f32[128,128]{1,0:T(8,128)} %depth.1, f32[8,128,128]{2,1,0:T(8,128)} %temp.5, f32[8,128,128]{2,1,0:T(8,128)} %north.3), custom_call_target="tpu_custom_call" | custom-call | flops 4000000 | bytes 1000000 | tf_op jit(solution)/shard_map/pallas_call | solution.py:44
  10.2 0.0 copy-start.2
  10.3 1.6 %collective-permute-start.1 = (f32[32,128]{1,0:T(8,128)S(1)}, f32[32,128]{1,0:T(8,128)S(1)}, u32[]{:S(2)}, u32[]{:S(2)}) collective-permute-start(f32[32,128]{1,0:T(8,128)S(1)} %get-tuple-element.16), channel_id=1, source_target_pairs={{0,1},{1,0},{2,3},{3,2},{4,5},{5,4},{6,7},{7,6},{8,9},{9,8},{10,11... | collective-permute-start | bytes 49160 | tf_op jit(solution)/shard_map/ppermute | solution.py:416
  11.8 2.2 %collective-permute-done.1.refs_0_ = f32[32,128]{1,0:T(8,128)S(1)} collective-permute-done((f32[32,128]{1,0:T(8,128)S(1)}, f32[32,128]{1,0:T(8,128)S(1)}, u32[]{:S(2)}, u32[]{:S(2)}) %collective-permute-start.1) | collective-permute-done | bytes 16416 | tf_op jit(solution)/shard_map/ppermute | solution.py:416
  14.1 1.8 %shard_map.113 = (f32[32,128]{1,0:T(8,128)S(1)}, f32[32,128]{1,0:T(8,128)S(1)}, f32[32,256]{1,0:T(8,128)S(1)}, f32[32,256]{1,0:T(8,128)S(1)}) custom-call(f32[3,128,128]{2,1,0:T(8,128)S(1)} %get-tuple-element.15.fields, s32[8,128,128]{2,1,0:T(8,128)} %mask.11, f32[8,128,128]{2,1,0:T(8,128)} %temp.5, f32[8,128,128]{2,1,0:T(8,128)} %east.3, ...), custom_call_target="tpu_custom_call" | custom-call | flops 4000000 | bytes 1000000 | tf_op jit(solution)/shard_map/pallas_call | solution.py:44
  15.9 0.1 collective-permute-start.2
  15.9 4.4 %collective-permute-start.3 = (f32[32,256]{1,0:T(8,128)S(1)}, f32[32,256]{1,0:T(8,128)S(1)}, u32[]{:S(2)}, u32[]{:S(2)}) collective-permute-start(f32[32,256]{1,0:T(8,128)S(1)} %get-tuple-element.20), channel_id=1, source_target_pairs={{0,30},{2,0},{4,2},{6,4},{8,6},{10,8},{12,10},{14,12},{16,14},{18,... | collective-permute-start | bytes 98312 | tf_op jit(solution)/shard_map/ppermute | solution.py:416
  20.4 1.3 %shard_map.115 = f32[32,1,128]{2,1,0:T(1,128)S(1)} custom-call(f32[3,128,128]{2,1,0:T(8,128)S(1)} %get-tuple-element.15.fields), custom_call_target="tpu_custom_call" | custom-call | flops 4000000 | bytes 1000000 | tf_op jit(solution)/shard_map/pallas_call | solution.py:44
  21.7 31.5 %all_to_all.10 = f32[32,1,128]{2,1,0:T(1,128)S(1)} all-to-all(f32[32,1,128]{2,1,0:T(1,128)S(1)} %shard_map.115), channel_id=1, replica_groups=mesh['gx'=16,'gy'=2] {'gx','gy'}, dimensions={0} | all-to-all | bytes 32768 | tf_op jit(solution)/shard_map/all_to_all | solution.py:420
  53.2 2.4 %shard_map.116 = (f32[9,144,256]{2,1,0:T(8,128)S(1)}, f32[32,1,128]{2,1,0:T(1,128)}) custom-call(f32[3,128,128]{2,1,0:T(8,128)S(1)} %get-tuple-element.15.fields, f32[32,128]{1,0:T(8,128)S(1)} %get-tuple-element.17.from_south, f32[32,128]{1,0:T(8,128)S(1)} %get-tuple-element.18.from_north, f32[32,256]{1,0:T(8,128)S(1)} %collective-permute-done.2.from_west, ...), custom_call_target="tpu_custom_call" | custom-call | flops 4000000 | bytes 1000000 | tf_op jit(solution)/shard_map/pallas_call | solution.py:44
  55.5 3.9 %all-to-all-start.1 = ((f32[32,1,128]{2,1,0:T(1,128)}), f32[32,1,128]{2,1,0:T(1,128)S(1)}, u32[]{:S(2)}, u32[]{:S(2)}) async-start(f32[32,1,128]{2,1,0:T(1,128)} %get-tuple-element.21), calls=%async_computation.1 | async-start | bytes 32768 | tf_op jit(solution)/shard_map/all_to_all | solution.py:420
  59.5 2.7 %collective-permute-start = (s32[1,1,8]{2,1,0:T(1,128)S(1)}, s32[1,1,8]{2,1,0:T(1,128)S(1)}, u32[]{:S(2)}, u32[]{:S(2)}) collective-permute-start(s32[1,1,8]{2,1,0:T(1,128)S(1)} %copy-done.2), channel_id=1, source_target_pairs={{0,16},{2,18},{4,20},{6,22},{8,24},{10,26},{12,28},{14,30},{16,0},... | collective-permute-start | bytes 104 | tf_op jit(solution)/shard_map/ppermute | solution.py:416
  62.2 2.0 %shard_map.114.tracer = f32[8,128,128]{2,1,0:T(8,128)S(1)} custom-call(f32[8,128,128]{2,1,0:T(8,128)} %temp.5, f32[8,128,128]{2,1,0:T(8,128)} %east.3, f32[8,128,128]{2,1,0:T(8,128)} %north.3, s32[8,128,128]{2,1,0:T(8,128)} %mask.11, f32[32,128]{1,0:T(8,128)S(1)} %get-tuple-element.17.from_south, f32[32,128]{1,0:T(8,128)S(1)} %get-tuple-element.18.from_north), custom_call_target="tpu_custom_call" | custom-call | flops 4000000 | bytes 1000000 | tf_op jit(solution)/shard_map/pallas_call | solution.py:44
  64.2 0.0 copy-start.1
  64.2 0.8 %copy-done.1 = f32[8,128,128]{2,1,0:T(8,128)} copy-done((f32[8,128,128]{2,1,0:T(8,128)}, f32[8,128,128]{2,1,0:T(8,128)S(1)}, u32[]{:S(2)}) %copy-start.1) | copy-done | bytes 524312
  65.0 1.6 %all-to-all-done.1 = f32[32,1,128]{2,1,0:T(1,128)S(1)} async-done(((f32[32,1,128]{2,1,0:T(1,128)}), f32[32,1,128]{2,1,0:T(1,128)S(1)}, u32[]{:S(2)}, u32[]{:S(2)}) %all-to-all-start.1) | async-done | bytes 16416 | tf_op jit(solution)/shard_map/all_to_all | solution.py:420
  66.6 1.0 %shard_map.117 = (f32[128,128]{1,0:T(8,128)}, f32[128,128]{1,0:T(8,128)S(1)}) custom-call(f32[32,128]{1,0:T(8,128)S(1)} %bitcast.3, f32[9,144,256]{2,1,0:T(8,128)S(1)} %get-tuple-element.22.basis), custom_call_target="tpu_custom_call" | custom-call | flops 4000000 | bytes 1000000 | tf_op jit(solution)/shard_map/pallas_call | solution.py:44
  67.6 2.5 %shard_map.118 = (f32[8,128,128]{2,1,0:T(8,128)S(1)}, f32[8,128,128]{2,1,0:T(8,128)}) custom-call(s32[8]{0:T(128)S(1)} %bitcast.5, f32[8,128,128]{2,1,0:T(8,128)} %copy-done.1, f32[128,128]{1,0:T(8,128)S(1)} %get-tuple-element.23.pressure, f32[32,256]{1,0:T(8,128)S(1)} %collective-permute-done.2.from_west, f32[32,256]{1,0:T(8,128)S(1)} %collective-permute-done.3.from_east, ...), custom_call_target="tpu_custom_call" | custom-call | flops 4000000 | bytes 1000000 | tf_op jit(solution)/shard_map/pallas_call | solution.py:44
  70.1 1.3 %shard_map.119.refs_0_ = f32[8,128,128]{2,1,0:T(8,128)} custom-call(s32[8]{0:T(128)S(1)} %bitcast.6, f32[8,128,128]{2,1,0:T(8,128)S(1)} %get-tuple-element.24.partial, f32[128,128]{1,0:T(8,128)S(1)} %get-tuple-element.23.pressure, s32[8,128,128]{2,1,0:T(8,128)S(1)} %copy-done, f32[4,128,128]{2,1,0:T(8,128)S(1)} %collective-permute-done.6.part), custom_call_target="tpu_custom_call" | custom-call | flops 1000000 | bytes 1000000 | tf_op jit(solution)/shard_map/pallas_call | solution.py:398
  71.5 1.3 %shard_map.120 = f32[8,128,128]{2,1,0:T(8,128)} custom-call(s32[8]{0:T(128)S(1)} %bitcast.7, f32[8,128,128]{2,1,0:T(8,128)S(1)} %get-tuple-element.24.partial, f32[128,128]{1,0:T(8,128)S(1)} %get-tuple-element.23.pressure, s32[8,128,128]{2,1,0:T(8,128)S(1)} %copy-done, ...), custom_call_target="tpu_custom_call", output_to_operand_aliasing={{}: (5, {})} | custom-call | flops 1000000 | bytes 1000000 | tf_op jit(solution)/shard_map/pallas_call | solution.py:398
  (9 shorter events, 0.0 us)
Async XLA Ops:
  0.6 67.0 %collective-permute-start.4 = (f32[8,128,128]{2,1,0:T(8,128)}, f32[8,128,128]{2,1,0:T(8,128)S(1)}, u32[]{:S(2)}, u32[]{:S(2)}) collective-permute-start(f32[8,128,128]{2,1,0:T(8,128)} %param.13), channel_id=1, source_target_pairs={{0,16},{2,18},{4,20},{6,22},{8,24},{10,26},{12,28},{14,30},{16,0},... | collective-permute-start | bytes 1572872 | tf_op jit(solution)/shard_map/ppermute | solution.py:416
  5.8 64.3 %collective-permute-start.6 = (f32[4,128,128]{2,1,0:T(8,128)S(1)}, f32[4,128,128]{2,1,0:T(8,128)S(1)}, u32[]{:S(2)}, u32[]{:S(2)}) collective-permute-start(f32[4,128,128]{2,1,0:T(8,128)S(1)} %get-tuple-element.27), channel_id=1, source_target_pairs={{0,16},{2,18},{4,20},{6,22},{8,24},{10,26},{12,28},{14,30},{16,0},... | collective-permute-start | bytes 786440 | tf_op jit(solution)/shard_map/ppermute | solution.py:416
  5.9 65.5 %collective-permute-start.5 = (f32[4,128,128]{2,1,0:T(8,128)S(1)}, f32[4,128,128]{2,1,0:T(8,128)S(1)}, u32[]{:S(2)}, u32[]{:S(2)}) collective-permute-start(f32[4,128,128]{2,1,0:T(8,128)S(1)} %get-tuple-element.28), channel_id=1, source_target_pairs={{0,16},{2,18},{4,20},{6,22},{8,24},{10,26},{12,28},{14,30},{16,0},... | collective-permute-start | bytes 786440 | tf_op jit(solution)/shard_map/ppermute | solution.py:416
  10.2 49.2 %copy-start.2 = (s32[1,1,8]{2,1,0:T(1,128)S(1)}, s32[1,1,8]{2,1,0:T(1,128)}, u32[]{:S(2)}) copy-start(s32[1,1,8]{2,1,0:T(1,128)} %param.15) | copy-start | bytes 100
  10.3 3.8 %collective-permute-start.1 = (f32[32,128]{1,0:T(8,128)S(1)}, f32[32,128]{1,0:T(8,128)S(1)}, u32[]{:S(2)}, u32[]{:S(2)}) collective-permute-start(f32[32,128]{1,0:T(8,128)S(1)} %get-tuple-element.16), channel_id=1, source_target_pairs={{0,1},{1,0},{2,3},{3,2},{4,5},{5,4},{6,7},{7,6},{8,9},{9,8},{10,11... | collective-permute-start | bytes 49160 | tf_op jit(solution)/shard_map/ppermute | solution.py:416
  15.9 37.3 %collective-permute-start.2 = (f32[32,256]{1,0:T(8,128)S(1)}, f32[32,256]{1,0:T(8,128)S(1)}, u32[]{:S(2)}, u32[]{:S(2)}) collective-permute-start(f32[32,256]{1,0:T(8,128)S(1)} %get-tuple-element.19), channel_id=1, source_target_pairs={{0,2},{2,4},{4,6},{6,8},{8,10},{10,12},{12,14},{14,16},{16,18},{18... | collective-permute-start | bytes 98312 | tf_op jit(solution)/shard_map/ppermute | solution.py:416
  15.9 37.2 %collective-permute-start.3 = (f32[32,256]{1,0:T(8,128)S(1)}, f32[32,256]{1,0:T(8,128)S(1)}, u32[]{:S(2)}, u32[]{:S(2)}) collective-permute-start(f32[32,256]{1,0:T(8,128)S(1)} %get-tuple-element.20), channel_id=1, source_target_pairs={{0,30},{2,0},{4,2},{6,4},{8,6},{10,8},{12,10},{14,12},{16,14},{18,... | collective-permute-start | bytes 98312 | tf_op jit(solution)/shard_map/ppermute | solution.py:416
  55.5 11.1 %all-to-all-start.1 = ((f32[32,1,128]{2,1,0:T(1,128)}), f32[32,1,128]{2,1,0:T(1,128)S(1)}, u32[]{:S(2)}, u32[]{:S(2)}) async-start(f32[32,1,128]{2,1,0:T(1,128)} %get-tuple-element.21), calls=%async_computation.1 | async-start | bytes 32768 | tf_op jit(solution)/shard_map/all_to_all | solution.py:420
  59.5 8.1 %collective-permute-start = (s32[1,1,8]{2,1,0:T(1,128)S(1)}, s32[1,1,8]{2,1,0:T(1,128)S(1)}, u32[]{:S(2)}, u32[]{:S(2)}) collective-permute-start(s32[1,1,8]{2,1,0:T(1,128)S(1)} %copy-done.2), channel_id=1, source_target_pairs={{0,16},{2,18},{4,20},{6,22},{8,24},{10,26},{12,28},{14,30},{16,0},... | collective-permute-start | bytes 104 | tf_op jit(solution)/shard_map/ppermute | solution.py:416
  64.2 0.8 %copy-start.1 = (f32[8,128,128]{2,1,0:T(8,128)}, f32[8,128,128]{2,1,0:T(8,128)S(1)}, u32[]{:S(2)}) copy-start(f32[8,128,128]{2,1,0:T(8,128)S(1)} %shard_map.114.tracer) | copy-start | bytes 1572868
  65.0 2.6 %copy-start = (s32[8,128,128]{2,1,0:T(8,128)S(1)}, s32[8,128,128]{2,1,0:T(8,128)}, u32[]{:S(2)}) copy-start(s32[8,128,128]{2,1,0:T(8,128)} %mask.11) | copy-start | bytes 1572868

commit v4 on v3

--- a/solution.py
+++ b/solution.py
@@ -173,7 +173,9 @@
             link = jnp.where(alive, jnp.sqrt(jnp.maximum(left, 0.0)), 0.0)
             before, vector = vector, (image - along * vector) * scale
             out = jnp.where(at == OFF_AT + step, link, out)
-    row_out[...] = jnp.broadcast_to(out[None], row_out.shape)
+    place = lax.axis_index("gx") * lax.axis_size("gy") + lax.axis_index("gy")
+    own = lax.broadcasted_iota(jnp.int32, row_out.shape, 0) == place
+    row_out[...] = jnp.where(own, out, 0.0)
 
 
 def merged_recurrence(tiles):
@@ -250,12 +252,12 @@
     partial = [sum(part[:, k : k + LANES] for k in range(0, columns, LANES)) for part in partial]
     partial = partial + [jnp.zeros((LANES - len(partial), LANES), jnp.float32)]
     table = jnp.transpose(jnp.concatenate(partial, axis=0))
-    products[...] = jnp.broadcast_to(jnp.sum(table, axis=0, keepdims=True)[None], products.shape)
+    products[...] = jnp.sum(table, axis=0, keepdims=True)
 
 
 def solve_kernel(gathered, basis, surface, pressure):
     rows, columns = surface.shape
-    summed = jnp.sum(gathered[...], axis=0, keepdims=True)
+    summed = gathered[...]
     known = basis[ITERS + 2, :1, :LANES]
     at = lane_index((1, LANES))
 
@@ -416,13 +418,27 @@
     return lax.ppermute(value, axis, pairs)
 
 
-def shared(rows):
-    rows = lax.all_to_all(rows, ("gx", "gy"), 0, 0)
-    return rows.reshape(rows.shape[0], LANES)
+def swapped(value, axis, flip):
+    pairs = [(i, i ^ flip) for i in range(lax.axis_size(axis))]
+    return lax.ppermute(value, axis, pairs)
+
+
+def shared(value):
+    count_x, count_y = lax.axis_size("gx"), lax.axis_size("gy")
+    inner = 4
+    assert count_x & (count_x - 1) == 0 and count_y & (count_y - 1) == 0 and count_x >= inner
+    flips = [("gy", 1 << bit) for bit in range(count_y.bit_length() - 1)] + [("gx", 2), ("gx", 1)]
+    for axis, flip in flips:
+        value = value + swapped(value, axis, flip)
+    terms = [value] + [swapped(value, "gx", flip) for flip in range(inner, count_x, inner)]
+    while len(terms) > 1:
+        terms = [a + b for a, b in zip(terms[::2], terms[1::2])]
+    return terms[0]
 
 
 def runs(levels):
-    return levels // 2, levels - levels // 2
+    most = 5 * levels // 8
+    return most, levels - most
 
 
 def body(
@@ -457,7 +473,7 @@
     else:
         arrived = [shifted(messages[0], "gy", 1, False)]
         arrived += [shifted(messages[1], "gy", -1, False)]
-    (tile_rows,) = call(tile_basis_kernel, [(devices, 1, LANES)], held(fields))
+    (tile_rows,) = call(tile_basis_kernel, [(devices, LANES)], held(fields))
     from_south, from_north, to_east, to_west = call(
         functools.partial(pack_x_kernel, levels, len(arrived)),
         [(strip, columns)] * 2 + [(strip, rows + LANES)] * 2,
@@ -479,9 +495,7 @@
     tiles = shared(tile_rows)
     salt_parts = [shifted(cut, "gx", half_cycle, True) for cut in cuts]
     beside = held(from_south, from_north, from_west, from_east)
-    basis, products = call(
-        krylov_kernel, [(ITERS + 3,) + full, (devices, 1, LANES)], held(fields) + beside + held(tiles)
-    )
+    basis, products = call(krylov_kernel, [(ITERS + 3,) + full, (1, LANES)], held(fields) + beside + held(tiles))
     gathered = shared(products)
     surface, pressure = call(solve_kernel, [(rows, columns)] * 2, held(gathered, basis), keep=[False, True])
     partial, salt_back = call(

time: 73.1 us -> 76.6 us (1.048)
  blocking collectives: 31.5 us -> 0 us
  waiting for transfers between devices: 3.82 us -> 32 us
  starting transfers between devices: 19.8 us -> 28.3 us
  local copies, waits for them, and re-layouts: 1.86 us -> 0.84 us
    all_to_all x1 -> x0, blocking collectives: 31.5 us -> none  [shared(): rows = lax.all_to_all(rows, ('gx', 'gy'), 0, 0)]
    ppermute x0 -> x12, waiting for transfers between devices: none -> 25.3 us  [swapped(): return lax.ppermute(value, axis, pairs)]
    ppermute x0 -> x12, starting transfers between devices: none -> 16.1 us  [swapped(): return lax.ppermute(value, axis, pairs)]
    ppermute x7, waiting for transfers between devices: 2.23 us -> 6.78 us  [shifted(): return lax.ppermute(value, axis, pairs)]
    all_to_all x1 -> x0, starting transfers between devices: 3.92 us -> none  [shared(): rows = lax.all_to_all(rows, ('gx', 'gy'), 0, 0)]
    ppermute x7, starting transfers between devices: 15.9 us -> 12.2 us  [shifted(): return lax.ppermute(value, axis, pairs)]
    all_to_all x1 -> x0, waiting for transfers between devices: 1.59 us -> none  [shared(): rows = lax.all_to_all(rows, ('gx', 'gy'), 0, 0)]
    slice x1 -> x2, local copies, waits for them, and re-layouts: 1.06 us -> 0.04 us  [body(): cuts.append(lax.slice_in_dim(salt_store, start, start + size))]
  transfers between devices with their start and end apart: 8 -> 19, of which waited for: 2 -> 9; matrix products, arithmetic and copies ran while one was open for 1% -> 0% of each run, Pallas kernels for 19% -> 17%
where the time goes in v4:
time: 76.6 us; the launch traced here: 76.3 us
  waiting for transfers between devices  32 us (42%)
  starting transfers between devices  28.3 us (37%)
  Pallas kernels  14.4 us (19%)
  local copies, waits for them, and re-layouts  0.84 us (1%)
    ppermute x12, waiting for transfers between devices, swapped(): return lax.ppermute(value, axis, pairs)  25.3 us
    ppermute x12, starting transfers between devices, swapped(): return lax.ppermute(value, axis, pairs)  16.1 us
    ppermute x7, starting transfers between devices, shifted(): return lax.ppermute(value, axis, pairs)  12.2 us
    pallas_call x7, Pallas kernels, call(): pl.pallas_call(kernel, out_shape=shapes, in_specs=specs, out_specs=[VMEM]...  11.8 us
    ppermute x7, waiting for transfers between devices, shifted(): return lax.ppermute(value, axis, pairs)  6.78 us
    pallas_call x2, Pallas kernels, finish(): pl.pallas_call(functools.partial(salt_kernel, levels, first), out_shape=j...  2.59 us
  transfers between devices with their start and end apart: 19, of which 9 were waited for; matrix products, arithmetic and copies ran while one was open for 0% of the time, Pallas kernels for 17%

profile of v4, /device:TPU:0, one launch (start us, length us, event | category | flops | bytes accessed | tf_op | source)
XLA Modules:
  0.0 76.3 jit_solution(15384667739247347796)
XLA Ops:
  0.6 4.1 %collective-permute-start.16 = (f32[8,128,128]{2,1,0:T(8,128)}, f32[8,128,128]{2,1,0:T(8,128)S(1)}, u32[]{:S(2)}, u32[]{:S(2)}) collective-permute-start(f32[8,128,128]{2,1,0:T(8,128)} %param.13), channel_id=1, source_target_pairs={{0,16},{2,18},{4,20},{6,22},{8,24},{10,26},{12,28},{14,30},{16,0},... | collective-permute-start | bytes 1572872 | tf_op jit(solution)/shard_map/ppermute | solution.py:418
  4.8 1.4 %shard_map.112 = (f32[3,128,128]{2,1,0:T(8,128)S(1)}, f32[32,128]{1,0:T(8,128)S(1)}) custom-call(f32[128,128]{1,0:T(8,128)} %height.1, s32[8,128,128]{2,1,0:T(8,128)} %mask.11, f32[128,128]{1,0:T(8,128)} %depth.1, f32[8,128,128]{2,1,0:T(8,128)} %temp.5, f32[8,128,128]{2,1,0:T(8,128)} %north.3), custom_call_target="tpu_custom_call" | custom-call | flops 4000000 | bytes 1000000 | tf_op jit(solution)/shard_map/pallas_call | solution.py:44
  7.5 1.5 %collective-permute-start.4 = (f32[32,128]{1,0:T(8,128)S(1)}, f32[32,128]{1,0:T(8,128)S(1)}, u32[]{:S(2)}, u32[]{:S(2)}) collective-permute-start(f32[32,128]{1,0:T(8,128)S(1)} %shard_map.115), channel_id=1, source_target_pairs={{0,1},{1,0},{2,3},{3,2},{4,5},{5,4},{6,7},{7,6},{8,9},{9,8},{10,11... | collective-permute-start | bytes 49160 | tf_op jit(solution)/shard_map/ppermute | solution.py:423
  9.0 2.2 %collective-permute-done.4 = f32[32,128]{1,0:T(8,128)S(1)} collective-permute-done((f32[32,128]{1,0:T(8,128)S(1)}, f32[32,128]{1,0:T(8,128)S(1)}, u32[]{:S(2)}, u32[]{:S(2)}) %collective-permute-start.4) | collective-permute-done | bytes 16416 | tf_op jit(solution)/shard_map/ppermute | solution.py:423
  11.3 1.5 %collective-permute-start.5 = (f32[32,128]{1,0:T(8,128)S(1)}, f32[32,128]{1,0:T(8,128)S(1)}, u32[]{:S(2)}, u32[]{:S(2)}) collective-permute-start(f32[32,128]{1,0:T(8,128)S(1)} %add.36), channel_id=1, source_target_pairs={{0,4},{2,6},{4,0},{6,2},{8,12},{10,14},{12,8},{14,10},{16,20},{18,... | collective-permute-start | bytes 49160 | tf_op jit(solution)/shard_map/ppermute | solution.py:423
  12.7 2.2 %collective-permute-done.5 = f32[32,128]{1,0:T(8,128)S(1)} collective-permute-done((f32[32,128]{1,0:T(8,128)S(1)}, f32[32,128]{1,0:T(8,128)S(1)}, u32[]{:S(2)}, u32[]{:S(2)}) %collective-permute-start.5) | collective-permute-done | bytes 16416 | tf_op jit(solution)/shard_map/ppermute | solution.py:423
  15.0 1.6 %collective-permute-start.1 = (f32[32,128]{1,0:T(8,128)S(1)}, f32[32,128]{1,0:T(8,128)S(1)}, u32[]{:S(2)}, u32[]{:S(2)}) collective-permute-start(f32[32,128]{1,0:T(8,128)S(1)} %get-tuple-element.16), channel_id=1, source_target_pairs={{0,1},{1,0},{2,3},{3,2},{4,5},{5,4},{6,7},{7,6},{8,9},{9,8},{10,11... | collective-permute-start | bytes 49160 | tf_op jit(solution)/shard_map/ppermute | solution.py:418
  16.6 1.6 %collective-permute-start.7 = (f32[32,128]{1,0:T(8,128)S(1)}, f32[32,128]{1,0:T(8,128)S(1)}, u32[]{:S(2)}, u32[]{:S(2)}) collective-permute-start(f32[32,128]{1,0:T(8,128)S(1)} %add.38), channel_id=1, source_target_pairs={{0,8},{2,10},{4,12},{6,14},{8,0},{10,2},{12,4},{14,6},{16,24},{18,... | collective-permute-start | bytes 49160 | tf_op jit(solution)/shard_map/ppermute | solution.py:423
  18.6 2.5 %collective-permute-start.9 = (f32[32,128]{1,0:T(8,128)S(1)}, f32[32,128]{1,0:T(8,128)S(1)}, u32[]{:S(2)}, u32[]{:S(2)}) collective-permute-start(f32[32,128]{1,0:T(8,128)S(1)} %add.38), channel_id=1, source_target_pairs={{0,24},{2,26},{4,28},{6,30},{8,16},{10,18},{12,20},{14,22},{16,8},... | collective-permute-start | bytes 49160 | tf_op jit(solution)/shard_map/ppermute | solution.py:423
  21.3 1.8 %shard_map.113 = (f32[32,128]{1,0:T(8,128)S(1)}, f32[32,128]{1,0:T(8,128)S(1)}, f32[32,256]{1,0:T(8,128)S(1)}, f32[32,256]{1,0:T(8,128)S(1)}) custom-call(f32[3,128,128]{2,1,0:T(8,128)S(1)} %get-tuple-element.15.fields, s32[8,128,128]{2,1,0:T(8,128)} %mask.11, f32[8,128,128]{2,1,0:T(8,128)} %temp.5, f32[8,128,128]{2,1,0:T(8,128)} %east.3, ...), custom_call_target="tpu_custom_call" | custom-call | flops 4000000 | bytes 1000000 | tf_op jit(solution)/shard_map/pallas_call | solution.py:44
  23.1 14.0 %collective-permute-done.8 = f32[32,128]{1,0:T(8,128)S(1)} collective-permute-done((f32[32,128]{1,0:T(8,128)S(1)}, f32[32,128]{1,0:T(8,128)S(1)}, u32[]{:S(2)}, u32[]{:S(2)}) %collective-permute-start.8) | collective-permute-done | bytes 16416 | tf_op jit(solution)/shard_map/ppermute | solution.py:423
  37.1 3.2 %collective-permute-start.3 = (f32[32,256]{1,0:T(8,128)S(1)}, f32[32,256]{1,0:T(8,128)S(1)}, u32[]{:S(2)}, u32[]{:S(2)}) collective-permute-start(f32[32,256]{1,0:T(8,128)S(1)} %get-tuple-element.20), channel_id=1, source_target_pairs={{0,30},{2,0},{4,2},{6,4},{8,6},{10,8},{12,10},{14,12},{16,14},{18,... | collective-permute-start | bytes 98312 | tf_op jit(solution)/shard_map/ppermute | solution.py:418
  40.4 1.6 %collective-permute-done.3.from_east = f32[32,256]{1,0:T(8,128)S(1)} collective-permute-done((f32[32,256]{1,0:T(8,128)S(1)}, f32[32,256]{1,0:T(8,128)S(1)}, u32[]{:S(2)}, u32[]{:S(2)}) %collective-permute-start.3) | collective-permute-done | bytes 32800 | tf_op jit(solution)/shard_map/ppermute | solution.py:418
  41.9 1.8 %shard_map.116 = (f32[9,144,256]{2,1,0:T(8,128)S(1)}, f32[1,128]{1,0:T(1,128)S(1)}) custom-call(f32[3,128,128]{2,1,0:T(8,128)S(1)} %get-tuple-element.15.fields, f32[32,128]{1,0:T(8,128)S(1)} %get-tuple-element.17.from_south, f32[32,128]{1,0:T(8,128)S(1)} %get-tuple-element.18.from_north, f32[32,256]{1,0:T(8,128)S(1)} %collective-permute-done.2.from_west, ...), custom_call_target="tpu_custom_call" | custom-call | flops 4000000 | bytes 1000000 | tf_op jit(solution)/shard_map/pallas_call | solution.py:44
  43.7 1.5 %collective-permute-start.10 = (f32[1,128]{1,0:T(1,128)S(1)}, f32[1,128]{1,0:T(1,128)S(1)}, u32[]{:S(2)}, u32[]{:S(2)}) collective-permute-start(f32[1,128]{1,0:T(1,128)S(1)} %get-tuple-element.21), channel_id=1, source_target_pairs={{0,1},{1,0},{2,3},{3,2},{4,5},{5,4},{6,7},{7,6},{8,9},{9,8},{10,11... | collective-permute-start | bytes 1544 | tf_op jit(solution)/shard_map/ppermute | solution.py:423
  45.3 2.1 %collective-permute-done.10 = f32[1,128]{1,0:T(1,128)S(1)} collective-permute-done((f32[1,128]{1,0:T(1,128)S(1)}, f32[1,128]{1,0:T(1,128)S(1)}, u32[]{:S(2)}, u32[]{:S(2)}) %collective-permute-start.10) | collective-permute-done | bytes 544 | tf_op jit(solution)/shard_map/ppermute | solution.py:423
  47.4 3.6 %collective-permute-done.11 = f32[1,128]{1,0:T(1,128)S(1)} collective-permute-done((f32[1,128]{1,0:T(1,128)S(1)}, f32[1,128]{1,0:T(1,128)S(1)}, u32[]{:S(2)}, u32[]{:S(2)}) %collective-permute-start.11) | collective-permute-done | bytes 544 | tf_op jit(solution)/shard_map/ppermute | solution.py:423
  52.1 1.6 %collective-permute-start.13 = (f32[1,128]{1,0:T(1,128)S(1)}, f32[1,128]{1,0:T(1,128)S(1)}, u32[]{:S(2)}, u32[]{:S(2)}) collective-permute-start(f32[1,128]{1,0:T(1,128)S(1)} %add.44), channel_id=1, source_target_pairs={{0,8},{2,10},{4,12},{6,14},{8,0},{10,2},{12,4},{14,6},{16,24},{18,... | collective-permute-start | bytes 1544 | tf_op jit(solution)/shard_map/ppermute | solution.py:423
  53.7 4.1 %collective-permute-start.14 = (f32[1,128]{1,0:T(1,128)S(1)}, f32[1,128]{1,0:T(1,128)S(1)}, u32[]{:S(2)}, u32[]{:S(2)}) collective-permute-start(f32[1,128]{1,0:T(1,128)S(1)} %add.44), channel_id=1, source_target_pairs={{0,16},{2,18},{4,20},{6,22},{8,24},{10,26},{12,28},{14,30},{16,0},... | collective-permute-start | bytes 1544 | tf_op jit(solution)/shard_map/ppermute | solution.py:423
  57.8 1.4 %collective-permute-start.15 = (f32[1,128]{1,0:T(1,128)S(1)}, f32[1,128]{1,0:T(1,128)S(1)}, u32[]{:S(2)}, u32[]{:S(2)}) collective-permute-start(f32[1,128]{1,0:T(1,128)S(1)} %add.44), channel_id=1, source_target_pairs={{0,24},{2,26},{4,28},{6,30},{8,16},{10,18},{12,20},{14,22},{16,8},... | collective-permute-start | bytes 1544 | tf_op jit(solution)/shard_map/ppermute | solution.py:423
  59.2 2.0 %shard_map.114.tracer = f32[8,128,128]{2,1,0:T(8,128)S(1)} custom-call(f32[8,128,128]{2,1,0:T(8,128)} %temp.5, f32[8,128,128]{2,1,0:T(8,128)} %east.3, f32[8,128,128]{2,1,0:T(8,128)} %north.3, s32[8,128,128]{2,1,0:T(8,128)} %mask.11, f32[32,128]{1,0:T(8,128)S(1)} %get-tuple-element.17.from_south, f32[32,128]{1,0:T(8,128)S(1)} %get-tuple-element.18.from_north), custom_call_target="tpu_custom_call" | custom-call | flops 4000000 | bytes 1000000 | tf_op jit(solution)/shard_map/pallas_call | solution.py:44
  62.0 2.1 %collective-permute-start = (s32[1,1,8]{2,1,0:T(1,128)S(1)}, s32[1,1,8]{2,1,0:T(1,128)S(1)}, u32[]{:S(2)}, u32[]{:S(2)}) collective-permute-start(s32[1,1,8]{2,1,0:T(1,128)S(1)} %copy-done.3), channel_id=1, source_target_pairs={{0,16},{2,18},{4,20},{6,22},{8,24},{10,26},{12,28},{14,30},{16,0},... | collective-permute-start | bytes 104 | tf_op jit(solution)/shard_map/ppermute | solution.py:418
  66.6 2.5 %shard_map.118 = (f32[8,128,128]{2,1,0:T(8,128)S(1)}, f32[8,128,128]{2,1,0:T(8,128)}) custom-call(s32[8]{0:T(128)S(1)} %bitcast.1, f32[8,128,128]{2,1,0:T(8,128)} %copy-done.1, f32[128,128]{1,0:T(8,128)S(1)} %get-tuple-element.23.pressure, f32[32,256]{1,0:T(8,128)S(1)} %collective-permute-done.2.from_west, f32[32,256]{1,0:T(8,128)S(1)} %collective-permute-done.3.from_east, ...), custom_call_target="tpu_custom_call" | custom-call | flops 4000000 | bytes 1000000 | tf_op jit(solution)/shard_map/pallas_call | solution.py:44
  70.4 4.6 %collective-permute-done.17.part = f32[3,128,128]{2,1,0:T(8,128)S(1)} collective-permute-done((f32[3,128,128]{2,1,0:T(8,128)S(1)}, f32[3,128,128]{2,1,0:T(8,128)S(1)}, u32[]{:S(2)}, u32[]{:S(2)}) %collective-permute-start.17) | collective-permute-done | bytes 196640 | tf_op jit(solution)/shard_map/ppermute | solution.py:418
  (41 shorter events, 9.0 us)
Async XLA Ops:
  0.6 20.4 %copy-start.2 = (f32[8,128,128]{2,1,0:T(8,128)S(1)}, f32[8,128,128]{2,1,0:T(8,128)}, u32[]{:S(2)}) copy-start(f32[8,128,128]{2,1,0:T(8,128)} %param.14) | copy-start | bytes 1572868
  0.6 65.9 %collective-permute-start.16 = (f32[8,128,128]{2,1,0:T(8,128)}, f32[8,128,128]{2,1,0:T(8,128)S(1)}, u32[]{:S(2)}, u32[]{:S(2)}) collective-permute-start(f32[8,128,128]{2,1,0:T(8,128)} %param.13), channel_id=1, source_target_pairs={{0,16},{2,18},{4,20},{6,22},{8,24},{10,26},{12,28},{14,30},{16,0},... | collective-permute-start | bytes 1572872 | tf_op jit(solution)/shard_map/ppermute | solution.py:418
  7.5 3.7 %collective-permute-start.4 = (f32[32,128]{1,0:T(8,128)S(1)}, f32[32,128]{1,0:T(8,128)S(1)}, u32[]{:S(2)}, u32[]{:S(2)}) collective-permute-start(f32[32,128]{1,0:T(8,128)S(1)} %shard_map.115), channel_id=1, source_target_pairs={{0,1},{1,0},{2,3},{3,2},{4,5},{5,4},{6,7},{7,6},{8,9},{9,8},{10,11... | collective-permute-start | bytes 49160 | tf_op jit(solution)/shard_map/ppermute | solution.py:423
  11.3 3.7 %collective-permute-start.5 = (f32[32,128]{1,0:T(8,128)S(1)}, f32[32,128]{1,0:T(8,128)S(1)}, u32[]{:S(2)}, u32[]{:S(2)}) collective-permute-start(f32[32,128]{1,0:T(8,128)S(1)} %add.36), channel_id=1, source_target_pairs={{0,4},{2,6},{4,0},{6,2},{8,12},{10,14},{12,8},{14,10},{16,20},{18,... | collective-permute-start | bytes 49160 | tf_op jit(solution)/shard_map/ppermute | solution.py:423
  15.0 1.6 %collective-permute-start.6 = (f32[32,128]{1,0:T(8,128)S(1)}, f32[32,128]{1,0:T(8,128)S(1)}, u32[]{:S(2)}, u32[]{:S(2)}) collective-permute-start(f32[32,128]{1,0:T(8,128)S(1)} %add.37), channel_id=1, source_target_pairs={{0,2},{2,0},{4,6},{6,4},{8,10},{10,8},{12,14},{14,12},{16,18},{18,... | collective-permute-start | bytes 49160 | tf_op jit(solution)/shard_map/ppermute | solution.py:423
  15.0 6.1 %collective-permute-start.1 = (f32[32,128]{1,0:T(8,128)S(1)}, f32[32,128]{1,0:T(8,128)S(1)}, u32[]{:S(2)}, u32[]{:S(2)}) collective-permute-start(f32[32,128]{1,0:T(8,128)S(1)} %get-tuple-element.16), channel_id=1, source_target_pairs={{0,1},{1,0},{2,3},{3,2},{4,5},{5,4},{6,7},{7,6},{8,9},{9,8},{10,11... | collective-permute-start | bytes 49160 | tf_op jit(solution)/shard_map/ppermute | solution.py:418
  16.6 6.5 %collective-permute-start.7 = (f32[32,128]{1,0:T(8,128)S(1)}, f32[32,128]{1,0:T(8,128)S(1)}, u32[]{:S(2)}, u32[]{:S(2)}) collective-permute-start(f32[32,128]{1,0:T(8,128)S(1)} %add.38), channel_id=1, source_target_pairs={{0,8},{2,10},{4,12},{6,14},{8,0},{10,2},{12,4},{14,6},{16,24},{18,... | collective-permute-start | bytes 49160 | tf_op jit(solution)/shard_map/ppermute | solution.py:423
  18.2 18.9 %collective-permute-start.8 = (f32[32,128]{1,0:T(8,128)S(1)}, f32[32,128]{1,0:T(8,128)S(1)}, u32[]{:S(2)}, u32[]{:S(2)}) collective-permute-start(f32[32,128]{1,0:T(8,128)S(1)} %add.38), channel_id=1, source_target_pairs={{0,16},{2,18},{4,20},{6,22},{8,24},{10,26},{12,28},{14,30},{16,0},... | collective-permute-start | bytes 49160 | tf_op jit(solution)/shard_map/ppermute | solution.py:423
  18.6 21.8 %collective-permute-start.9 = (f32[32,128]{1,0:T(8,128)S(1)}, f32[32,128]{1,0:T(8,128)S(1)}, u32[]{:S(2)}, u32[]{:S(2)}) collective-permute-start(f32[32,128]{1,0:T(8,128)S(1)} %add.38), channel_id=1, source_target_pairs={{0,24},{2,26},{4,28},{6,30},{8,16},{10,18},{12,20},{14,22},{16,8},... | collective-permute-start | bytes 49160 | tf_op jit(solution)/shard_map/ppermute | solution.py:423
  21.1 48.0 %collective-permute-start.18 = (f32[5,128,128]{2,1,0:T(8,128)S(1)}, f32[5,128,128]{2,1,0:T(8,128)S(1)}, u32[]{:S(2)}, u32[]{:S(2)}) collective-permute-start(f32[5,128,128]{2,1,0:T(8,128)S(1)} %slice.7), channel_id=1, source_target_pairs={{0,16},{2,18},{4,20},{6,22},{8,24},{10,26},{12,28},{14,30},{16,0},... | collective-permute-start | bytes 983048 | tf_op jit(solution)/shard_map/ppermute | solution.py:418
  23.1 17.3 %collective-permute-start.2 = (f32[32,256]{1,0:T(8,128)S(1)}, f32[32,256]{1,0:T(8,128)S(1)}, u32[]{:S(2)}, u32[]{:S(2)}) collective-permute-start(f32[32,256]{1,0:T(8,128)S(1)} %get-tuple-element.19), channel_id=1, source_target_pairs={{0,2},{2,4},{4,6},{6,8},{8,10},{10,12},{12,14},{14,16},{16,18},{18... | collective-permute-start | bytes 98312 | tf_op jit(solution)/shard_map/ppermute | solution.py:418
  37.1 4.8 %collective-permute-start.3 = (f32[32,256]{1,0:T(8,128)S(1)}, f32[32,256]{1,0:T(8,128)S(1)}, u32[]{:S(2)}, u32[]{:S(2)}) collective-permute-start(f32[32,256]{1,0:T(8,128)S(1)} %get-tuple-element.20), channel_id=1, source_target_pairs={{0,30},{2,0},{4,2},{6,4},{8,6},{10,8},{12,10},{14,12},{16,14},{18,... | collective-permute-start | bytes 98312 | tf_op jit(solution)/shard_map/ppermute | solution.py:418
  43.7 3.6 %collective-permute-start.10 = (f32[1,128]{1,0:T(1,128)S(1)}, f32[1,128]{1,0:T(1,128)S(1)}, u32[]{:S(2)}, u32[]{:S(2)}) collective-permute-start(f32[1,128]{1,0:T(1,128)S(1)} %get-tuple-element.21), channel_id=1, source_target_pairs={{0,1},{1,0},{2,3},{3,2},{4,5},{5,4},{6,7},{7,6},{8,9},{9,8},{10,11... | collective-permute-start | bytes 1544 | tf_op jit(solution)/shard_map/ppermute | solution.py:423
  47.4 3.6 %collective-permute-start.11 = (f32[1,128]{1,0:T(1,128)S(1)}, f32[1,128]{1,0:T(1,128)S(1)}, u32[]{:S(2)}, u32[]{:S(2)}) collective-permute-start(f32[1,128]{1,0:T(1,128)S(1)} %add.42), channel_id=1, source_target_pairs={{0,4},{2,6},{4,0},{6,2},{8,12},{10,14},{12,8},{14,10},{16,20},{18,... | collective-permute-start | bytes 1544 | tf_op jit(solution)/shard_map/ppermute | solution.py:423
  51.0 1.2 %collective-permute-start.12 = (f32[1,128]{1,0:T(1,128)S(1)}, f32[1,128]{1,0:T(1,128)S(1)}, u32[]{:S(2)}, u32[]{:S(2)}) collective-permute-start(f32[1,128]{1,0:T(1,128)S(1)} %add.43), channel_id=1, source_target_pairs={{0,2},{2,0},{4,6},{6,4},{8,10},{10,8},{12,14},{14,12},{16,18},{18,... | collective-permute-start | bytes 1544 | tf_op jit(solution)/shard_map/ppermute | solution.py:423
  52.1 9.9 %copy-start.3 = (s32[1,1,8]{2,1,0:T(1,128)S(1)}, s32[1,1,8]{2,1,0:T(1,128)}, u32[]{:S(2)}) copy-start(s32[1,1,8]{2,1,0:T(1,128)} %param.15) | copy-start | bytes 100
  52.1 9.9 %collective-permute-start.13 = (f32[1,128]{1,0:T(1,128)S(1)}, f32[1,128]{1,0:T(1,128)S(1)}, u32[]{:S(2)}, u32[]{:S(2)}) collective-permute-start(f32[1,128]{1,0:T(1,128)S(1)} %add.44), channel_id=1, source_target_pairs={{0,8},{2,10},{4,12},{6,14},{8,0},{10,2},{12,4},{14,6},{16,24},{18,... | collective-permute-start | bytes 1544 | tf_op jit(solution)/shard_map/ppermute | solution.py:423
  53.7 10.4 %collective-permute-start.14 = (f32[1,128]{1,0:T(1,128)S(1)}, f32[1,128]{1,0:T(1,128)S(1)}, u32[]{:S(2)}, u32[]{:S(2)}) collective-permute-start(f32[1,128]{1,0:T(1,128)S(1)} %add.44), channel_id=1, source_target_pairs={{0,16},{2,18},{4,20},{6,22},{8,24},{10,26},{12,28},{14,30},{16,0},... | collective-permute-start | bytes 1544 | tf_op jit(solution)/shard_map/ppermute | solution.py:423
  57.8 7.2 %collective-permute-start.15 = (f32[1,128]{1,0:T(1,128)S(1)}, f32[1,128]{1,0:T(1,128)S(1)}, u32[]{:S(2)}, u32[]{:S(2)}) collective-permute-start(f32[1,128]{1,0:T(1,128)S(1)} %add.44), channel_id=1, source_target_pairs={{0,24},{2,26},{4,28},{6,30},{8,16},{10,18},{12,20},{14,22},{16,8},... | collective-permute-start | bytes 1544 | tf_op jit(solution)/shard_map/ppermute | solution.py:423
  61.2 0.8 %copy-start.1 = (f32[8,128,128]{2,1,0:T(8,128)}, f32[8,128,128]{2,1,0:T(8,128)S(1)}, u32[]{:S(2)}) copy-start(f32[8,128,128]{2,1,0:T(8,128)S(1)} %shard_map.114.tracer) | copy-start | bytes 1572868
  62.0 4.5 %copy-start = (s32[8,128,128]{2,1,0:T(8,128)S(1)}, s32[8,128,128]{2,1,0:T(8,128)}, u32[]{:S(2)}) copy-start(s32[8,128,128]{2,1,0:T(8,128)} %mask.11) | copy-start | bytes 1572868
  62.0 4.5 %collective-permute-start = (s32[1,1,8]{2,1,0:T(1,128)S(1)}, s32[1,1,8]{2,1,0:T(1,128)S(1)}, u32[]{:S(2)}, u32[]{:S(2)}) collective-permute-start(s32[1,1,8]{2,1,0:T(1,128)S(1)} %copy-done.3), channel_id=1, source_target_pairs={{0,16},{2,18},{4,20},{6,22},{8,24},{10,26},{12,28},{14,30},{16,0},... | collective-permute-start | bytes 104 | tf_op jit(solution)/shard_map/ppermute | solution.py:418
  64.1 11.0 %collective-permute-start.17 = (f32[3,128,128]{2,1,0:T(8,128)S(1)}, f32[3,128,128]{2,1,0:T(8,128)S(1)}, u32[]{:S(2)}, u32[]{:S(2)}) collective-permute-start(f32[3,128,128]{2,1,0:T(8,128)S(1)} %slice.6), channel_id=1, source_target_pairs={{0,16},{2,18},{4,20},{6,22},{8,24},{10,26},{12,28},{14,30},{16,0},... | collective-permute-start | bytes 589832 | tf_op jit(solution)/shard_map/ppermute | solution.py:418

commit v5 on v3

--- a/solution.py
+++ b/solution.py
@@ -27,8 +27,8 @@
 SMEM = pl.BlockSpec(memory_space=pltpu.SMEM)
 HBM = pl.BlockSpec(memory_space=pltpu.HBM)
 
-OFF_AT, WEIGHT_AT = 16, 32
 PAIRS = [(i, j) for i in range(ITERS + 1) for j in range(i, ITERS + 1)]
+MIDDLE_AT, LINK_AT, BACK_AT, WEIGHT_AT = 32, 40, 48, 56
 
 
 def call(kernel, outs, args, specs=None, keep=None, flops=4000000):
@@ -135,75 +135,7 @@
     return jnp.transpose(jnp.concatenate([from_east[span, :], middle, from_west[span, :]], axis=0))
 
 
-def tile_basis_kernel(fields, row_out):
-    rows, columns = fields.shape[1:]
-    wet, deep = fields[1], fields[2]
-    row = lax.broadcasted_iota(jnp.int32, (rows, columns), 0)
-    lane = lane_index((rows, columns))
-    east_weight = (
-        STIFFNESS * 0.5 * (deep + pltpu.roll(deep, columns - 1, 1)) * wet * pltpu.roll(wet, columns - 1, 1)
-    )
-    east_weight = jnp.where(lane == columns - 1, 0.0, east_weight)
-    west_weight = pltpu.roll(east_weight, 1, 1)
-    north_weight = STIFFNESS * 0.5 * (deep + pltpu.roll(deep, rows - 1, 0)) * wet * pltpu.roll(wet, rows - 1, 0)
-    north_weight = jnp.where(row == rows - 1, 0.0, north_weight)
-    south_weight = pltpu.roll(north_weight, 1, 0)
-
-    def spread(field):
-        out = west_weight * (field - pltpu.roll(field, 1, 1))
-        out = out + east_weight * (field - pltpu.roll(field, columns - 1, 1))
-        out = out + south_weight * (field - pltpu.roll(field, 1, 0))
-        return out + north_weight * (field - pltpu.roll(field, rows - 1, 0))
-
-    field = fields[0]
-    square = total(field * field)
-    weight = jnp.sqrt(square)
-    vector = field * jnp.where(square > 0.0, lax.rsqrt(jnp.maximum(square, 1e-30)), 0.0)
-    before, link = jnp.zeros_like(vector), jnp.zeros_like(square)
-    at = lane_index((1, LANES))
-    out = jnp.where(at == WEIGHT_AT, weight, 0.0)
-    for step in range(ITERS):
-        image = spread(vector) - link * before
-        along, size = total(image * vector), total(image * image)
-        out = jnp.where(at == step, along, out)
-        if step + 1 < ITERS:
-            left = size - along * along
-            alive = left > 1e-6 * size
-            scale = jnp.where(alive, lax.rsqrt(jnp.maximum(left, 1e-30)), 0.0)
-            link = jnp.where(alive, jnp.sqrt(jnp.maximum(left, 0.0)), 0.0)
-            before, vector = vector, (image - along * vector) * scale
-            out = jnp.where(at == OFF_AT + step, link, out)
-    row_out[...] = jnp.broadcast_to(out[None], row_out.shape)
-
-
-def merged_recurrence(tiles):
-    at = lane_index(tiles.shape)
-    diagonal = jnp.where(at < ITERS, tiles, 0.0)
-    above = jnp.where(at < ITERS - 1, pltpu.roll(tiles, LANES - OFF_AT, 1), 0.0)
-    below = pltpu.roll(above, 1, 1)
-    vector = jnp.where(at == 0, pltpu.roll(tiles, LANES - WEIGHT_AT, 1), 0.0)
-    square = total(vector * vector)
-    vector = vector * jnp.where(square > 0.0, lax.rsqrt(jnp.maximum(square, 1e-30)), 0.0)
-    before, link = jnp.zeros_like(vector), jnp.zeros_like(square)
-    running = jnp.ones_like(square)
-    steps = []
-    for _ in range(ITERS):
-        image = diagonal * vector - link * before
-        image = image + above * pltpu.roll(vector, LANES - 1, 1) + below * pltpu.roll(vector, 1, 1)
-        along, size = total(image * vector), total(image * image)
-        left = size - along * along
-        alive = left > 1e-6 * size
-        middle = jnp.where(running > 0.0, along, 4.0 * STIFFNESS)
-        back = link
-        scale = jnp.where(alive, lax.rsqrt(jnp.maximum(left, 1e-30)), 0.0)
-        link = jnp.where(alive, jnp.sqrt(jnp.maximum(left, 0.0)), 0.0)
-        steps.append((middle, jnp.where(alive, link, 2.0 * STIFFNESS), back))
-        running = jnp.where(alive, running, 0.0)
-        before, vector = vector, (image - along * vector) * scale
-    return steps
-
-
-def krylov_kernel(fields, from_south, from_north, from_west, from_east, tiles, basis, products):
+def krylov_kernel(fields, from_south, from_north, from_west, from_east, basis, row_out):
     rows, columns = fields.shape[1:]
     full_rows, full_columns = rows + 2 * RING, columns + LANES
 
@@ -227,56 +159,117 @@
         out = out + south_weight * (value - pltpu.roll(value, 1, 0))
         return out + north_weight * (value - pltpu.roll(value, full_rows - 1, 0))
 
-    steps = merged_recurrence(tiles[...])
     at = lane_index((1, LANES))
-    row = jnp.zeros((1, LANES), jnp.float32)
-    for step, entries in enumerate(steps):
-        for kind, entry in enumerate(entries):
-            row = jnp.where(at == kind * OFF_AT + step, entry, row)
-    basis[ITERS + 2, :1, :LANES] = row
-    vectors = [field]
-    before, value = None, field
-    basis[0] = field
-    for step, (middle, link, back) in enumerate(steps):
-        image = spread(value) - middle * value
-        if step:
-            image = image - back * before
-        before, value = value, image * (1.0 / link)
+    square = total(field * field)
+    row = jnp.where(at == WEIGHT_AT, jnp.sqrt(square), 0.0)
+    value = field * jnp.where(square > 0.0, lax.rsqrt(jnp.maximum(square, 1e-30)), 0.0)
+    running = jnp.where(square > 0.0, 1.0, 0.0)
+    before, back = jnp.zeros_like(value), jnp.zeros_like(square)
+    vectors = [value]
+    basis[0] = value
+    for step in range(ITERS):
+        image = spread(value) - back * before
+        along, size = total(image * value), total(image * image)
+        middle, link, scale, alive = next_step(along, size, running)
+        for start, entry in ((MIDDLE_AT, middle), (LINK_AT, link), (BACK_AT, back)):
+            row = jnp.where(at == start + step, entry, row)
+        before, value = value, (image - middle * value) * scale
+        running, back = alive, link * alive
+        vectors.append(value)
         if step + 1 < ITERS:
             basis[step + 1] = value
-        vectors.append(value)
     cut = [vector[:rows, :columns] for vector in vectors]
     partial = [jnp.sum(cut[i] * cut[j], axis=0, keepdims=True) for i, j in PAIRS]
     partial = [sum(part[:, k : k + LANES] for k in range(0, columns, LANES)) for part in partial]
     partial = partial + [jnp.zeros((LANES - len(partial), LANES), jnp.float32)]
     table = jnp.transpose(jnp.concatenate(partial, axis=0))
-    products[...] = jnp.broadcast_to(jnp.sum(table, axis=0, keepdims=True)[None], products.shape)
+    row = row + jnp.sum(table, axis=0, keepdims=True)
+    row_out[...] = jnp.broadcast_to(row[None], row_out.shape)
+
+
+def next_step(along, size, running):
+    left = size - along * along
+    alive = jnp.where((left > 1e-6 * size) & (running > 0.0), 1.0, 0.0)
+    safe = jnp.maximum(left, 1e-30)
+    middle = jnp.where(running > 0.0, along, 4.0 * STIFFNESS)
+    link = jnp.where(alive > 0.0, jnp.sqrt(safe), 2.0 * STIFFNESS)
+    scale = jnp.where(alive > 0.0, lax.rsqrt(safe), 1.0 / (2.0 * STIFFNESS))
+    return middle, link, scale, alive
+
+
+def merged_recurrence(tiles):
+    at = lane_index(tiles.shape)
+    diagonal = jnp.where(at < ITERS, pltpu.roll(tiles, LANES - MIDDLE_AT, 1), 0.0)
+    above = jnp.where(at < ITERS - 1, pltpu.roll(tiles, LANES - BACK_AT - 1, 1), 0.0)
+    below = pltpu.roll(above, 1, 1)
+    vector = jnp.where(at == 0, pltpu.roll(tiles, LANES - WEIGHT_AT, 1), 0.0)
+    square = total(vector * vector)
+    vector = vector * jnp.where(square > 0.0, lax.rsqrt(jnp.maximum(square, 1e-30)), 0.0)
+    before, back = jnp.zeros_like(vector), jnp.zeros_like(square)
+    running = jnp.ones_like(square)
+    steps = []
+    for _ in range(ITERS):
+        image = diagonal * vector - back * before
+        image = image + above * pltpu.roll(vector, LANES - 1, 1) + below * pltpu.roll(vector, 1, 1)
+        along, size = total(image * vector), total(image * image)
+        middle, link, scale, alive = next_step(along, size, running)
+        steps.append((middle, link, scale, back))
+        before, vector = vector, (image - along * vector) * (scale * alive)
+        running, back = alive, link * alive
+    return steps
 
 
 def solve_kernel(gathered, basis, surface, pressure):
     rows, columns = surface.shape
-    summed = jnp.sum(gathered[...], axis=0, keepdims=True)
-    known = basis[ITERS + 2, :1, :LANES]
-    at = lane_index((1, LANES))
-
-    def entry(row, index):
-        return jnp.sum(jnp.where(at == index, row, 0.0), axis=1, keepdims=True)
-
+    place = lax.axis_index("gx") * lax.axis_size("gy") + lax.axis_index("gy")
+    tiles = gathered[...]
+    steps = merged_recurrence(tiles)
+    spare = -tiles.shape[0] % LANES
+    if spare:
+        tiles = jnp.concatenate([tiles, jnp.zeros((spare, LANES), jnp.float32)], axis=0)
+    table = jnp.transpose(tiles)
+
+    def known(index):
+        return table[index : index + 1, :]
+
+    products = {}
+    for index, (i, j) in enumerate(PAIRS):
+        products[i, j] = products[j, i] = known(index)
+    change = [[known(WEIGHT_AT)]]
+    for step, (middle, _, scale, back) in enumerate(steps):
+        last = change[step]
+        out = [None] * (step + 2)
+
+        def add(at, term):
+            out[at] = term if out[at] is None else out[at] + term
+
+        for j, part in enumerate(last):
+            add(j, (known(MIDDLE_AT + j) - middle) * part)
+            add(j + 1, known(LINK_AT + j) * part)
+            if j:
+                add(j - 1, known(BACK_AT + j) * part)
+        if step:
+            for j, part in enumerate(change[step - 1]):
+                add(j, -back * part)
+        change.append([scale * term for term in out])
     gram = {}
-    for index, (i, j) in enumerate(PAIRS):
-        gram[i, j] = gram[j, i] = entry(summed, index)
-    middle = [entry(known, step) for step in range(ITERS)]
-    link = [entry(known, OFF_AT + step) for step in range(ITERS)]
-    back = [entry(known, 2 * OFF_AT + step) for step in range(ITERS)]
+    for k in range(ITERS + 1):
+        half = [
+            sum(change[k][i] * products[i, j] for i in range(k + 1)) for j in range(ITERS + 1)
+        ]
+        for m in range(k, ITERS + 1):
+            both = sum(half[j] * change[m][j] for j in range(m + 1))
+            gram[k, m] = gram[m, k] = jnp.sum(both, axis=1, keepdims=True)
     zero = jnp.zeros((1, 1), jnp.float32)
 
     def applied(vector):
         out = [zero] * (len(vector) + 1)
         for i, part in enumerate(vector):
-            out[i] = out[i] + part + middle[i] * part
-            out[i + 1] = out[i + 1] + link[i] * part
+            middle, link, _, back = steps[i]
+            out[i] = out[i] + part + middle * part
+            out[i + 1] = out[i + 1] + link * part
             if i:
-                out[i - 1] = out[i - 1] + back[i] * part
+                out[i - 1] = out[i - 1] + back * part
         return out
 
     def inner(left, right):
@@ -308,9 +301,12 @@
             growth = jnp.where(norm_now > 0.0, norm_next / norm_now, 0.0)
             direction = scaled_add(residual, growth, direction)
             norm_now = norm_next
-    value = iterate[0] * basis[0]
-    for k in range(1, ITERS):
-        value = value + iterate[k] * basis[k]
+    mine = lane_index((1, table.shape[1])) == place
+    value = None
+    for j in range(ITERS):
+        weight = sum(iterate[k] * change[k][j] for k in range(j, ITERS))
+        weight = jnp.sum(jnp.where(mine, weight, 0.0), axis=1, keepdims=True)
+        value = weight * basis[j] if value is None else value + weight * basis[j]
     surface[...] = value[:rows, :columns]
     opening = basis[ITERS]
     load = basis[ITERS + 1] * value
@@ -359,7 +355,7 @@
     return thickness * pressure[...] * mask[level].astype(jnp.float32)
 
 
-def warm_kernel(levels, slots, tracer, pressure, from_west, from_east, mask, warm, partial, salt):
+def warm_kernel(levels, slots, tracer, pressure, from_west, from_east, mask, outer, inner, partial, salt):
     rows, columns = pressure.shape
     lane = lane_index((rows, columns))
     sides = beside_tile(from_west, from_east, 3 * RING, levels)[:rows]
@@ -371,19 +367,19 @@
     for slot in range(levels):
         level = level_of_slot(slots, slot, levels)
         dense = density(level, levels, pressure, mask)
-        value = warm[slot]
+        value = jnp.where(from_outer(), outer[slot], inner[slot])
         salt[level] = (HALINE + CABBELING * value) * dense
         partial[level] = partial[level] + (THERMAL + 2.0 * NONLINEAR * value) * dense
 
 
-def salt_kernel(levels, first, slots, partial, pressure, mask, part, *refs):
+def salt_kernel(levels, first, slots, partial, pressure, mask, inner, part, *refs):
     result, done, sems = refs[-3:]
     size = part.shape[0]
     copies = []
     for at in range(size):
         level = level_of_slot(slots, first + at, levels)
         dense = density(level, levels, pressure, mask)
-        done[at] = partial[level] + CABBELING * part[at] * dense
+        done[at] = partial[level] + CABBELING * jnp.where(from_outer(), part[at], inner[first + at]) * dense
         copies.append(pltpu.make_async_copy(done.at[at], result.at[level], sems.at[at]))
         copies[-1].start()
     for copy in copies:
@@ -421,6 +417,24 @@
     return rows.reshape(rows.shape[0], LANES)
 
 
+QUARTERS = {"a": (2, 0, 3, 1), "b": (1, 3, 0, 2)}
+
+
+def fetched(value, kind):
+    quarter = lax.axis_size("gx") // 4
+    pairs = [
+        (source * quarter + i, target * quarter + i)
+        for source, target in enumerate(QUARTERS[kind])
+        for i in range(quarter)
+    ]
+    return lax.ppermute(value, "gx", pairs)
+
+
+def from_outer():
+    place, count = lax.axis_index("gx"), lax.axis_size("gx")
+    return (place >= count // 4) & (place < count - count // 4)
+
+
 def runs(levels):
     return levels // 2, levels - levels // 2
 
@@ -444,7 +458,8 @@
 
     salt_sizes = runs(levels)
     slots = shifted(slot_map, "gx", half_cycle, True).reshape(-1)
-    warm = shifted(temp_store, "gx", half_cycle, True)
+    warm_a, warm_b = (fetched(temp_store, kind) for kind in QUARTERS)
+    salt_b = fetched(salt_store, "b")
 
     swap = lax.axis_size("gy") == 2
     fields, *messages = call(
@@ -457,7 +472,6 @@
     else:
         arrived = [shifted(messages[0], "gy", 1, False)]
         arrived += [shifted(messages[1], "gy", -1, False)]
-    (tile_rows,) = call(tile_basis_kernel, [(devices, 1, LANES)], held(fields))
     from_south, from_north, to_east, to_west = call(
         functools.partial(pack_x_kernel, levels, len(arrived)),
         [(strip, columns)] * 2 + [(strip, rows + LANES)] * 2,
@@ -476,24 +490,21 @@
     for size in salt_sizes:
         cuts.append(lax.slice_in_dim(salt_store, start, start + size))
         start += size
-    tiles = shared(tile_rows)
-    salt_parts = [shifted(cut, "gx", half_cycle, True) for cut in cuts]
+    salt_parts = [fetched(cut, "a") for cut in cuts]
     beside = held(from_south, from_north, from_west, from_east)
-    basis, products = call(
-        krylov_kernel, [(ITERS + 3,) + full, (devices, 1, LANES)], held(fields) + beside + held(tiles)
-    )
-    gathered = shared(products)
+    basis, tile_rows = call(krylov_kernel, [(ITERS + 2,) + full, (devices, 1, LANES)], held(fields) + beside)
+    gathered = shared(tile_rows)
     surface, pressure = call(solve_kernel, [(rows, columns)] * 2, held(gathered, basis), keep=[False, True])
     partial, salt_back = call(
         functools.partial(warm_kernel, levels),
         [temp_adjoint.shape] * 2,
-        free(slots) + stored(tracer) + held(pressure, from_west, from_east) + free(land_mask, warm),
-        specs=[SMEM] + [VMEM] * 6,
+        free(slots) + stored(tracer) + held(pressure, from_west, from_east) + free(land_mask, warm_a, warm_b),
+        specs=[SMEM] + [VMEM] * 7,
         keep=[True, False],
     )
     temp_back, first = None, 0
     for size, part in zip(salt_sizes, salt_parts):
-        args = (slots, partial, pressure, land_mask, part)
+        args = (slots, partial, pressure, land_mask, salt_b, part)
         temp_back = finish(levels, first, args, temp_back)
         first += size
     return (temp_back, salt_back, surface)

time: 73.1 us -> 69.9 us (0.956)
  blocking collectives: 31.5 us -> 0 us
  waiting for transfers between devices: 3.82 us -> 33.2 us
  starting transfers between devices: 19.8 us -> 17.9 us
    all_to_all x1 -> x0, blocking collectives: 31.5 us -> none  [shared(): rows = lax.all_to_all(rows, ('gx', 'gy'), 0, 0)]
    ppermute x7 -> x4, waiting for transfers between devices: 2.23 us -> 28.9 us  [shifted(): return lax.ppermute(value, axis, pairs)]
    ppermute x7 -> x4, starting transfers between devices: 15.9 us -> 5.62 us  [shifted(): return lax.ppermute(value, axis, pairs)]
    ppermute x0 -> x5, starting transfers between devices: none -> 6.03 us  [fetched(): return lax.ppermute(value, 'gx', pairs)]
    all_to_all x1, waiting for transfers between devices: 1.59 us -> 4.33 us  [shared(): rows = lax.all_to_all(rows, ('gx', 'gy'), 0, 0)]
    all_to_all x1, starting transfers between devices: 3.92 us -> 6.21 us  [shared(): rows = lax.all_to_all(rows, ('gx', 'gy'), 0, 0)]
    pallas_call x7 -> x6, Pallas kernels: 12.4 us -> 12.5 us  [call(): pl.pallas_call(kernel, out_shape=shapes, in_specs=specs, out_specs=[VMEM]...]
  transfers between devices with their start and end apart: 8 -> 10, of which waited for: 2 -> 4; matrix products, arithmetic and copies ran while one was open for 1% -> 1% of each run, Pallas kernels for 19% -> 20%
where the time goes in v5:
time: 69.9 us; the launch traced here: 69.6 us
  waiting for transfers between devices  33.2 us (47%)
  starting transfers between devices  17.9 us (26%)
  Pallas kernels  15.5 us (22%)
  local copies, waits for them, and re-layouts  2.25 us (3%)
  between operations  0.75 us (1%)
    ppermute x4, waiting for transfers between devices, shifted(): return lax.ppermute(value, axis, pairs)  28.9 us
    pallas_call x6, Pallas kernels, call(): pl.pallas_call(kernel, out_shape=shapes, in_specs=specs, out_specs=[VMEM]...  12.5 us
    all_to_all x1, starting transfers between devices, shared(): rows = lax.all_to_all(rows, ('gx', 'gy'), 0, 0)  6.21 us
    ppermute x5, starting transfers between devices, fetched(): return lax.ppermute(value, 'gx', pairs)  6.03 us
    ppermute x4, starting transfers between devices, shifted(): return lax.ppermute(value, axis, pairs)  5.62 us
    all_to_all x1, waiting for transfers between devices, shared(): rows = lax.all_to_all(rows, ('gx', 'gy'), 0, 0)  4.33 us
    pallas_call x2, Pallas kernels, finish(): pl.pallas_call(functools.partial(salt_kernel, levels, first), out_shape=j...  3.02 us
    unnamed x20, local copies, waits for them, and re-layouts  1.41 us
  transfers between devices with their start and end apart: 10, of which 4 were waited for; matrix products, arithmetic and copies ran while one was open for 1% of the time, Pallas kernels for 20%

profile of v5, /device:TPU:0, one launch (start us, length us, event | category | flops | bytes accessed | tf_op | source)
XLA Modules:
  0.0 69.6 jit_solution(10087523414567457652)
XLA Ops:
  0.6 4.1 %collective-permute-start.4 = (f32[8,128,128]{2,1,0:T(8,128)}, f32[8,128,128]{2,1,0:T(8,128)S(1)}, u32[]{:S(2)}, u32[]{:S(2)}) collective-permute-start(f32[8,128,128]{2,1,0:T(8,128)} %param.13), channel_id=1, source_target_pairs={{0,16},{2,18},{4,20},{6,22},{8,0},{10,2},{12,4},{14,6},{16,24},{18... | collective-permute-start | bytes 1572872 | tf_op jit(solution)/shard_map/ppermute | solution.py:430
  4.8 1.9 %collective-permute-start.6 = (f32[8,128,128]{2,1,0:T(8,128)}, f32[8,128,128]{2,1,0:T(8,128)S(1)}, u32[]{:S(2)}, u32[]{:S(2)}) collective-permute-start(f32[8,128,128]{2,1,0:T(8,128)} %param.14), channel_id=1, source_target_pairs={{0,8},{2,10},{4,12},{6,14},{8,24},{10,26},{12,28},{14,30},{16,0},{... | collective-permute-start | bytes 1572872 | tf_op jit(solution)/shard_map/ppermute | solution.py:430
  6.7 1.4 %shard_map.112 = (f32[3,128,128]{2,1,0:T(8,128)S(1)}, f32[32,128]{1,0:T(8,128)S(1)}) custom-call(f32[128,128]{1,0:T(8,128)} %height.1, s32[8,128,128]{2,1,0:T(8,128)} %mask.11, f32[128,128]{1,0:T(8,128)} %depth.1, f32[8,128,128]{2,1,0:T(8,128)} %temp.5, f32[8,128,128]{2,1,0:T(8,128)} %north.3), custom_call_target="tpu_custom_call" | custom-call | flops 4000000 | bytes 1000000 | tf_op jit(solution)/shard_map/pallas_call | solution.py:44
  8.1 0.0 copy-start.8
  8.1 1.6 %collective-permute-start.1 = (f32[32,128]{1,0:T(8,128)S(1)}, f32[32,128]{1,0:T(8,128)S(1)}, u32[]{:S(2)}, u32[]{:S(2)}) collective-permute-start(f32[32,128]{1,0:T(8,128)S(1)} %get-tuple-element.16), channel_id=1, source_target_pairs={{0,1},{1,0},{2,3},{3,2},{4,5},{5,4},{6,7},{7,6},{8,9},{9,8},{10,11... | collective-permute-start | bytes 49160 | tf_op jit(solution)/shard_map/ppermute | solution.py:412
  9.7 1.0 %collective-permute-start = (s32[1,1,8]{2,1,0:T(1,128)S(1)}, s32[1,1,8]{2,1,0:T(1,128)S(1)}, u32[]{:S(2)}, u32[]{:S(2)}) collective-permute-start(s32[1,1,8]{2,1,0:T(1,128)S(1)} %copy-done.9), channel_id=1, source_target_pairs={{0,16},{2,18},{4,20},{6,22},{8,24},{10,26},{12,28},{14,30},{16,0},... | collective-permute-start | bytes 104 | tf_op jit(solution)/shard_map/ppermute | solution.py:412
  10.7 1.2 %collective-permute-done.1.refs_0_ = f32[32,128]{1,0:T(8,128)S(1)} collective-permute-done((f32[32,128]{1,0:T(8,128)S(1)}, f32[32,128]{1,0:T(8,128)S(1)}, u32[]{:S(2)}, u32[]{:S(2)}) %collective-permute-start.1) | collective-permute-done | bytes 16416 | tf_op jit(solution)/shard_map/ppermute | solution.py:412
  11.9 1.8 %shard_map.113 = (f32[32,128]{1,0:T(8,128)S(1)}, f32[32,128]{1,0:T(8,128)S(1)}, f32[32,256]{1,0:T(8,128)S(1)}, f32[32,256]{1,0:T(8,128)S(1)}) custom-call(f32[3,128,128]{2,1,0:T(8,128)S(1)} %get-tuple-element.15.fields, s32[8,128,128]{2,1,0:T(8,128)} %mask.11, f32[8,128,128]{2,1,0:T(8,128)} %temp.5, f32[8,128,128]{2,1,0:T(8,128)} %east.3, ...), custom_call_target="tpu_custom_call" | custom-call | flops 4000000 | bytes 1000000 | tf_op jit(solution)/shard_map/pallas_call | solution.py:44
  13.7 0.1 collective-permute-start.2
  13.8 26.8 %collective-permute-done = s32[1,1,8]{2,1,0:T(1,128)S(1)} collective-permute-done((s32[1,1,8]{2,1,0:T(1,128)S(1)}, s32[1,1,8]{2,1,0:T(1,128)S(1)}, u32[]{:S(2)}, u32[]{:S(2)}) %collective-permute-start) | collective-permute-done | bytes 64 | tf_op jit(solution)/shard_map/ppermute | solution.py:412
  40.5 0.6 copy-done.6
  41.1 2.9 %collective-permute-start.3 = (f32[32,256]{1,0:T(8,128)S(1)}, f32[32,256]{1,0:T(8,128)S(1)}, u32[]{:S(2)}, u32[]{:S(2)}) collective-permute-start(f32[32,256]{1,0:T(8,128)S(1)} %get-tuple-element.20), channel_id=1, source_target_pairs={{0,30},{2,0},{4,2},{6,4},{8,6},{10,8},{12,10},{14,12},{16,14},{18,... | collective-permute-start | bytes 98312 | tf_op jit(solution)/shard_map/ppermute | solution.py:412
  44.1 0.8 %fusion = (f32[4,128,128]{2,1,0:T(8,128)}, f32[4,128,128]{2,1,0:T(8,128)}) fusion(f32[8,128,128]{2,1,0:T(8,128)S(1)} %copy-done.8), kind=kLoop, calls=%fused_computation | loop fusion | bytes 1048576 | tf_op jit(solution)/shard_map/slice | solution.py:491
  44.9 0.9 %collective-permute-done.3.from_east = f32[32,256]{1,0:T(8,128)S(1)} collective-permute-done((f32[32,256]{1,0:T(8,128)S(1)}, f32[32,256]{1,0:T(8,128)S(1)}, u32[]{:S(2)}, u32[]{:S(2)}) %collective-permute-start.3) | collective-permute-done | bytes 32800 | tf_op jit(solution)/shard_map/ppermute | solution.py:412
  45.8 2.5 %shard_map.115 = (f32[8,144,256]{2,1,0:T(8,128)S(1)}, f32[32,1,128]{2,1,0:T(1,128)}) custom-call(f32[3,128,128]{2,1,0:T(8,128)S(1)} %get-tuple-element.15.fields, f32[32,128]{1,0:T(8,128)S(1)} %get-tuple-element.17.from_south, f32[32,128]{1,0:T(8,128)S(1)} %get-tuple-element.18.from_north, f32[32,256]{1,0:T(8,128)S(1)} %collective-permute-done.2.from_west, ...), custom_call_target="tpu_custom_call" | custom-call | flops 4000000 | bytes 1000000 | tf_op jit(solution)/shard_map/pallas_call | solution.py:44
  48.4 6.2 %all-to-all-start = ((f32[32,1,128]{2,1,0:T(1,128)}), f32[32,1,128]{2,1,0:T(1,128)S(1)}, u32[]{:S(2)}, u32[]{:S(2)}) async-start(f32[32,1,128]{2,1,0:T(1,128)} %get-tuple-element.21), calls=%async_computation | async-start | bytes 32768 | tf_op jit(solution)/shard_map/all_to_all | solution.py:416
  54.6 2.0 %shard_map.114.tracer = f32[8,128,128]{2,1,0:T(8,128)S(1)} custom-call(f32[8,128,128]{2,1,0:T(8,128)} %temp.5, f32[8,128,128]{2,1,0:T(8,128)} %east.3, f32[8,128,128]{2,1,0:T(8,128)} %north.3, s32[8,128,128]{2,1,0:T(8,128)} %mask.11, f32[32,128]{1,0:T(8,128)S(1)} %get-tuple-element.17.from_south, f32[32,128]{1,0:T(8,128)S(1)} %get-tuple-element.18.from_north), custom_call_target="tpu_custom_call" | custom-call | flops 4000000 | bytes 1000000 | tf_op jit(solution)/shard_map/pallas_call | solution.py:44
  56.6 0.0 copy-start.1
  56.6 0.8 %copy-done.1 = f32[8,128,128]{2,1,0:T(8,128)} copy-done((f32[8,128,128]{2,1,0:T(8,128)}, f32[8,128,128]{2,1,0:T(8,128)S(1)}, u32[]{:S(2)}) %copy-start.1) | copy-done | bytes 524312
  57.4 4.3 %all-to-all-done = f32[32,1,128]{2,1,0:T(1,128)S(1)} async-done(((f32[32,1,128]{2,1,0:T(1,128)}), f32[32,1,128]{2,1,0:T(1,128)S(1)}, u32[]{:S(2)}, u32[]{:S(2)}) %all-to-all-start) | async-done | bytes 16416 | tf_op jit(solution)/shard_map/all_to_all | solution.py:416
  61.7 2.2 %shard_map.116 = (f32[128,128]{1,0:T(8,128)}, f32[128,128]{1,0:T(8,128)S(1)}) custom-call(f32[32,128]{1,0:T(8,128)S(1)} %bitcast.2, f32[8,144,256]{2,1,0:T(8,128)S(1)} %get-tuple-element.22.basis), custom_call_target="tpu_custom_call" | custom-call | flops 4000000 | bytes 1000000 | tf_op jit(solution)/shard_map/pallas_call | solution.py:44
  63.9 2.6 %shard_map.117 = (f32[8,128,128]{2,1,0:T(8,128)S(1)}, f32[8,128,128]{2,1,0:T(8,128)}) custom-call(s32[8]{0:T(128)S(1)} %bitcast.3, f32[8,128,128]{2,1,0:T(8,128)} %copy-done.1, f32[128,128]{1,0:T(8,128)S(1)} %get-tuple-element.23.pressure, f32[32,256]{1,0:T(8,128)S(1)} %copy-done.3, f32[32,256]{1,0:T(8,128)S(1)} %copy-done.5, s32[8,128,128]{2,1,0:T(8,128)S(1)} %copy-done, ...), custom_call_target="tpu_custom_call" | custom-call | flops 4000000 | bytes 1000000 | tf_op jit(solution)/shard_map/pallas_call | solution.py:44
  66.5 1.7 %shard_map.118.refs_0_ = f32[8,128,128]{2,1,0:T(8,128)} custom-call(s32[8]{0:T(128)S(1)} %bitcast.4, f32[8,128,128]{2,1,0:T(8,128)S(1)} %get-tuple-element.24.partial, f32[128,128]{1,0:T(8,128)S(1)} %get-tuple-element.23.pressure, s32[8,128,128]{2,1,0:T(8,128)S(1)} %copy-done, f32[8,128,128]{2,1,0:T(8,128)S(1)} %collective-permute-done.6.inner, ...), custom_call_target="tpu_custom_call" | custom-call | flops 1000000 | bytes 1000000 | tf_op jit(solution)/shard_map/pallas_call | solution.py:394
  68.3 1.3 %shard_map.119 = f32[8,128,128]{2,1,0:T(8,128)} custom-call(s32[8]{0:T(128)S(1)} %bitcast.5, f32[8,128,128]{2,1,0:T(8,128)S(1)} %get-tuple-element.24.partial, f32[128,128]{1,0:T(8,128)S(1)} %get-tuple-element.23.pressure, s32[8,128,128]{2,1,0:T(8,128)S(1)} %copy-done, ...), custom_call_target="tpu_custom_call", output_to_operand_aliasing={{}: (6, {})} | custom-call | flops 1000000 | bytes 1000000 | tf_op jit(solution)/shard_map/pallas_call | solution.py:394
  (25 shorter events, 0.1 us)
Async XLA Ops:
  0.6 9.1 %copy-start.9 = (s32[1,1,8]{2,1,0:T(1,128)S(1)}, s32[1,1,8]{2,1,0:T(1,128)}, u32[]{:S(2)}) copy-start(s32[1,1,8]{2,1,0:T(1,128)} %param.15) | copy-start | bytes 100
  0.6 63.3 %collective-permute-start.4 = (f32[8,128,128]{2,1,0:T(8,128)}, f32[8,128,128]{2,1,0:T(8,128)S(1)}, u32[]{:S(2)}, u32[]{:S(2)}) collective-permute-start(f32[8,128,128]{2,1,0:T(8,128)} %param.13), channel_id=1, source_target_pairs={{0,16},{2,18},{4,20},{6,22},{8,0},{10,2},{12,4},{14,6},{16,24},{18... | collective-permute-start | bytes 1572872 | tf_op jit(solution)/shard_map/ppermute | solution.py:430
  4.8 59.2 %collective-permute-start.5 = (f32[8,128,128]{2,1,0:T(8,128)}, f32[8,128,128]{2,1,0:T(8,128)S(1)}, u32[]{:S(2)}, u32[]{:S(2)}) collective-permute-start(f32[8,128,128]{2,1,0:T(8,128)} %param.13), channel_id=1, source_target_pairs={{0,8},{2,10},{4,12},{6,14},{8,24},{10,26},{12,28},{14,30},{16,0},{... | collective-permute-start | bytes 1572872 | tf_op jit(solution)/shard_map/ppermute | solution.py:430
  4.8 61.8 %collective-permute-start.6 = (f32[8,128,128]{2,1,0:T(8,128)}, f32[8,128,128]{2,1,0:T(8,128)S(1)}, u32[]{:S(2)}, u32[]{:S(2)}) collective-permute-start(f32[8,128,128]{2,1,0:T(8,128)} %param.14), channel_id=1, source_target_pairs={{0,8},{2,10},{4,12},{6,14},{8,24},{10,26},{12,28},{14,30},{16,0},{... | collective-permute-start | bytes 1572872 | tf_op jit(solution)/shard_map/ppermute | solution.py:430
  8.1 36.0 %copy-start.8 = (f32[8,128,128]{2,1,0:T(8,128)S(1)}, f32[8,128,128]{2,1,0:T(8,128)}, u32[]{:S(2)}) copy-start(f32[8,128,128]{2,1,0:T(8,128)} %param.14) | copy-start | bytes 1572868
  8.1 3.8 %collective-permute-start.1 = (f32[32,128]{1,0:T(8,128)S(1)}, f32[32,128]{1,0:T(8,128)S(1)}, u32[]{:S(2)}, u32[]{:S(2)}) collective-permute-start(f32[32,128]{1,0:T(8,128)S(1)} %get-tuple-element.16), channel_id=1, source_target_pairs={{0,1},{1,0},{2,3},{3,2},{4,5},{5,4},{6,7},{7,6},{8,9},{9,8},{10,11... | collective-permute-start | bytes 49160 | tf_op jit(solution)/shard_map/ppermute | solution.py:412
  9.7 30.8 %collective-permute-start = (s32[1,1,8]{2,1,0:T(1,128)S(1)}, s32[1,1,8]{2,1,0:T(1,128)S(1)}, u32[]{:S(2)}, u32[]{:S(2)}) collective-permute-start(s32[1,1,8]{2,1,0:T(1,128)S(1)} %copy-done.9), channel_id=1, source_target_pairs={{0,16},{2,18},{4,20},{6,22},{8,24},{10,26},{12,28},{14,30},{16,0},... | collective-permute-start | bytes 104 | tf_op jit(solution)/shard_map/ppermute | solution.py:412
  13.7 31.2 %collective-permute-start.2 = (f32[32,256]{1,0:T(8,128)S(1)}, f32[32,256]{1,0:T(8,128)S(1)}, u32[]{:S(2)}, u32[]{:S(2)}) collective-permute-start(f32[32,256]{1,0:T(8,128)S(1)} %get-tuple-element.19), channel_id=1, source_target_pairs={{0,2},{2,4},{4,6},{6,8},{8,10},{10,12},{12,14},{14,16},{16,18},{18... | collective-permute-start | bytes 98312 | tf_op jit(solution)/shard_map/ppermute | solution.py:412
  40.5 0.6 copy-start.6
  41.1 4.7 %collective-permute-start.3 = (f32[32,256]{1,0:T(8,128)S(1)}, f32[32,256]{1,0:T(8,128)S(1)}, u32[]{:S(2)}, u32[]{:S(2)}) collective-permute-start(f32[32,256]{1,0:T(8,128)S(1)} %get-tuple-element.20), channel_id=1, source_target_pairs={{0,30},{2,0},{4,2},{6,4},{8,6},{10,8},{12,10},{14,12},{16,14},{18,... | collective-permute-start | bytes 98312 | tf_op jit(solution)/shard_map/ppermute | solution.py:412
  44.9 3.5 %copy-start.2 = (f32[32,256]{1,0:T(8,128)}, f32[32,256]{1,0:T(8,128)S(1)}, u32[]{:S(2)}) copy-start(f32[32,256]{1,0:T(8,128)S(1)} %collective-permute-done.2.from_west) | copy-start | bytes 98308
  44.9 21.6 %collective-permute-start.8 = (f32[4,128,128]{2,1,0:T(8,128)}, f32[4,128,128]{2,1,0:T(8,128)}, u32[]{:S(2)}, u32[]{:S(2)}) collective-permute-start(f32[4,128,128]{2,1,0:T(8,128)} %get-tuple-element.27), channel_id=1, source_target_pairs={{0,16},{2,18},{4,20},{6,22},{8,0},{10,2},{12,4},{14,6},{16,24},{18... | collective-permute-start | bytes 786440 | tf_op jit(solution)/shard_map/ppermute | solution.py:430
  45.8 2.5 %copy-start.4 = (f32[32,256]{1,0:T(8,128)}, f32[32,256]{1,0:T(8,128)S(1)}, u32[]{:S(2)}) copy-start(f32[32,256]{1,0:T(8,128)S(1)} %collective-permute-done.3.from_east) | copy-start | bytes 98308
  45.8 22.4 %collective-permute-start.7 = (f32[4,128,128]{2,1,0:T(8,128)}, f32[4,128,128]{2,1,0:T(8,128)S(1)}, u32[]{:S(2)}, u32[]{:S(2)}) collective-permute-start(f32[4,128,128]{2,1,0:T(8,128)} %get-tuple-element.28), channel_id=1, source_target_pairs={{0,16},{2,18},{4,20},{6,22},{8,0},{10,2},{12,4},{14,6},{16,24},{18... | collective-permute-start | bytes 786440 | tf_op jit(solution)/shard_map/ppermute | solution.py:430
  48.4 13.4 %all-to-all-start = ((f32[32,1,128]{2,1,0:T(1,128)}), f32[32,1,128]{2,1,0:T(1,128)S(1)}, u32[]{:S(2)}, u32[]{:S(2)}) async-start(f32[32,1,128]{2,1,0:T(1,128)} %get-tuple-element.21), calls=%async_computation | async-start | bytes 32768 | tf_op jit(solution)/shard_map/all_to_all | solution.py:416
  56.6 0.8 %copy-start.1 = (f32[8,128,128]{2,1,0:T(8,128)}, f32[8,128,128]{2,1,0:T(8,128)S(1)}, u32[]{:S(2)}) copy-start(f32[8,128,128]{2,1,0:T(8,128)S(1)} %shard_map.114.tracer) | copy-start | bytes 1572868
  57.4 6.5 %copy-start = (s32[8,128,128]{2,1,0:T(8,128)S(1)}, s32[8,128,128]{2,1,0:T(8,128)}, u32[]{:S(2)}) copy-start(s32[8,128,128]{2,1,0:T(8,128)} %mask.11) | copy-start | bytes 1572868
  61.7 2.2 %copy-start.3 = (f32[32,256]{1,0:T(8,128)S(1)}, f32[32,256]{1,0:T(8,128)}, u32[]{:S(2)}) copy-start(f32[32,256]{1,0:T(8,128)} %copy-done.2) | copy-start | bytes 98308
  61.7 2.2 %copy-start.5 = (f32[32,256]{1,0:T(8,128)S(1)}, f32[32,256]{1,0:T(8,128)}, u32[]{:S(2)}) copy-start(f32[32,256]{1,0:T(8,128)} %copy-done.4) | copy-start | bytes 98308
  61.7 2.2 %copy-start.7 = (s32[1,1,8]{2,1,0:T(1,128)S(1)}, s32[1,1,8]{2,1,0:T(1,128)}, u32[]{:S(2)}) copy-start(s32[1,1,8]{2,1,0:T(1,128)} %copy-done.6) | copy-start | bytes 100

commit v6 on v5

--- a/solution.py
+++ b/solution.py
@@ -99,7 +99,17 @@
         send(slice(base + level, base + level + 1), flux_north[-1:], flux_south[:1])
 
 
-def pack_x_kernel(levels, received, fields, mask, temp, east, *refs):
+def pack_t_kernel(levels, mask, temp, east, to_east, to_west):
+    for level in range(levels):
+        at = slice(level, level + 1)
+        masked = mask[level].astype(jnp.float32) * temp[level]
+        flux_east = (DIFFUSE - 0.5 * east[level]) * masked
+        flux_west = (DIFFUSE + 0.5 * east[level]) * masked
+        to_east[at, :] = jnp.transpose(flux_east[:, -LANES:])[-1:]
+        to_west[at, :] = jnp.transpose(flux_west[:, :LANES])[:1]
+
+
+def pack_x_kernel(levels, received, fields, tracer_east, tracer_west, *refs):
     arrived, (from_south, from_north, to_east, to_west) = refs[:received], refs[received:]
     if received == 1:
         lower = lax.axis_index("gy") == 0
@@ -116,17 +126,11 @@
         flipped = jnp.transpose(jnp.concatenate([fields[at]] + beside, axis=0))
         to_west[span, :] = flipped[:RING]
         to_east[span, :] = flipped[-RING:]
-    base = 3 * RING
-    for level in range(levels):
-        at = slice(base + level, base + level + 1)
-        masked = mask[level].astype(jnp.float32) * temp[level]
-        flux_east = (DIFFUSE - 0.5 * east[level]) * masked
-        flux_west = (DIFFUSE + 0.5 * east[level]) * masked
-        to_east[at, :rows] = jnp.transpose(flux_east[:, -LANES:])[-1:]
-        to_west[at, :rows] = jnp.transpose(flux_west[:, :LANES])[:1]
-    spare = slice(base, base + levels)
-    to_east[spare, rows:] = jnp.zeros((levels, LANES), jnp.float32)
-    to_west[spare, rows:] = jnp.zeros((levels, LANES), jnp.float32)
+    span = slice(3 * RING, 3 * RING + levels)
+    to_east[span, :rows] = tracer_east[...]
+    to_west[span, :rows] = tracer_west[...]
+    to_east[span, rows:] = jnp.zeros((levels, LANES), jnp.float32)
+    to_west[span, rows:] = jnp.zeros((levels, LANES), jnp.float32)
 
 
 def beside_tile(from_west, from_east, start, size):
@@ -374,16 +378,27 @@
 
 def salt_kernel(levels, first, slots, partial, pressure, mask, inner, part, *refs):
     result, done, sems = refs[-3:]
-    size = part.shape[0]
-    copies = []
-    for at in range(size):
-        level = level_of_slot(slots, first + at, levels)
-        dense = density(level, levels, pressure, mask)
-        done[at] = partial[level] + CABBELING * jnp.where(from_outer(), part[at], inner[first + at]) * dense
-        copies.append(pltpu.make_async_copy(done.at[at], result.at[level], sems.at[at]))
-        copies[-1].start()
-    for copy in copies:
-        copy.wait()
+
+    def finished(values, start):
+        copies = []
+        for at in range(values.shape[0]):
+            level = level_of_slot(slots, start + at, levels)
+            dense = density(level, levels, pressure, mask)
+            done[at] = partial[level] + CABBELING * values[at] * dense
+            copies.append(pltpu.make_async_copy(done.at[at], result.at[level], sems.at[at]))
+            copies[-1].start()
+        for copy in copies:
+            copy.wait()
+
+    @pl.when(from_outer())
+    def _():
+        finished(part, first)
+
+    if first == 0:
+
+        @pl.when(jnp.logical_not(from_outer()))
+        def _():
+            finished(inner, 0)
 
 
 def finish(levels, first, args, before):
@@ -397,8 +412,8 @@
         in_specs=[SMEM] + [VMEM] * len(held_args) + ([] if before is None else [HBM]),
         out_specs=HBM,
         scratch_shapes=[
-            pltpu.VMEM(part.shape, jnp.float32),
-            pltpu.SemaphoreType.DMA((part.shape[0],)),
+            pltpu.VMEM(shape, jnp.float32),
+            pltpu.SemaphoreType.DMA((levels,)),
         ],
         input_output_aliases={} if before is None else {len(operands) - 1: 0},
         compiler_params=pltpu.CompilerParams(vmem_limit_bytes=KERNEL_VMEM),
@@ -436,7 +451,8 @@
 
 
 def runs(levels):
-    return levels // 2, levels - levels // 2
+    most = 5 * levels // 8
+    return most, levels - most
 
 
 def body(
@@ -472,10 +488,13 @@
     else:
         arrived = [shifted(messages[0], "gy", 1, False)]
         arrived += [shifted(messages[1], "gy", -1, False)]
+    tracer_east, tracer_west = call(
+        functools.partial(pack_t_kernel, levels), [(levels, rows)] * 2, stored(land_mask, temp_adjoint, east_velocity)
+    )
     from_south, from_north, to_east, to_west = call(
         functools.partial(pack_x_kernel, levels, len(arrived)),
         [(strip, columns)] * 2 + [(strip, rows + LANES)] * 2,
-        held(fields) + stored(land_mask, temp_adjoint, east_velocity) + held(*arrived),
+        held(fields, tracer_east, tracer_west, *arrived),
     )
     from_west = shifted(to_east, "gx", 1, True)
     from_east = shifted(to_west, "gx", -1, True)

time: 69.9 us -> 76.9 us (1.10)
  waiting for transfers between devices: 33.2 us -> 39.8 us
  local copies, waits for them, and re-layouts: 2.25 us -> 4.18 us
  starting transfers between devices: 17.9 us -> 16.8 us
    ppermute x4, waiting for transfers between devices: 28.9 us -> 35.5 us  [shifted(): return lax.ppermute(value, axis, pairs)]
    ppermute x5, starting transfers between devices: 6.03 us -> 8.66 us  [fetched(): return lax.ppermute(value, 'gx', pairs)]
    slice x1 -> x2, local copies, waits for them, and re-layouts: 0.84 us -> 3.37 us  [body(): cuts.append(lax.slice_in_dim(salt_store, start, start + size))]
    ppermute x4, starting transfers between devices: 5.62 us -> 3.59 us  [shifted(): return lax.ppermute(value, axis, pairs)]
    all_to_all x1, starting transfers between devices: 6.21 us -> 4.56 us  [shared(): rows = lax.all_to_all(rows, ('gx', 'gy'), 0, 0)]
    pallas_call x6 -> x7, Pallas kernels: 12.5 us -> 12.5 us  [call(): pl.pallas_call(kernel, out_shape=shapes, in_specs=specs, out_specs=[VMEM]...]
  transfers between devices with their start and end apart: 10 -> 10, of which waited for: 4 -> 4; matrix products, arithmetic and copies ran while one was open for 1% -> 4% of each run, Pallas kernels for 20% -> 19%
where the time goes in v6:
time: 76.9 us; the launch traced here: 76.6 us
  waiting for transfers between devices  39.8 us (52%)
  starting transfers between devices  16.8 us (22%)
  Pallas kernels  15 us (20%)
  local copies, waits for them, and re-layouts  4.18 us (5%)
    ppermute x4, waiting for transfers between devices, shifted(): return lax.ppermute(value, axis, pairs)  35.5 us
    pallas_call x7, Pallas kernels, call(): pl.pallas_call(kernel, out_shape=shapes, in_specs=specs, out_specs=[VMEM]...  12.5 us
    ppermute x5, starting transfers between devices, fetched(): return lax.ppermute(value, 'gx', pairs)  8.66 us
    all_to_all x1, starting transfers between devices, shared(): rows = lax.all_to_all(rows, ('gx', 'gy'), 0, 0)  4.56 us
    all_to_all x1, waiting for transfers between devices, shared(): rows = lax.all_to_all(rows, ('gx', 'gy'), 0, 0)  4.33 us
    ppermute x4, starting transfers between devices, shifted(): return lax.ppermute(value, axis, pairs)  3.59 us
    slice x2, local copies, waits for them, and re-layouts, body(): cuts.append(lax.slice_in_dim(salt_store, start, start + size))  3.37 us
    pallas_call x2, Pallas kernels, finish(): pl.pallas_call(functools.partial(salt_kernel, levels, first), out_shape=j...  2.51 us
  transfers between devices with their start and end apart: 10, of which 4 were waited for; matrix products, arithmetic and copies ran while one was open for 4% of the time, Pallas kernels for 19%

profile of v6, /device:TPU:0, one launch (start us, length us, event | category | flops | bytes accessed | tf_op | source)
XLA Modules:
  0.0 76.6 jit_solution(7086000431941944263)
XLA Ops:
  0.6 4.1 %collective-permute-start.4 = (f32[8,128,128]{2,1,0:T(8,128)}, f32[8,128,128]{2,1,0:T(8,128)S(1)}, u32[]{:S(2)}, u32[]{:S(2)}) collective-permute-start(f32[8,128,128]{2,1,0:T(8,128)} %param.13), channel_id=1, source_target_pairs={{0,16},{2,18},{4,20},{6,22},{8,0},{10,2},{12,4},{14,6},{16,24},{18... | collective-permute-start | bytes 1572872 | tf_op jit(solution)/shard_map/ppermute | solution.py:445
  4.8 1.9 %collective-permute-start.6 = (f32[8,128,128]{2,1,0:T(8,128)}, f32[8,128,128]{2,1,0:T(8,128)S(1)}, u32[]{:S(2)}, u32[]{:S(2)}) collective-permute-start(f32[8,128,128]{2,1,0:T(8,128)} %param.14), channel_id=1, source_target_pairs={{0,8},{2,10},{4,12},{6,14},{8,24},{10,26},{12,28},{14,30},{16,0},{... | collective-permute-start | bytes 1572872 | tf_op jit(solution)/shard_map/ppermute | solution.py:445
  6.7 1.8 %slice.7 = f32[5,128,128]{2,1,0:T(8,128)} slice(f32[8,128,128]{2,1,0:T(8,128)} %param.14), slice={[0:5], [0:128], [0:128]} | slice | bytes 655360 | tf_op jit(solution)/shard_map/slice | solution.py:510
  8.4 1.0 %collective-permute-start.8 = (f32[5,128,128]{2,1,0:T(8,128)}, f32[5,128,128]{2,1,0:T(8,128)}, u32[]{:S(2)}, u32[]{:S(2)}) collective-permute-start(f32[5,128,128]{2,1,0:T(8,128)} %slice.7), channel_id=1, source_target_pairs={{0,16},{2,18},{4,20},{6,22},{8,0},{10,2},{12,4},{14,6},{16,24},{18... | collective-permute-start | bytes 983048 | tf_op jit(solution)/shard_map/ppermute | solution.py:445
  9.5 1.4 %shard_map.112 = (f32[3,128,128]{2,1,0:T(8,128)S(1)}, f32[32,128]{1,0:T(8,128)S(1)}) custom-call(f32[128,128]{1,0:T(8,128)} %height.1, s32[8,128,128]{2,1,0:T(8,128)} %mask.11, f32[128,128]{1,0:T(8,128)} %depth.1, f32[8,128,128]{2,1,0:T(8,128)} %temp.5, f32[8,128,128]{2,1,0:T(8,128)} %north.3), custom_call_target="tpu_custom_call" | custom-call | flops 4000000 | bytes 1000000 | tf_op jit(solution)/shard_map/pallas_call | solution.py:44
  10.9 0.0 copy-start.4
  10.9 1.6 %collective-permute-start.1 = (f32[32,128]{1,0:T(8,128)S(1)}, f32[32,128]{1,0:T(8,128)S(1)}, u32[]{:S(2)}, u32[]{:S(2)}) collective-permute-start(f32[32,128]{1,0:T(8,128)S(1)} %get-tuple-element.20), channel_id=1, source_target_pairs={{0,1},{1,0},{2,3},{3,2},{4,5},{5,4},{6,7},{7,6},{8,9},{9,8},{10,11... | collective-permute-start | bytes 49160 | tf_op jit(solution)/shard_map/ppermute | solution.py:427
  12.5 1.7 %shard_map.113 = (f32[8,128]{1,0:T(8,128)S(1)}, f32[8,128]{1,0:T(8,128)S(1)}) custom-call(s32[8,128,128]{2,1,0:T(8,128)} %mask.11, f32[8,128,128]{2,1,0:T(8,128)} %temp.5, f32[8,128,128]{2,1,0:T(8,128)} %east.3), custom_call_target="tpu_custom_call" | custom-call | flops 4000000 | bytes 1000000 | tf_op jit(solution)/shard_map/pallas_call | solution.py:44
  14.2 0.5 collective-permute-done.1.refs_0_
  14.7 2.0 %collective-permute-start = (s32[1,1,8]{2,1,0:T(1,128)S(1)}, s32[1,1,8]{2,1,0:T(1,128)S(1)}, u32[]{:S(2)}, u32[]{:S(2)}) collective-permute-start(s32[1,1,8]{2,1,0:T(1,128)S(1)} %copy-done.4), channel_id=1, source_target_pairs={{0,16},{2,18},{4,20},{6,22},{8,24},{10,26},{12,28},{14,30},{16,0},... | collective-permute-start | bytes 104 | tf_op jit(solution)/shard_map/ppermute | solution.py:427
  16.7 0.2 shard_map.114
  16.9 28.9 %collective-permute-done = s32[1,1,8]{2,1,0:T(1,128)S(1)} collective-permute-done((s32[1,1,8]{2,1,0:T(1,128)S(1)}, s32[1,1,8]{2,1,0:T(1,128)S(1)}, u32[]{:S(2)}, u32[]{:S(2)}) %collective-permute-start) | collective-permute-done | bytes 64 | tf_op jit(solution)/shard_map/ppermute | solution.py:427
  45.8 6.0 %collective-permute-done.2.from_west = f32[32,256]{1,0:T(8,128)S(1)} collective-permute-done((f32[32,256]{1,0:T(8,128)S(1)}, f32[32,256]{1,0:T(8,128)S(1)}, u32[]{:S(2)}, u32[]{:S(2)}) %collective-permute-start.2) | collective-permute-done | bytes 32800 | tf_op jit(solution)/shard_map/ppermute | solution.py:427
  51.8 1.6 %slice.6 = f32[3,128,128]{2,1,0:T(8,128)} slice(f32[8,128,128]{2,1,0:T(8,128)} %param.14), slice={[5:8], [0:128], [0:128]} | slice | bytes 393216 | tf_op jit(solution)/shard_map/slice | solution.py:510
  53.4 1.6 %collective-permute-start.7 = (f32[3,128,128]{2,1,0:T(8,128)}, f32[3,128,128]{2,1,0:T(8,128)S(1)}, u32[]{:S(2)}, u32[]{:S(2)}) collective-permute-start(f32[3,128,128]{2,1,0:T(8,128)} %slice.6), channel_id=1, source_target_pairs={{0,16},{2,18},{4,20},{6,22},{8,0},{10,2},{12,4},{14,6},{16,24},{18... | collective-permute-start | bytes 589832 | tf_op jit(solution)/shard_map/ppermute | solution.py:445
  55.0 2.5 %shard_map.116 = (f32[8,144,256]{2,1,0:T(8,128)S(1)}, f32[32,1,128]{2,1,0:T(1,128)}) custom-call(f32[3,128,128]{2,1,0:T(8,128)S(1)} %get-tuple-element.17.fields, f32[32,128]{1,0:T(8,128)S(1)} %get-tuple-element.21.from_south, f32[32,128]{1,0:T(8,128)S(1)} %get-tuple-element.22.from_north, f32[32,256]{1,0:T(8,128)S(1)} %collective-permute-done.2.from_west, ...), custom_call_target="tpu_custom_call" | custom-call | flops 4000000 | bytes 1000000 | tf_op jit(solution)/shard_map/pallas_call | solution.py:44
  57.6 4.6 %all-to-all-start = ((f32[32,1,128]{2,1,0:T(1,128)}), f32[32,1,128]{2,1,0:T(1,128)S(1)}, u32[]{:S(2)}, u32[]{:S(2)}) async-start(f32[32,1,128]{2,1,0:T(1,128)} %get-tuple-element.25), calls=%async_computation | async-start | bytes 32768 | tf_op jit(solution)/shard_map/all_to_all | solution.py:431
  62.1 2.0 %shard_map.115.tracer = f32[8,128,128]{2,1,0:T(8,128)S(1)} custom-call(f32[8,128,128]{2,1,0:T(8,128)} %temp.5, f32[8,128,128]{2,1,0:T(8,128)} %east.3, f32[8,128,128]{2,1,0:T(8,128)} %north.3, s32[8,128,128]{2,1,0:T(8,128)} %mask.11, f32[32,128]{1,0:T(8,128)S(1)} %get-tuple-element.21.from_south, f32[32,128]{1,0:T(8,128)S(1)} %get-tuple-element.22.from_north), custom_call_target="tpu_custom_call" | custom-call | flops 4000000 | bytes 1000000 | tf_op jit(solution)/shard_map/pallas_call | solution.py:44
  64.2 0.8 %copy-done.1 = f32[8,128,128]{2,1,0:T(8,128)} copy-done((f32[8,128,128]{2,1,0:T(8,128)}, f32[8,128,128]{2,1,0:T(8,128)S(1)}, u32[]{:S(2)}) %copy-start.1) | copy-done | bytes 524312
  65.0 4.3 %all-to-all-done = f32[32,1,128]{2,1,0:T(1,128)S(1)} async-done(((f32[32,1,128]{2,1,0:T(1,128)}), f32[32,1,128]{2,1,0:T(1,128)S(1)}, u32[]{:S(2)}, u32[]{:S(2)}) %all-to-all-start) | async-done | bytes 16416 | tf_op jit(solution)/shard_map/all_to_all | solution.py:431
  69.3 2.2 %shard_map.117 = (f32[128,128]{1,0:T(8,128)}, f32[128,128]{1,0:T(8,128)S(1)}) custom-call(f32[32,128]{1,0:T(8,128)S(1)} %bitcast.2, f32[8,144,256]{2,1,0:T(8,128)S(1)} %get-tuple-element.26.basis), custom_call_target="tpu_custom_call" | custom-call | flops 4000000 | bytes 1000000 | tf_op jit(solution)/shard_map/pallas_call | solution.py:44
  71.5 2.6 %shard_map.118 = (f32[8,128,128]{2,1,0:T(8,128)S(1)}, f32[8,128,128]{2,1,0:T(8,128)}) custom-call(s32[8]{0:T(128)S(1)} %bitcast.3, f32[8,128,128]{2,1,0:T(8,128)} %copy-done.1, f32[128,128]{1,0:T(8,128)S(1)} %get-tuple-element.27.pressure, f32[32,256]{1,0:T(8,128)S(1)} %collective-permute-done.2.from_west, f32[32,256]{1,0:T(8,128)S(1)} %collective-permute-done.3.from_east, ...), custom_call_target="tpu_custom_call" | custom-call | flops 4000000 | bytes 1000000 | tf_op jit(solution)/shard_map/pallas_call | solution.py:44
  74.0 1.9 %shard_map.119.refs_0_ = f32[8,128,128]{2,1,0:T(8,128)} custom-call(s32[8]{0:T(128)S(1)} %bitcast.4, f32[8,128,128]{2,1,0:T(8,128)S(1)} %get-tuple-element.28.partial, f32[128,128]{1,0:T(8,128)S(1)} %get-tuple-element.27.pressure, s32[8,128,128]{2,1,0:T(8,128)S(1)} %copy-done, f32[8,128,128]{2,1,0:T(8,128)S(1)} %collective-permute-done.6.inner, ...), custom_call_target="tpu_custom_call" | custom-call | flops 1000000 | bytes 1000000 | tf_op jit(solution)/shard_map/pallas_call | solution.py:409
  75.9 0.6 shard_map.120
  (17 shorter events, 0.0 us)
Async XLA Ops:
  0.6 70.8 %collective-permute-start.4 = (f32[8,128,128]{2,1,0:T(8,128)}, f32[8,128,128]{2,1,0:T(8,128)S(1)}, u32[]{:S(2)}, u32[]{:S(2)}) collective-permute-start(f32[8,128,128]{2,1,0:T(8,128)} %param.13), channel_id=1, source_target_pairs={{0,16},{2,18},{4,20},{6,22},{8,0},{10,2},{12,4},{14,6},{16,24},{18... | collective-permute-start | bytes 1572872 | tf_op jit(solution)/shard_map/ppermute | solution.py:445
  4.7 66.7 %collective-permute-start.5 = (f32[8,128,128]{2,1,0:T(8,128)}, f32[8,128,128]{2,1,0:T(8,128)S(1)}, u32[]{:S(2)}, u32[]{:S(2)}) collective-permute-start(f32[8,128,128]{2,1,0:T(8,128)} %param.13), channel_id=1, source_target_pairs={{0,8},{2,10},{4,12},{6,14},{8,24},{10,26},{12,28},{14,30},{16,0},{... | collective-permute-start | bytes 1572872 | tf_op jit(solution)/shard_map/ppermute | solution.py:445
  4.8 69.3 %collective-permute-start.6 = (f32[8,128,128]{2,1,0:T(8,128)}, f32[8,128,128]{2,1,0:T(8,128)S(1)}, u32[]{:S(2)}, u32[]{:S(2)}) collective-permute-start(f32[8,128,128]{2,1,0:T(8,128)} %param.14), channel_id=1, source_target_pairs={{0,8},{2,10},{4,12},{6,14},{8,24},{10,26},{12,28},{14,30},{16,0},{... | collective-permute-start | bytes 1572872 | tf_op jit(solution)/shard_map/ppermute | solution.py:445
  8.4 65.6 %collective-permute-start.8 = (f32[5,128,128]{2,1,0:T(8,128)}, f32[5,128,128]{2,1,0:T(8,128)}, u32[]{:S(2)}, u32[]{:S(2)}) collective-permute-start(f32[5,128,128]{2,1,0:T(8,128)} %slice.7), channel_id=1, source_target_pairs={{0,16},{2,18},{4,20},{6,22},{8,0},{10,2},{12,4},{14,6},{16,24},{18... | collective-permute-start | bytes 983048 | tf_op jit(solution)/shard_map/ppermute | solution.py:445
  10.9 3.8 %copy-start.4 = (s32[1,1,8]{2,1,0:T(1,128)S(1)}, s32[1,1,8]{2,1,0:T(1,128)}, u32[]{:S(2)}) copy-start(s32[1,1,8]{2,1,0:T(1,128)} %param.15) | copy-start | bytes 100
  10.9 3.8 %collective-permute-start.1 = (f32[32,128]{1,0:T(8,128)S(1)}, f32[32,128]{1,0:T(8,128)S(1)}, u32[]{:S(2)}, u32[]{:S(2)}) collective-permute-start(f32[32,128]{1,0:T(8,128)S(1)} %get-tuple-element.20), channel_id=1, source_target_pairs={{0,1},{1,0},{2,3},{3,2},{4,5},{5,4},{6,7},{7,6},{8,9},{9,8},{10,11... | collective-permute-start | bytes 49160 | tf_op jit(solution)/shard_map/ppermute | solution.py:427
  14.7 31.1 %collective-permute-start = (s32[1,1,8]{2,1,0:T(1,128)S(1)}, s32[1,1,8]{2,1,0:T(1,128)S(1)}, u32[]{:S(2)}, u32[]{:S(2)}) collective-permute-start(s32[1,1,8]{2,1,0:T(1,128)S(1)} %copy-done.4), channel_id=1, source_target_pairs={{0,16},{2,18},{4,20},{6,22},{8,24},{10,26},{12,28},{14,30},{16,0},... | collective-permute-start | bytes 104 | tf_op jit(solution)/shard_map/ppermute | solution.py:427
  45.8 11.8 %copy-start.2 = (s32[1,1,8]{2,1,0:T(1,128)}, s32[1,1,8]{2,1,0:T(1,128)S(1)}, u32[]{:S(2)}) copy-start(s32[1,1,8]{2,1,0:T(1,128)S(1)} %collective-permute-done) | copy-start | bytes 100
  45.8 6.0 %collective-permute-start.2 = (f32[32,256]{1,0:T(8,128)S(1)}, f32[32,256]{1,0:T(8,128)S(1)}, u32[]{:S(2)}, u32[]{:S(2)}) collective-permute-start(f32[32,256]{1,0:T(8,128)S(1)} %get-tuple-element.23), channel_id=1, source_target_pairs={{0,2},{2,4},{4,6},{6,8},{8,10},{10,12},{12,14},{14,16},{16,18},{18... | collective-permute-start | bytes 98312 | tf_op jit(solution)/shard_map/ppermute | solution.py:427
  51.8 1.6 %collective-permute-start.3 = (f32[32,256]{1,0:T(8,128)S(1)}, f32[32,256]{1,0:T(8,128)S(1)}, u32[]{:S(2)}, u32[]{:S(2)}) collective-permute-start(f32[32,256]{1,0:T(8,128)S(1)} %get-tuple-element.24), channel_id=1, source_target_pairs={{0,30},{2,0},{4,2},{6,4},{8,6},{10,8},{12,10},{14,12},{16,14},{18,... | collective-permute-start | bytes 98312 | tf_op jit(solution)/shard_map/ppermute | solution.py:427
  53.4 22.5 %collective-permute-start.7 = (f32[3,128,128]{2,1,0:T(8,128)}, f32[3,128,128]{2,1,0:T(8,128)S(1)}, u32[]{:S(2)}, u32[]{:S(2)}) collective-permute-start(f32[3,128,128]{2,1,0:T(8,128)} %slice.6), channel_id=1, source_target_pairs={{0,16},{2,18},{4,20},{6,22},{8,0},{10,2},{12,4},{14,6},{16,24},{18... | collective-permute-start | bytes 589832 | tf_op jit(solution)/shard_map/ppermute | solution.py:445
  57.6 11.7 %all-to-all-start = ((f32[32,1,128]{2,1,0:T(1,128)}), f32[32,1,128]{2,1,0:T(1,128)S(1)}, u32[]{:S(2)}, u32[]{:S(2)}) async-start(f32[32,1,128]{2,1,0:T(1,128)} %get-tuple-element.25), calls=%async_computation | async-start | bytes 32768 | tf_op jit(solution)/shard_map/all_to_all | solution.py:431
  64.2 0.8 %copy-start.1 = (f32[8,128,128]{2,1,0:T(8,128)}, f32[8,128,128]{2,1,0:T(8,128)S(1)}, u32[]{:S(2)}) copy-start(f32[8,128,128]{2,1,0:T(8,128)S(1)} %shard_map.115.tracer) | copy-start | bytes 1572868
  64.9 6.5 %copy-start = (s32[8,128,128]{2,1,0:T(8,128)S(1)}, s32[8,128,128]{2,1,0:T(8,128)}, u32[]{:S(2)}) copy-start(s32[8,128,128]{2,1,0:T(8,128)} %mask.11) | copy-start | bytes 1572868
  69.3 2.2 %copy-start.3 = (s32[1,1,8]{2,1,0:T(1,128)S(1)}, s32[1,1,8]{2,1,0:T(1,128)}, u32[]{:S(2)}) copy-start(s32[1,1,8]{2,1,0:T(1,128)} %copy-done.2) | copy-start | bytes 100

commit v7 on v6

--- a/solution.py
+++ b/solution.py
@@ -376,13 +376,21 @@
         partial[level] = partial[level] + (THERMAL + 2.0 * NONLINEAR * value) * dense
 
 
-def salt_kernel(levels, first, slots, partial, pressure, mask, inner, part, *refs):
+def sort_kernel(sizes, slots, store, *parts):
+    level = 0
+    for size, part in zip(sizes, parts):
+        for at in range(size):
+            part[at] = store[slots[level]]
+            level += 1
+
+
+def salt_kernel(levels, first, partial, pressure, mask, part, *refs):
     result, done, sems = refs[-3:]
 
-    def finished(values, start):
+    def finished(values, place):
         copies = []
         for at in range(values.shape[0]):
-            level = level_of_slot(slots, start + at, levels)
+            level = place(at)
             dense = density(level, levels, pressure, mask)
             done[at] = partial[level] + CABBELING * values[at] * dense
             copies.append(pltpu.make_async_copy(done.at[at], result.at[level], sems.at[at]))
@@ -392,30 +400,37 @@
 
     @pl.when(from_outer())
     def _():
-        finished(part, first)
+        finished(part, lambda at: jnp.int32(first + at))
 
     if first == 0:
+        inner, slots = refs[:2]
 
         @pl.when(jnp.logical_not(from_outer()))
         def _():
-            finished(inner, 0)
-
-
-def finish(levels, first, args, before):
+            finished(inner, lambda at: level_of_slot(slots, at, levels))
+
+
+def finish(levels, first, args, whole, before):
     part = args[-1]
     shape = (levels,) + part.shape[1:]
-    held_args = [pltpu.with_memory_space_constraint(arg, pltpu.VMEM) for arg in args[1:]]
-    operands = [args[0]] + held_args + ([] if before is None else [before])
+    operands = [pltpu.with_memory_space_constraint(arg, pltpu.VMEM) for arg in args]
+    specs = [VMEM] * len(operands)
+    if first == 0:
+        operands += [pltpu.with_memory_space_constraint(whole[0], pltpu.VMEM), whole[1]]
+        specs += [VMEM, SMEM]
+    else:
+        operands.append(before)
+        specs.append(HBM)
     return pl.pallas_call(
         functools.partial(salt_kernel, levels, first),
         out_shape=jax.ShapeDtypeStruct(shape, jnp.float32),
-        in_specs=[SMEM] + [VMEM] * len(held_args) + ([] if before is None else [HBM]),
+        in_specs=specs,
         out_specs=HBM,
         scratch_shapes=[
             pltpu.VMEM(shape, jnp.float32),
             pltpu.SemaphoreType.DMA((levels,)),
         ],
-        input_output_aliases={} if before is None else {len(operands) - 1: 0},
+        input_output_aliases={len(operands) - 1: 0} if first else {},
         compiler_params=pltpu.CompilerParams(vmem_limit_bytes=KERNEL_VMEM),
         cost_estimate=pl.CostEstimate(flops=1000000, bytes_accessed=1000000, transcendentals=0),
     )(*operands)
@@ -505,10 +520,13 @@
         + held(from_south, from_north),
         keep=[False],
     )
-    cuts, start = [], 0
-    for size in salt_sizes:
-        cuts.append(lax.slice_in_dim(salt_store, start, start + size))
-        start += size
+    cuts = call(
+        functools.partial(sort_kernel, salt_sizes),
+        [(size, rows, columns) for size in salt_sizes],
+        free(slot_map.reshape(-1)) + stored(salt_store),
+        specs=[SMEM, VMEM],
+        keep=[False] * len(salt_sizes),
+    )
     salt_parts = [fetched(cut, "a") for cut in cuts]
     beside = held(from_south, from_north, from_west, from_east)
     basis, tile_rows = call(krylov_kernel, [(ITERS + 2,) + full, (devices, 1, LANES)], held(fields) + beside)
@@ -523,8 +541,8 @@
     )
     temp_back, first = None, 0
     for size, part in zip(salt_sizes, salt_parts):
-        args = (slots, partial, pressure, land_mask, salt_b, part)
-        temp_back = finish(levels, first, args, temp_back)
+        args = (partial, pressure, land_mask, part)
+        temp_back = finish(levels, first, args, (salt_b, slots), temp_back)
         first += size
     return (temp_back, salt_back, surface)
 

time: 76.9 us -> 76.4 us (level)
  local copies, waits for them, and re-layouts: 4.18 us -> 1.46 us
  Pallas kernels: 15 us -> 16.4 us
  waiting for transfers between devices: 39.8 us -> 40.6 us
    slice x2 -> x0, local copies, waits for them, and re-layouts: 3.37 us -> none  [body(): cuts.append(lax.slice_in_dim(salt_store, start, start + size))]
    pallas_call x7 -> x8, Pallas kernels: 12.5 us -> 14.4 us  [call(): pl.pallas_call(kernel, out_shape=shapes, in_specs=specs, out_specs=[VMEM]...]
    ppermute x4, waiting for transfers between devices: 35.5 us -> 36.3 us  [shifted(): return lax.ppermute(value, axis, pairs)]
  transfers between devices with their start and end apart: 10 -> 10, of which waited for: 4 -> 5; matrix products, arithmetic and copies ran while one was open for 4% -> 0% of each run, Pallas kernels for 19% -> 21%
where the time goes in v7:
time: 76.4 us; the launch traced here: 76 us
  waiting for transfers between devices  40.6 us (53%)
  starting transfers between devices  16.8 us (22%)
  Pallas kernels  16.4 us (21%)
  local copies, waits for them, and re-layouts  1.46 us (2%)
    ppermute x4, waiting for transfers between devices, shifted(): return lax.ppermute(value, axis, pairs)  36.3 us
    pallas_call x8, Pallas kernels, call(): pl.pallas_call(kernel, out_shape=shapes, in_specs=specs, out_specs=[VMEM]...  14.4 us
    ppermute x5, starting transfers between devices, fetched(): return lax.ppermute(value, 'gx', pairs)  8.66 us
    all_to_all x1, starting transfers between devices, shared(): rows = lax.all_to_all(rows, ('gx', 'gy'), 0, 0)  4.58 us
    all_to_all x1, waiting for transfers between devices, shared(): rows = lax.all_to_all(rows, ('gx', 'gy'), 0, 0)  4.33 us
    ppermute x4, starting transfers between devices, shifted(): return lax.ppermute(value, axis, pairs)  3.59 us
    pallas_call x2, Pallas kernels, finish(): pl.pallas_call(functools.partial(salt_kernel, levels, first), out_shape=j...  1.97 us
  transfers between devices with their start and end apart: 10, of which 5 were waited for; matrix products, arithmetic and copies ran while one was open for 0% of the time, Pallas kernels for 21%

profile of v7, /device:TPU:0, one launch (start us, length us, event | category | flops | bytes accessed | tf_op | source)
XLA Modules:
  0.0 76.0 jit_solution(8550170388740781373)
XLA Ops:
  0.6 4.1 %collective-permute-start.4 = (f32[8,128,128]{2,1,0:T(8,128)}, f32[8,128,128]{2,1,0:T(8,128)S(1)}, u32[]{:S(2)}, u32[]{:S(2)}) collective-permute-start(f32[8,128,128]{2,1,0:T(8,128)} %param.13), channel_id=1, source_target_pairs={{0,16},{2,18},{4,20},{6,22},{8,0},{10,2},{12,4},{14,6},{16,24},{18... | collective-permute-start | bytes 1572872 | tf_op jit(solution)/shard_map/ppermute | solution.py:460
  4.8 1.9 %collective-permute-start.8 = (f32[8,128,128]{2,1,0:T(8,128)}, f32[8,128,128]{2,1,0:T(8,128)S(1)}, u32[]{:S(2)}, u32[]{:S(2)}) collective-permute-start(f32[8,128,128]{2,1,0:T(8,128)} %store.1), channel_id=1, source_target_pairs={{0,8},{2,10},{4,12},{6,14},{8,24},{10,26},{12,28},{14,30},{16,0},{... | collective-permute-start | bytes 1572872 | tf_op jit(solution)/shard_map/ppermute | solution.py:460
  6.7 0.7 copy-done.4
  7.3 1.9 %shard_map.119 = (f32[5,128,128]{2,1,0:T(8,128)}, f32[3,128,128]{2,1,0:T(8,128)}) custom-call(s32[8]{0:T(128)S(1)} %bitcast.6, f32[8,128,128]{2,1,0:T(8,128)} %store.1), custom_call_target="tpu_custom_call" | custom-call | flops 4000000 | bytes 1000000 | tf_op jit(solution)/shard_map/pallas_call | solution.py:44
  9.2 1.0 %collective-permute-start.7 = (f32[5,128,128]{2,1,0:T(8,128)}, f32[5,128,128]{2,1,0:T(8,128)}, u32[]{:S(2)}, u32[]{:S(2)}) collective-permute-start(f32[5,128,128]{2,1,0:T(8,128)} %get-tuple-element.32), channel_id=1, source_target_pairs={{0,16},{2,18},{4,20},{6,22},{8,0},{10,2},{12,4},{14,6},{16,24},{18... | collective-permute-start | bytes 983048 | tf_op jit(solution)/shard_map/ppermute | solution.py:460
  10.2 1.4 %shard_map.112 = (f32[3,128,128]{2,1,0:T(8,128)S(1)}, f32[32,128]{1,0:T(8,128)S(1)}) custom-call(f32[128,128]{1,0:T(8,128)} %height.1, s32[8,128,128]{2,1,0:T(8,128)} %mask.11, f32[128,128]{1,0:T(8,128)} %depth.1, f32[8,128,128]{2,1,0:T(8,128)} %temp.5, f32[8,128,128]{2,1,0:T(8,128)} %north.3), custom_call_target="tpu_custom_call" | custom-call | flops 4000000 | bytes 1000000 | tf_op jit(solution)/shard_map/pallas_call | solution.py:44
  11.7 1.6 %collective-permute-start.1 = (f32[32,128]{1,0:T(8,128)S(1)}, f32[32,128]{1,0:T(8,128)S(1)}, u32[]{:S(2)}, u32[]{:S(2)}) collective-permute-start(f32[32,128]{1,0:T(8,128)S(1)} %get-tuple-element.22), channel_id=1, source_target_pairs={{0,1},{1,0},{2,3},{3,2},{4,5},{5,4},{6,7},{7,6},{8,9},{9,8},{10,11... | collective-permute-start | bytes 49160 | tf_op jit(solution)/shard_map/ppermute | solution.py:442
  13.3 1.7 %shard_map.113 = (f32[8,128]{1,0:T(8,128)S(1)}, f32[8,128]{1,0:T(8,128)S(1)}) custom-call(s32[8,128,128]{2,1,0:T(8,128)} %mask.11, f32[8,128,128]{2,1,0:T(8,128)} %temp.5, f32[8,128,128]{2,1,0:T(8,128)} %east.3), custom_call_target="tpu_custom_call" | custom-call | flops 4000000 | bytes 1000000 | tf_op jit(solution)/shard_map/pallas_call | solution.py:44
  15.0 0.5 collective-permute-done.1.refs_0_
  15.5 2.0 %collective-permute-start = (s32[1,1,8]{2,1,0:T(1,128)S(1)}, s32[1,1,8]{2,1,0:T(1,128)S(1)}, u32[]{:S(2)}, u32[]{:S(2)}) collective-permute-start(s32[1,1,8]{2,1,0:T(1,128)S(1)} %copy-done.5), channel_id=1, source_target_pairs={{0,16},{2,18},{4,20},{6,22},{8,24},{10,26},{12,28},{14,30},{16,0},... | collective-permute-start | bytes 104 | tf_op jit(solution)/shard_map/ppermute | solution.py:442
  17.5 0.2 shard_map.114
  17.7 28.1 %collective-permute-done = s32[1,1,8]{2,1,0:T(1,128)S(1)} collective-permute-done((s32[1,1,8]{2,1,0:T(1,128)S(1)}, s32[1,1,8]{2,1,0:T(1,128)S(1)}, u32[]{:S(2)}, u32[]{:S(2)}) %collective-permute-start) | collective-permute-done | bytes 64 | tf_op jit(solution)/shard_map/ppermute | solution.py:442
  45.8 6.0 %collective-permute-done.2.from_west = f32[32,256]{1,0:T(8,128)S(1)} collective-permute-done((f32[32,256]{1,0:T(8,128)S(1)}, f32[32,256]{1,0:T(8,128)S(1)}, u32[]{:S(2)}, u32[]{:S(2)}) %collective-permute-start.2) | collective-permute-done | bytes 32800 | tf_op jit(solution)/shard_map/ppermute | solution.py:442
  51.8 1.6 %collective-permute-done.3.from_east = f32[32,256]{1,0:T(8,128)S(1)} collective-permute-done((f32[32,256]{1,0:T(8,128)S(1)}, f32[32,256]{1,0:T(8,128)S(1)}, u32[]{:S(2)}, u32[]{:S(2)}) %collective-permute-start.3) | collective-permute-done | bytes 32800 | tf_op jit(solution)/shard_map/ppermute | solution.py:442
  53.4 1.6 %collective-permute-start.6 = (f32[3,128,128]{2,1,0:T(8,128)}, f32[3,128,128]{2,1,0:T(8,128)S(1)}, u32[]{:S(2)}, u32[]{:S(2)}) collective-permute-start(f32[3,128,128]{2,1,0:T(8,128)} %get-tuple-element.31), channel_id=1, source_target_pairs={{0,16},{2,18},{4,20},{6,22},{8,0},{10,2},{12,4},{14,6},{16,24},{18... | collective-permute-start | bytes 589832 | tf_op jit(solution)/shard_map/ppermute | solution.py:460
  55.0 2.5 %shard_map.116 = (f32[8,144,256]{2,1,0:T(8,128)S(1)}, f32[32,1,128]{2,1,0:T(1,128)}) custom-call(f32[3,128,128]{2,1,0:T(8,128)S(1)} %get-tuple-element.19.fields, f32[32,128]{1,0:T(8,128)S(1)} %get-tuple-element.23.from_south, f32[32,128]{1,0:T(8,128)S(1)} %get-tuple-element.24.from_north, f32[32,256]{1,0:T(8,128)S(1)} %collective-permute-done.2.from_west, ...), custom_call_target="tpu_custom_call" | custom-call | flops 4000000 | bytes 1000000 | tf_op jit(solution)/shard_map/pallas_call | solution.py:44
  57.5 4.6 %all-to-all-start = ((f32[32,1,128]{2,1,0:T(1,128)}), f32[32,1,128]{2,1,0:T(1,128)S(1)}, u32[]{:S(2)}, u32[]{:S(2)}) async-start(f32[32,1,128]{2,1,0:T(1,128)} %get-tuple-element.27), calls=%async_computation | async-start | bytes 32768 | tf_op jit(solution)/shard_map/all_to_all | solution.py:446
  62.1 2.0 %shard_map.115.tracer = f32[8,128,128]{2,1,0:T(8,128)S(1)} custom-call(f32[8,128,128]{2,1,0:T(8,128)} %temp.5, f32[8,128,128]{2,1,0:T(8,128)} %east.3, f32[8,128,128]{2,1,0:T(8,128)} %north.3, s32[8,128,128]{2,1,0:T(8,128)} %mask.11, f32[32,128]{1,0:T(8,128)S(1)} %get-tuple-element.23.from_south, f32[32,128]{1,0:T(8,128)S(1)} %get-tuple-element.24.from_north), custom_call_target="tpu_custom_call" | custom-call | flops 4000000 | bytes 1000000 | tf_op jit(solution)/shard_map/pallas_call | solution.py:44
  64.2 0.8 %copy-done.1 = f32[8,128,128]{2,1,0:T(8,128)} copy-done((f32[8,128,128]{2,1,0:T(8,128)}, f32[8,128,128]{2,1,0:T(8,128)S(1)}, u32[]{:S(2)}) %copy-start.1) | copy-done | bytes 524312
  65.0 4.3 %all-to-all-done = f32[32,1,128]{2,1,0:T(1,128)S(1)} async-done(((f32[32,1,128]{2,1,0:T(1,128)}), f32[32,1,128]{2,1,0:T(1,128)S(1)}, u32[]{:S(2)}, u32[]{:S(2)}) %all-to-all-start) | async-done | bytes 16416 | tf_op jit(solution)/shard_map/all_to_all | solution.py:446
  69.3 2.2 %shard_map.117 = (f32[128,128]{1,0:T(8,128)}, f32[128,128]{1,0:T(8,128)S(1)}) custom-call(f32[32,128]{1,0:T(8,128)S(1)} %bitcast.3, f32[8,144,256]{2,1,0:T(8,128)S(1)} %get-tuple-element.28.basis), custom_call_target="tpu_custom_call" | custom-call | flops 4000000 | bytes 1000000 | tf_op jit(solution)/shard_map/pallas_call | solution.py:44
  71.5 2.6 %shard_map.118 = (f32[8,128,128]{2,1,0:T(8,128)S(1)}, f32[8,128,128]{2,1,0:T(8,128)}) custom-call(s32[8]{0:T(128)S(1)} %bitcast.4, f32[8,128,128]{2,1,0:T(8,128)} %copy-done.1, f32[128,128]{1,0:T(8,128)S(1)} %get-tuple-element.29.pressure, f32[32,256]{1,0:T(8,128)S(1)} %collective-permute-done.2.from_west, f32[32,256]{1,0:T(8,128)S(1)} %collective-permute-done.3.from_east, ...), custom_call_target="tpu_custom_call" | custom-call | flops 4000000 | bytes 1000000 | tf_op jit(solution)/shard_map/pallas_call | solution.py:44
  74.0 1.9 %shard_map.120.refs_0_ = f32[8,128,128]{2,1,0:T(8,128)} custom-call(f32[8,128,128]{2,1,0:T(8,128)S(1)} %get-tuple-element.30.partial, f32[128,128]{1,0:T(8,128)S(1)} %get-tuple-element.29.pressure, s32[8,128,128]{2,1,0:T(8,128)S(1)} %copy-done, f32[5,128,128]{2,1,0:T(8,128)} %collective-permute-done.7.part, ...), custom_call_target="tpu_custom_call" | custom-call | flops 1000000 | bytes 1000000 | tf_op jit(solution)/shard_map/pallas_call | solution.py:424
  75.9 0.1 shard_map.121
  (18 shorter events, 0.0 us)
Async XLA Ops:
  0.6 70.8 %collective-permute-start.4 = (f32[8,128,128]{2,1,0:T(8,128)}, f32[8,128,128]{2,1,0:T(8,128)S(1)}, u32[]{:S(2)}, u32[]{:S(2)}) collective-permute-start(f32[8,128,128]{2,1,0:T(8,128)} %param.13), channel_id=1, source_target_pairs={{0,16},{2,18},{4,20},{6,22},{8,0},{10,2},{12,4},{14,6},{16,24},{18... | collective-permute-start | bytes 1572872 | tf_op jit(solution)/shard_map/ppermute | solution.py:460
  4.7 66.7 %collective-permute-start.5 = (f32[8,128,128]{2,1,0:T(8,128)}, f32[8,128,128]{2,1,0:T(8,128)S(1)}, u32[]{:S(2)}, u32[]{:S(2)}) collective-permute-start(f32[8,128,128]{2,1,0:T(8,128)} %param.13), channel_id=1, source_target_pairs={{0,8},{2,10},{4,12},{6,14},{8,24},{10,26},{12,28},{14,30},{16,0},{... | collective-permute-start | bytes 1572872 | tf_op jit(solution)/shard_map/ppermute | solution.py:460
  4.8 69.3 %collective-permute-start.8 = (f32[8,128,128]{2,1,0:T(8,128)}, f32[8,128,128]{2,1,0:T(8,128)S(1)}, u32[]{:S(2)}, u32[]{:S(2)}) collective-permute-start(f32[8,128,128]{2,1,0:T(8,128)} %store.1), channel_id=1, source_target_pairs={{0,8},{2,10},{4,12},{6,14},{8,24},{10,26},{12,28},{14,30},{16,0},{... | collective-permute-start | bytes 1572872 | tf_op jit(solution)/shard_map/ppermute | solution.py:460
  6.7 0.7 copy-start.4
  9.2 64.8 %collective-permute-start.7 = (f32[5,128,128]{2,1,0:T(8,128)}, f32[5,128,128]{2,1,0:T(8,128)}, u32[]{:S(2)}, u32[]{:S(2)}) collective-permute-start(f32[5,128,128]{2,1,0:T(8,128)} %get-tuple-element.32), channel_id=1, source_target_pairs={{0,16},{2,18},{4,20},{6,22},{8,0},{10,2},{12,4},{14,6},{16,24},{18... | collective-permute-start | bytes 983048 | tf_op jit(solution)/shard_map/ppermute | solution.py:460
  11.7 3.8 %copy-start.5 = (s32[1,1,8]{2,1,0:T(1,128)S(1)}, s32[1,1,8]{2,1,0:T(1,128)}, u32[]{:S(2)}) copy-start(s32[1,1,8]{2,1,0:T(1,128)} %param.15) | copy-start | bytes 100
  11.7 3.8 %collective-permute-start.1 = (f32[32,128]{1,0:T(8,128)S(1)}, f32[32,128]{1,0:T(8,128)S(1)}, u32[]{:S(2)}, u32[]{:S(2)}) collective-permute-start(f32[32,128]{1,0:T(8,128)S(1)} %get-tuple-element.22), channel_id=1, source_target_pairs={{0,1},{1,0},{2,3},{3,2},{4,5},{5,4},{6,7},{7,6},{8,9},{9,8},{10,11... | collective-permute-start | bytes 49160 | tf_op jit(solution)/shard_map/ppermute | solution.py:442
  15.5 30.3 %collective-permute-start = (s32[1,1,8]{2,1,0:T(1,128)S(1)}, s32[1,1,8]{2,1,0:T(1,128)S(1)}, u32[]{:S(2)}, u32[]{:S(2)}) collective-permute-start(s32[1,1,8]{2,1,0:T(1,128)S(1)} %copy-done.5), channel_id=1, source_target_pairs={{0,16},{2,18},{4,20},{6,22},{8,24},{10,26},{12,28},{14,30},{16,0},... | collective-permute-start | bytes 104 | tf_op jit(solution)/shard_map/ppermute | solution.py:442
  45.8 11.8 %copy-start.2 = (s32[1,1,8]{2,1,0:T(1,128)}, s32[1,1,8]{2,1,0:T(1,128)S(1)}, u32[]{:S(2)}) copy-start(s32[1,1,8]{2,1,0:T(1,128)S(1)} %collective-permute-done) | copy-start | bytes 100
  45.8 6.0 %collective-permute-start.2 = (f32[32,256]{1,0:T(8,128)S(1)}, f32[32,256]{1,0:T(8,128)S(1)}, u32[]{:S(2)}, u32[]{:S(2)}) collective-permute-start(f32[32,256]{1,0:T(8,128)S(1)} %get-tuple-element.25), channel_id=1, source_target_pairs={{0,2},{2,4},{4,6},{6,8},{8,10},{10,12},{12,14},{14,16},{16,18},{18... | collective-permute-start | bytes 98312 | tf_op jit(solution)/shard_map/ppermute | solution.py:442
  51.8 1.6 %collective-permute-start.3 = (f32[32,256]{1,0:T(8,128)S(1)}, f32[32,256]{1,0:T(8,128)S(1)}, u32[]{:S(2)}, u32[]{:S(2)}) collective-permute-start(f32[32,256]{1,0:T(8,128)S(1)} %get-tuple-element.26), channel_id=1, source_target_pairs={{0,30},{2,0},{4,2},{6,4},{8,6},{10,8},{12,10},{14,12},{16,14},{18,... | collective-permute-start | bytes 98312 | tf_op jit(solution)/shard_map/ppermute | solution.py:442
  53.4 22.5 %collective-permute-start.6 = (f32[3,128,128]{2,1,0:T(8,128)}, f32[3,128,128]{2,1,0:T(8,128)S(1)}, u32[]{:S(2)}, u32[]{:S(2)}) collective-permute-start(f32[3,128,128]{2,1,0:T(8,128)} %get-tuple-element.31), channel_id=1, source_target_pairs={{0,16},{2,18},{4,20},{6,22},{8,0},{10,2},{12,4},{14,6},{16,24},{18... | collective-permute-start | bytes 589832 | tf_op jit(solution)/shard_map/ppermute | solution.py:460
  57.5 11.7 %all-to-all-start = ((f32[32,1,128]{2,1,0:T(1,128)}), f32[32,1,128]{2,1,0:T(1,128)S(1)}, u32[]{:S(2)}, u32[]{:S(2)}) async-start(f32[32,1,128]{2,1,0:T(1,128)} %get-tuple-element.27), calls=%async_computation | async-start | bytes 32768 | tf_op jit(solution)/shard_map/all_to_all | solution.py:446
  64.2 0.8 %copy-start.1 = (f32[8,128,128]{2,1,0:T(8,128)}, f32[8,128,128]{2,1,0:T(8,128)S(1)}, u32[]{:S(2)}) copy-start(f32[8,128,128]{2,1,0:T(8,128)S(1)} %shard_map.115.tracer) | copy-start | bytes 1572868
  64.9 6.5 %copy-start = (s32[8,128,128]{2,1,0:T(8,128)S(1)}, s32[8,128,128]{2,1,0:T(8,128)}, u32[]{:S(2)}) copy-start(s32[8,128,128]{2,1,0:T(8,128)} %mask.11) | copy-start | bytes 1572868
  69.3 2.2 %copy-start.3 = (s32[1,1,8]{2,1,0:T(1,128)S(1)}, s32[1,1,8]{2,1,0:T(1,128)}, u32[]{:S(2)}) copy-start(s32[1,1,8]{2,1,0:T(1,128)} %copy-done.2) | copy-start | bytes 100

commit v8 on v7

--- a/solution.py
+++ b/solution.py
@@ -384,53 +384,46 @@
             level += 1
 
 
-def salt_kernel(levels, first, partial, pressure, mask, part, *refs):
-    result, done, sems = refs[-3:]
-
-    def finished(values, place):
-        copies = []
-        for at in range(values.shape[0]):
-            level = place(at)
-            dense = density(level, levels, pressure, mask)
-            done[at] = partial[level] + CABBELING * values[at] * dense
-            copies.append(pltpu.make_async_copy(done.at[at], result.at[level], sems.at[at]))
-            copies[-1].start()
-        for copy in copies:
-            copy.wait()
-
+def finish_levels(levels, partial, pressure, mask, values, place, result, done, sems):
+    copies = []
+    for at in range(values.shape[0]):
+        level = place(at)
+        dense = density(level, levels, pressure, mask)
+        done[at] = partial[level] + CABBELING * values[at] * dense
+        copies.append(pltpu.make_async_copy(done.at[at], result.at[level], sems.at[at]))
+        copies[-1].start()
+    for copy in copies:
+        copy.wait()
+
+
+def inner_kernel(levels, partial, pressure, mask, values, slots, *refs):
+    @pl.when(jnp.logical_not(from_outer()))
+    def _():
+        place = lambda at: level_of_slot(slots, at, levels)
+        finish_levels(levels, partial, pressure, mask, values, place, *refs)
+
+
+def outer_kernel(levels, first, partial, pressure, mask, values, before, *refs):
     @pl.when(from_outer())
     def _():
-        finished(part, lambda at: jnp.int32(first + at))
-
-    if first == 0:
-        inner, slots = refs[:2]
-
-        @pl.when(jnp.logical_not(from_outer()))
-        def _():
-            finished(inner, lambda at: level_of_slot(slots, at, levels))
-
-
-def finish(levels, first, args, whole, before):
+        place = lambda at: jnp.int32(first + at)
+        finish_levels(levels, partial, pressure, mask, values, place, *refs)
+
+
+def finish(kernel, levels, args, extra):
     part = args[-1]
-    shape = (levels,) + part.shape[1:]
-    operands = [pltpu.with_memory_space_constraint(arg, pltpu.VMEM) for arg in args]
-    specs = [VMEM] * len(operands)
-    if first == 0:
-        operands += [pltpu.with_memory_space_constraint(whole[0], pltpu.VMEM), whole[1]]
-        specs += [VMEM, SMEM]
-    else:
-        operands.append(before)
-        specs.append(HBM)
+    operands = [pltpu.with_memory_space_constraint(arg, pltpu.VMEM) for arg in args] + [extra]
+    begins = extra.ndim == 1
     return pl.pallas_call(
-        functools.partial(salt_kernel, levels, first),
-        out_shape=jax.ShapeDtypeStruct(shape, jnp.float32),
-        in_specs=specs,
+        kernel,
+        out_shape=jax.ShapeDtypeStruct((levels,) + part.shape[1:], jnp.float32),
+        in_specs=[VMEM] * len(args) + [SMEM if begins else HBM],
         out_specs=HBM,
         scratch_shapes=[
-            pltpu.VMEM(shape, jnp.float32),
-            pltpu.SemaphoreType.DMA((levels,)),
+            pltpu.VMEM(part.shape, jnp.float32),
+            pltpu.SemaphoreType.DMA((part.shape[0],)),
         ],
-        input_output_aliases={len(operands) - 1: 0} if first else {},
+        input_output_aliases={} if begins else {len(args): 0},
         compiler_params=pltpu.CompilerParams(vmem_limit_bytes=KERNEL_VMEM),
         cost_estimate=pl.CostEstimate(flops=1000000, bytes_accessed=1000000, transcendentals=0),
     )(*operands)
@@ -466,7 +459,7 @@
 
 
 def runs(levels):
-    most = 5 * levels // 8
+    most = 6 * levels // 8
     return most, levels - most
 
 
@@ -539,10 +532,12 @@
         specs=[SMEM] + [VMEM] * 7,
         keep=[True, False],
     )
-    temp_back, first = None, 0
+    common = (partial, pressure, land_mask)
+    inner = functools.partial(inner_kernel, levels)
+    temp_back, first = finish(inner, levels, (*common, salt_b), slots), 0
     for size, part in zip(salt_sizes, salt_parts):
-        args = (partial, pressure, land_mask, part)
-        temp_back = finish(levels, first, args, (salt_b, slots), temp_back)
+        outer = functools.partial(outer_kernel, levels, first)
+        temp_back = finish(outer, levels, (*common, part), temp_back)
         first += size
     return (temp_back, salt_back, surface)
 

time: 76.4 us -> 78.4 us (1.026)
  waiting for transfers between devices: 40.6 us -> 42 us
    ppermute x4, waiting for transfers between devices: 36.3 us -> 37.7 us  [shifted(): return lax.ppermute(value, axis, pairs)]
    pallas_call x2 -> x3, Pallas kernels: 1.97 us -> 2.52 us  [finish(): pl.pallas_call(kernel, out_shape=jax.ShapeDtypeStruct((levels,) + part.sh...]
  transfers between devices with their start and end apart: 10 -> 10, of which waited for: 5 -> 5; matrix products, arithmetic and copies ran while one was open for 0% -> 0% of each run, Pallas kernels for 21% -> 22%
where the time goes in v8:
time: 78.4 us; the launch traced here: 78 us
  waiting for transfers between devices  42 us (54%)
  Pallas kernels  16.9 us (22%)
  starting transfers between devices  16.8 us (21%)
  local copies, waits for them, and re-layouts  1.45 us (2%)
    ppermute x4, waiting for transfers between devices, shifted(): return lax.ppermute(value, axis, pairs)  37.7 us
    pallas_call x8, Pallas kernels, call(): pl.pallas_call(kernel, out_shape=shapes, in_specs=specs, out_specs=[VMEM]...  14.4 us
    ppermute x5, starting transfers between devices, fetched(): return lax.ppermute(value, 'gx', pairs)  8.66 us
    all_to_all x1, starting transfers between devices, shared(): rows = lax.all_to_all(rows, ('gx', 'gy'), 0, 0)  4.58 us
    all_to_all x1, waiting for transfers between devices, shared(): rows = lax.all_to_all(rows, ('gx', 'gy'), 0, 0)  4.33 us
    ppermute x4, starting transfers between devices, shifted(): return lax.ppermute(value, axis, pairs)  3.59 us
    pallas_call x3, Pallas kernels, finish(): pl.pallas_call(kernel, out_shape=jax.ShapeDtypeStruct((levels,) + part.sh...  2.52 us
  transfers between devices with their start and end apart: 10, of which 5 were waited for; matrix products, arithmetic and copies ran while one was open for 0% of the time, Pallas kernels for 22%

profile of v8, /device:TPU:0, one launch (start us, length us, event | category | flops | bytes accessed | tf_op | source)
XLA Modules:
  0.0 78.0 jit_solution(18380095439549563737)
XLA Ops:
  0.6 4.1 %collective-permute-start.4 = (f32[8,128,128]{2,1,0:T(8,128)}, f32[8,128,128]{2,1,0:T(8,128)S(1)}, u32[]{:S(2)}, u32[]{:S(2)}) collective-permute-start(f32[8,128,128]{2,1,0:T(8,128)} %param.13), channel_id=1, source_target_pairs={{0,16},{2,18},{4,20},{6,22},{8,0},{10,2},{12,4},{14,6},{16,24},{18... | collective-permute-start | bytes 1572872 | tf_op jit(solution)/shard_map/ppermute | solution.py:453
  4.8 1.9 %collective-permute-start.8 = (f32[8,128,128]{2,1,0:T(8,128)}, f32[8,128,128]{2,1,0:T(8,128)S(1)}, u32[]{:S(2)}, u32[]{:S(2)}) collective-permute-start(f32[8,128,128]{2,1,0:T(8,128)} %store.1), channel_id=1, source_target_pairs={{0,8},{2,10},{4,12},{6,14},{8,24},{10,26},{12,28},{14,30},{16,0},{... | collective-permute-start | bytes 1572872 | tf_op jit(solution)/shard_map/ppermute | solution.py:453
  6.7 0.7 copy-done.2
  7.3 1.9 %shard_map.119 = (f32[6,128,128]{2,1,0:T(8,128)}, f32[2,128,128]{2,1,0:T(8,128)}) custom-call(s32[8]{0:T(128)S(1)} %bitcast.6, f32[8,128,128]{2,1,0:T(8,128)} %store.1), custom_call_target="tpu_custom_call" | custom-call | flops 4000000 | bytes 1000000 | tf_op jit(solution)/shard_map/pallas_call | solution.py:44
  9.2 1.0 %collective-permute-start.7 = (f32[6,128,128]{2,1,0:T(8,128)}, f32[6,128,128]{2,1,0:T(8,128)}, u32[]{:S(2)}, u32[]{:S(2)}) collective-permute-start(f32[6,128,128]{2,1,0:T(8,128)} %get-tuple-element.32), channel_id=1, source_target_pairs={{0,16},{2,18},{4,20},{6,22},{8,0},{10,2},{12,4},{14,6},{16,24},{18... | collective-permute-start | bytes 1179656 | tf_op jit(solution)/shard_map/ppermute | solution.py:453
  10.2 1.4 %shard_map.112 = (f32[3,128,128]{2,1,0:T(8,128)S(1)}, f32[32,128]{1,0:T(8,128)S(1)}) custom-call(f32[128,128]{1,0:T(8,128)} %height.1, s32[8,128,128]{2,1,0:T(8,128)} %mask.13, f32[128,128]{1,0:T(8,128)} %depth.1, f32[8,128,128]{2,1,0:T(8,128)} %temp.5, f32[8,128,128]{2,1,0:T(8,128)} %north.3), custom_call_target="tpu_custom_call" | custom-call | flops 4000000 | bytes 1000000 | tf_op jit(solution)/shard_map/pallas_call | solution.py:44
  11.7 1.6 %collective-permute-start.1 = (f32[32,128]{1,0:T(8,128)S(1)}, f32[32,128]{1,0:T(8,128)S(1)}, u32[]{:S(2)}, u32[]{:S(2)}) collective-permute-start(f32[32,128]{1,0:T(8,128)S(1)} %get-tuple-element.22), channel_id=1, source_target_pairs={{0,1},{1,0},{2,3},{3,2},{4,5},{5,4},{6,7},{7,6},{8,9},{9,8},{10,11... | collective-permute-start | bytes 49160 | tf_op jit(solution)/shard_map/ppermute | solution.py:435
  13.3 1.7 %shard_map.113 = (f32[8,128]{1,0:T(8,128)S(1)}, f32[8,128]{1,0:T(8,128)S(1)}) custom-call(s32[8,128,128]{2,1,0:T(8,128)} %mask.13, f32[8,128,128]{2,1,0:T(8,128)} %temp.5, f32[8,128,128]{2,1,0:T(8,128)} %east.3), custom_call_target="tpu_custom_call" | custom-call | flops 4000000 | bytes 1000000 | tf_op jit(solution)/shard_map/pallas_call | solution.py:44
  15.0 0.5 collective-permute-done.1.refs_0_
  15.5 2.0 %collective-permute-start = (s32[1,1,8]{2,1,0:T(1,128)S(1)}, s32[1,1,8]{2,1,0:T(1,128)S(1)}, u32[]{:S(2)}, u32[]{:S(2)}) collective-permute-start(s32[1,1,8]{2,1,0:T(1,128)S(1)} %copy-done.3), channel_id=1, source_target_pairs={{0,16},{2,18},{4,20},{6,22},{8,24},{10,26},{12,28},{14,30},{16,0},... | collective-permute-start | bytes 104 | tf_op jit(solution)/shard_map/ppermute | solution.py:435
  17.5 0.2 shard_map.114
  17.7 29.5 %collective-permute-done = s32[1,1,8]{2,1,0:T(1,128)S(1)} collective-permute-done((s32[1,1,8]{2,1,0:T(1,128)S(1)}, s32[1,1,8]{2,1,0:T(1,128)S(1)}, u32[]{:S(2)}, u32[]{:S(2)}) %collective-permute-start) | collective-permute-done | bytes 64 | tf_op jit(solution)/shard_map/ppermute | solution.py:435
  47.2 6.0 %collective-permute-done.2.from_west = f32[32,256]{1,0:T(8,128)S(1)} collective-permute-done((f32[32,256]{1,0:T(8,128)S(1)}, f32[32,256]{1,0:T(8,128)S(1)}, u32[]{:S(2)}, u32[]{:S(2)}) %collective-permute-start.2) | collective-permute-done | bytes 32800 | tf_op jit(solution)/shard_map/ppermute | solution.py:435
  53.2 1.6 %collective-permute-done.3.from_east = f32[32,256]{1,0:T(8,128)S(1)} collective-permute-done((f32[32,256]{1,0:T(8,128)S(1)}, f32[32,256]{1,0:T(8,128)S(1)}, u32[]{:S(2)}, u32[]{:S(2)}) %collective-permute-start.3) | collective-permute-done | bytes 32800 | tf_op jit(solution)/shard_map/ppermute | solution.py:435
  54.8 1.6 %collective-permute-start.6 = (f32[2,128,128]{2,1,0:T(8,128)}, f32[2,128,128]{2,1,0:T(8,128)S(1)}, u32[]{:S(2)}, u32[]{:S(2)}) collective-permute-start(f32[2,128,128]{2,1,0:T(8,128)} %get-tuple-element.31), channel_id=1, source_target_pairs={{0,16},{2,18},{4,20},{6,22},{8,0},{10,2},{12,4},{14,6},{16,24},{18... | collective-permute-start | bytes 393224 | tf_op jit(solution)/shard_map/ppermute | solution.py:453
  56.4 2.5 %shard_map.116 = (f32[8,144,256]{2,1,0:T(8,128)S(1)}, f32[32,1,128]{2,1,0:T(1,128)}) custom-call(f32[3,128,128]{2,1,0:T(8,128)S(1)} %get-tuple-element.19.fields, f32[32,128]{1,0:T(8,128)S(1)} %get-tuple-element.23.from_south, f32[32,128]{1,0:T(8,128)S(1)} %get-tuple-element.24.from_north, f32[32,256]{1,0:T(8,128)S(1)} %collective-permute-done.2.from_west, ...), custom_call_target="tpu_custom_call" | custom-call | flops 4000000 | bytes 1000000 | tf_op jit(solution)/shard_map/pallas_call | solution.py:44
  58.9 4.6 %all-to-all-start = ((f32[32,1,128]{2,1,0:T(1,128)}), f32[32,1,128]{2,1,0:T(1,128)S(1)}, u32[]{:S(2)}, u32[]{:S(2)}) async-start(f32[32,1,128]{2,1,0:T(1,128)} %get-tuple-element.27), calls=%async_computation | async-start | bytes 32768 | tf_op jit(solution)/shard_map/all_to_all | solution.py:439
  63.5 2.0 %shard_map.115.tracer = f32[8,128,128]{2,1,0:T(8,128)S(1)} custom-call(f32[8,128,128]{2,1,0:T(8,128)} %temp.5, f32[8,128,128]{2,1,0:T(8,128)} %east.3, f32[8,128,128]{2,1,0:T(8,128)} %north.3, s32[8,128,128]{2,1,0:T(8,128)} %mask.13, f32[32,128]{1,0:T(8,128)S(1)} %get-tuple-element.23.from_south, f32[32,128]{1,0:T(8,128)S(1)} %get-tuple-element.24.from_north), custom_call_target="tpu_custom_call" | custom-call | flops 4000000 | bytes 1000000 | tf_op jit(solution)/shard_map/pallas_call | solution.py:44
  65.6 0.8 %copy-done.1 = f32[8,128,128]{2,1,0:T(8,128)} copy-done((f32[8,128,128]{2,1,0:T(8,128)}, f32[8,128,128]{2,1,0:T(8,128)S(1)}, u32[]{:S(2)}) %copy-start.1) | copy-done | bytes 524312
  66.4 4.3 %all-to-all-done = f32[32,1,128]{2,1,0:T(1,128)S(1)} async-done(((f32[32,1,128]{2,1,0:T(1,128)}), f32[32,1,128]{2,1,0:T(1,128)S(1)}, u32[]{:S(2)}, u32[]{:S(2)}) %all-to-all-start) | async-done | bytes 16416 | tf_op jit(solution)/shard_map/all_to_all | solution.py:439
  70.7 2.2 %shard_map.117 = (f32[128,128]{1,0:T(8,128)}, f32[128,128]{1,0:T(8,128)S(1)}) custom-call(f32[32,128]{1,0:T(8,128)S(1)} %bitcast.3, f32[8,144,256]{2,1,0:T(8,128)S(1)} %get-tuple-element.28.basis), custom_call_target="tpu_custom_call" | custom-call | flops 4000000 | bytes 1000000 | tf_op jit(solution)/shard_map/pallas_call | solution.py:44
  72.9 2.6 %shard_map.118 = (f32[8,128,128]{2,1,0:T(8,128)S(1)}, f32[8,128,128]{2,1,0:T(8,128)}) custom-call(s32[8]{0:T(128)S(1)} %bitcast.4, f32[8,128,128]{2,1,0:T(8,128)} %copy-done.1, f32[128,128]{1,0:T(8,128)S(1)} %get-tuple-element.29.pressure, f32[32,256]{1,0:T(8,128)S(1)} %collective-permute-done.2.from_west, f32[32,256]{1,0:T(8,128)S(1)} %collective-permute-done.3.from_east, ...), custom_call_target="tpu_custom_call" | custom-call | flops 4000000 | bytes 1000000 | tf_op jit(solution)/shard_map/pallas_call | solution.py:44
  75.4 1.4 %shard_map.120.before = f32[8,128,128]{2,1,0:T(8,128)} custom-call(f32[8,128,128]{2,1,0:T(8,128)S(1)} %get-tuple-element.30.partial, f32[128,128]{1,0:T(8,128)S(1)} %get-tuple-element.29.pressure, s32[8,128,128]{2,1,0:T(8,128)S(1)} %copy-done, f32[8,128,128]{2,1,0:T(8,128)S(1)} %collective-permute-done.8.values, s32[8]{0:T(128)S(1)} %bitcast.5), custom_call_target="tpu_custom_call" | custom-call | flops 1000000 | bytes 1000000 | tf_op jit(solution)/shard_map/pallas_call | solution.py:417
  76.9 1.1 %shard_map.121.before = f32[8,128,128]{2,1,0:T(8,128)} custom-call(f32[8,128,128]{2,1,0:T(8,128)S(1)} %get-tuple-element.30.partial, f32[128,128]{1,0:T(8,128)S(1)} %get-tuple-element.29.pressure, s32[8,128,128]{2,1,0:T(8,128)S(1)} %copy-done, f32[6,128,128]{2,1,0:T(8,128)} %collective-permute-done.7.values, ...), custom_call_target="tpu_custom_call", output_to_operand_aliasing={{}: (4, {})} | custom-call | flops 1000000 | bytes 1000000 | tf_op jit(solution)/shard_map/pallas_call | solution.py:417
  (15 shorter events, 0.1 us)
Async XLA Ops:
  0.6 72.2 %collective-permute-start.4 = (f32[8,128,128]{2,1,0:T(8,128)}, f32[8,128,128]{2,1,0:T(8,128)S(1)}, u32[]{:S(2)}, u32[]{:S(2)}) collective-permute-start(f32[8,128,128]{2,1,0:T(8,128)} %param.13), channel_id=1, source_target_pairs={{0,16},{2,18},{4,20},{6,22},{8,0},{10,2},{12,4},{14,6},{16,24},{18... | collective-permute-start | bytes 1572872 | tf_op jit(solution)/shard_map/ppermute | solution.py:453
  4.7 68.1 %collective-permute-start.5 = (f32[8,128,128]{2,1,0:T(8,128)}, f32[8,128,128]{2,1,0:T(8,128)S(1)}, u32[]{:S(2)}, u32[]{:S(2)}) collective-permute-start(f32[8,128,128]{2,1,0:T(8,128)} %param.13), channel_id=1, source_target_pairs={{0,8},{2,10},{4,12},{6,14},{8,24},{10,26},{12,28},{14,30},{16,0},{... | collective-permute-start | bytes 1572872 | tf_op jit(solution)/shard_map/ppermute | solution.py:453
  4.8 70.7 %collective-permute-start.8 = (f32[8,128,128]{2,1,0:T(8,128)}, f32[8,128,128]{2,1,0:T(8,128)S(1)}, u32[]{:S(2)}, u32[]{:S(2)}) collective-permute-start(f32[8,128,128]{2,1,0:T(8,128)} %store.1), channel_id=1, source_target_pairs={{0,8},{2,10},{4,12},{6,14},{8,24},{10,26},{12,28},{14,30},{16,0},{... | collective-permute-start | bytes 1572872 | tf_op jit(solution)/shard_map/ppermute | solution.py:453
  6.7 0.7 copy-start.2
  9.2 67.7 %collective-permute-start.7 = (f32[6,128,128]{2,1,0:T(8,128)}, f32[6,128,128]{2,1,0:T(8,128)}, u32[]{:S(2)}, u32[]{:S(2)}) collective-permute-start(f32[6,128,128]{2,1,0:T(8,128)} %get-tuple-element.32), channel_id=1, source_target_pairs={{0,16},{2,18},{4,20},{6,22},{8,0},{10,2},{12,4},{14,6},{16,24},{18... | collective-permute-start | bytes 1179656 | tf_op jit(solution)/shard_map/ppermute | solution.py:453
  11.7 3.8 %copy-start.3 = (s32[1,1,8]{2,1,0:T(1,128)S(1)}, s32[1,1,8]{2,1,0:T(1,128)}, u32[]{:S(2)}) copy-start(s32[1,1,8]{2,1,0:T(1,128)} %param.15) | copy-start | bytes 100
  11.7 3.8 %collective-permute-start.1 = (f32[32,128]{1,0:T(8,128)S(1)}, f32[32,128]{1,0:T(8,128)S(1)}, u32[]{:S(2)}, u32[]{:S(2)}) collective-permute-start(f32[32,128]{1,0:T(8,128)S(1)} %get-tuple-element.22), channel_id=1, source_target_pairs={{0,1},{1,0},{2,3},{3,2},{4,5},{5,4},{6,7},{7,6},{8,9},{9,8},{10,11... | collective-permute-start | bytes 49160 | tf_op jit(solution)/shard_map/ppermute | solution.py:435
  15.5 31.7 %collective-permute-start = (s32[1,1,8]{2,1,0:T(1,128)S(1)}, s32[1,1,8]{2,1,0:T(1,128)S(1)}, u32[]{:S(2)}, u32[]{:S(2)}) collective-permute-start(s32[1,1,8]{2,1,0:T(1,128)S(1)} %copy-done.3), channel_id=1, source_target_pairs={{0,16},{2,18},{4,20},{6,22},{8,24},{10,26},{12,28},{14,30},{16,0},... | collective-permute-start | bytes 104 | tf_op jit(solution)/shard_map/ppermute | solution.py:435
  47.2 6.0 %collective-permute-start.2 = (f32[32,256]{1,0:T(8,128)S(1)}, f32[32,256]{1,0:T(8,128)S(1)}, u32[]{:S(2)}, u32[]{:S(2)}) collective-permute-start(f32[32,256]{1,0:T(8,128)S(1)} %get-tuple-element.25), channel_id=1, source_target_pairs={{0,2},{2,4},{4,6},{6,8},{8,10},{10,12},{12,14},{14,16},{16,18},{18... | collective-permute-start | bytes 98312 | tf_op jit(solution)/shard_map/ppermute | solution.py:435
  53.2 1.6 %collective-permute-start.3 = (f32[32,256]{1,0:T(8,128)S(1)}, f32[32,256]{1,0:T(8,128)S(1)}, u32[]{:S(2)}, u32[]{:S(2)}) collective-permute-start(f32[32,256]{1,0:T(8,128)S(1)} %get-tuple-element.26), channel_id=1, source_target_pairs={{0,30},{2,0},{4,2},{6,4},{8,6},{10,8},{12,10},{14,12},{16,14},{18,... | collective-permute-start | bytes 98312 | tf_op jit(solution)/shard_map/ppermute | solution.py:435
  54.8 23.1 %collective-permute-start.6 = (f32[2,128,128]{2,1,0:T(8,128)}, f32[2,128,128]{2,1,0:T(8,128)S(1)}, u32[]{:S(2)}, u32[]{:S(2)}) collective-permute-start(f32[2,128,128]{2,1,0:T(8,128)} %get-tuple-element.31), channel_id=1, source_target_pairs={{0,16},{2,18},{4,20},{6,22},{8,0},{10,2},{12,4},{14,6},{16,24},{18... | collective-permute-start | bytes 393224 | tf_op jit(solution)/shard_map/ppermute | solution.py:453
  58.9 11.7 %all-to-all-start = ((f32[32,1,128]{2,1,0:T(1,128)}), f32[32,1,128]{2,1,0:T(1,128)S(1)}, u32[]{:S(2)}, u32[]{:S(2)}) async-start(f32[32,1,128]{2,1,0:T(1,128)} %get-tuple-element.27), calls=%async_computation | async-start | bytes 32768 | tf_op jit(solution)/shard_map/all_to_all | solution.py:439
  65.6 0.8 %copy-start.1 = (f32[8,128,128]{2,1,0:T(8,128)}, f32[8,128,128]{2,1,0:T(8,128)S(1)}, u32[]{:S(2)}) copy-start(f32[8,128,128]{2,1,0:T(8,128)S(1)} %shard_map.115.tracer) | copy-start | bytes 1572868
  66.3 6.5 %copy-start = (s32[8,128,128]{2,1,0:T(8,128)S(1)}, s32[8,128,128]{2,1,0:T(8,128)}, u32[]{:S(2)}) copy-start(s32[8,128,128]{2,1,0:T(8,128)} %mask.13) | copy-start | bytes 1572868
